TPU v7x, 512 devices: a whole 4x4x16 slice. The times are simulated.
512 devices in a mesh: ka: 64 (over y, z_hi, x, core), col: 8 (over z_lo).
Axes of the slice: x: 4, y: 4, z: 16 (z_hi: 2, z_lo: 8; z = z_hi * 8 + z_lo), core: 2. Of those that a mesh axis runs over, the one named last changes fastest.
Arguments:
- correlations: bfloat16 [64, 8, 2, 512, 512], P('ka', None, None, 'col')
- gauge: bfloat16 [64, 512, 2, 256], P('ka', 'col'), may hold values from -1 to 1
- neighbours: int32 [64, 8], P('ka'), may hold values from 0 to 63, as said below
- shifts: int32 [64, 8, 3], P('ka'), may hold values from -1 to 1, as said below
Outputs:
- u_next: float32 [64, 512, 2, 256], P('ka', 'col')
- gradient: float32 [64, 2, 256, 256], P('ka', None, 'col')
- omega_od: float32 [], replicated
Inputs may be any that keep to these rules, and one draw needn't show every extreme that they name: For each k-point k with grid coordinates g(k) = (k // 16, k // 4 % 4, k % 4) on the 4 x 4 x 4 grid, the 8 entries neighbours[k, :] together with shifts[k, :, :] list the displacements d = +-(1,0,0), +-(0,1,0), +-(0,0,1), +-(1,1,1), each once, in some order: g(neighbours[k,b]) = g(k) + d - shifts[k,b] * (4, 4, 4), with each coordinate inside the grid. shifts[k,b] is the componentwise floor of (g(k) + d) / (4, 4, 4) for the displacement d that neighbours[k,b] names.
All inputs are finite; a program needn't handle non-finite values.
Results may differ from a plain program's by a relative error of at most 0.02.
Values may be sent and summed in bfloat16 or wider, within the bound.
No kernel may reach another device: no remote copies, remote signals or barrier semaphores. Data moves between devices by JAX's collectives and lax.ppermute only.
A program may use at most 128 MiB of HBM per device.

v0:
```python
import jax
import jax.numpy as jnp
from jax import lax
from jax.sharding import PartitionSpec as P

NS_STEPS = 3


product_precision = lax.Precision.DEFAULT
MIXING = 0.02
STEP_LENGTH = 0.2
SHELL_LIST = [
    (1, 0, 0),
    (-1, 0, 0),
    (0, 1, 0),
    (0, -1, 0),
    (0, 0, 1),
    (0, 0, -1),
    (1, 1, 1),
    (-1, -1, -1),
]


def shifted(x, axis, by):
    length = lax.axis_size(axis)
    return lax.ppermute(x, axis, [(i, (i + by) % length) for i in range(length)])


def from_everyone(x, axis):
    length = lax.axis_size(axis)
    return lax.all_to_all(jnp.broadcast_to(x[None], (length, *x.shape)), axis, 0, 0, tiled=True)


def laid_out(parts, dim):
    shape = list(parts.shape[1:])
    shape[dim] *= parts.shape[0]
    return jnp.moveaxis(parts, 0, dim).reshape(shape)


def gathered_copies(x, axis, dim):
    parts = from_everyone(x, axis)
    return laid_out(parts, dim)


def in_blocks(x, dim, length):
    shape = x.shape
    parts = x.reshape(*shape[:dim], length, shape[dim] // length, *shape[dim + 1 :])
    return jnp.moveaxis(parts, dim, 0)


def sent_and_summed(x, axis, dim):
    parts = in_blocks(x, dim, lax.axis_size(axis))
    arrived = lax.all_to_all(parts, axis, split_axis=0, concat_axis=0, tiled=True)
    return arrived.astype(jnp.float32).sum(axis=0)


def together(arrays, axis):
    vector, at, gathered = (jnp.concatenate([a.reshape(-1) for a in arrays]), 0, [])
    running = lax.psum(vector, axis)
    for a in arrays:
        gathered.append(running[at : at + a.size].reshape(a.shape))
        at += a.size
    return tuple(gathered)


def of_everyone(x, axis):
    return from_everyone(x, axis).sum(axis=0)


def gather_packed(arrays, axis, dims):
    vector = jnp.concatenate([a.reshape(-1) for a in arrays])
    lines, at, gathered = (lax.all_gather(vector, axis), 0, [])
    for a, dim in zip(arrays, dims):
        parts = lines[:, at : at + a.size].reshape(-1, *a.shape)
        gathered.append(laid_out(parts, dim))
        at += a.size
    return tuple(gathered)


def grid_positions(index):
    return jnp.stack([index // 16, index // 4 % 4, index % 4], -1)


def shell_vector_weights(kpoint_index, neighbour_list, shifts, leading_size):
    grid_sizes = jnp.array([leading_size, 4, 4], jnp.float32)
    fractional_position = (
        grid_positions(neighbour_list) - grid_positions(kpoint_index)[..., None, :]
    ).astype(jnp.float32) / grid_sizes
    fractional_position = fractional_position + shifts.astype(jnp.float32)
    cart_x = (
        -fractional_position[..., 0] + fractional_position[..., 1] + fractional_position[..., 2]
    )
    cart_y = fractional_position[..., 0] - fractional_position[..., 1] + fractional_position[..., 2]
    cart_z = fractional_position[..., 0] + fractional_position[..., 1] - fractional_position[..., 2]
    return 3.0 / (len(SHELL_LIST) * (cart_x * cart_x + cart_y * cart_y + cart_z * cart_z))


def cprod(form, ar, ai, br, bi, conj_left, conj_right, precision=None):
    sign_a = -1.0 if conj_left else 1.0
    sign_b = -1.0 if conj_right else 1.0
    e = lambda p, q: jnp.einsum(form, p, q, preferred_element_type=jnp.float32, precision=precision)
    real = e(ar, br) - sign_a * sign_b * e(ai, bi)
    imag = sign_b * e(ar, bi) + sign_a * e(ai, br)
    return (real, imag)


def outside(coord, step):
    moved = coord + step
    return jnp.logical_or(moved < 0, moved > 3)


def fetch(own, disp, lattice_positions, kpts):
    result = jnp.zeros_like(own)
    first = [0, 1] if disp[1] != 0 else [0]
    second = [0, 1] if disp[2] != 0 else [0]
    wrap_one = outside(lattice_positions[1], disp[1])
    wrap_two = outside(lattice_positions[2], disp[2])
    for flag_one in first:
        for flag_two in second:
            offset = (
                16 * disp[0]
                + 4 * (disp[1] - 4 * disp[1] * flag_one)
                + (disp[2] - 4 * disp[2] * flag_two)
            )
            amount = -offset % kpts
            moved = shifted(own, "ka", amount)
            match = jnp.logical_and(wrap_one == (flag_one == 1), wrap_two == (flag_two == 1))
            result = jnp.where(match, moved, result)
    return result


def local_terms(mtr, mti, shell_weights, kpts, width):
    mr, mi = (mtr.astype(jnp.float32), mti.astype(jnp.float32))
    wts = shell_weights[:, None, None]
    hr, hi = cprod("bmn,bkn->mk", wts * mr, wts * mi, mr, mi, False, True, product_precision)
    diag_r = jnp.diagonal(mr, 0, 1, 2)[:, None, :]
    diag_i = jnp.diagonal(mi, 0, 1, 2)[:, None, :]
    rr = mr * diag_r + mi * diag_i
    ri = mi * diag_r - mr * diag_i
    gr = 2.0 * jnp.sum(wts * (rr - jnp.swapaxes(rr, 1, 2)), 0)
    gi = 2.0 * jnp.sum(wts * (ri + jnp.swapaxes(ri, 1, 2)), 0)
    square = mr * mr + mi * mi
    offdiag = jnp.sum(square, (1, 2)) - jnp.sum(jnp.diagonal(square, 0, 1, 2), 1)
    omega = jnp.sum(shell_weights * offdiag) / (kpts * width)
    return (gr, gi, hr, hi, omega)


def gram(xr, xi):
    return cprod("rm,rn->mn", xr, xi, xr, xi, True, False, product_precision)


def newton_schulz(xr, xi, summed):
    width = xr.shape[1]
    sr, si = summed(xr, xi)
    scale = jnp.sqrt(width / (2.0 * jnp.trace(sr)))
    xr, xi = (xr * scale, xi * scale)
    sr, si = (sr * scale * scale, si * scale * scale)
    eye = jnp.eye(width, dtype=jnp.float32)
    for turn in range(NS_STEPS):
        xr, xi = cprod(
            "rm,mn->rn", xr, xi, (3.0 * eye - sr) / 2.0, -si / 2.0, False, False, product_precision
        )
        if turn + 1 < NS_STEPS:
            sr, si = summed(xr, xi)
    return (xr, xi)


def per_device(correlations, gauge, neighbours, shifts):
    bf = jnp.bfloat16
    kpts = lax.axis_size("ka")
    ncol = lax.axis_size("col")
    kpoint_index = lax.axis_index("ka")
    cindex = lax.axis_index("col")
    mats = correlations[0]
    own = gauge[0]
    rows = own.shape[0]
    width = own.shape[2]
    vectors = mats.shape[0]
    lattice_positions = (kpoint_index // 16, kpoint_index // 4 % 4, kpoint_index % 4)
    slots = jnp.stack([fetch(own, disp, lattice_positions, kpts) for disp in SHELL_LIST])
    leading_size = kpts // 16
    grid_sizes = jnp.array([leading_size, 4, 4], jnp.int32)
    moved = (
        grid_positions(neighbours[0])
        - jnp.stack(lattice_positions)[None, :]
        + shifts[0] * grid_sizes
    )
    table = jnp.array(SHELL_LIST, jnp.int32)
    onehot = jnp.all(moved[:, None, :] == table[None, :, :], -1).astype(bf)
    chosen = jnp.einsum("bs,srcw->brcw", onehot, slots, preferred_element_type=jnp.float32).astype(
        bf
    )
    shell_weights = shell_vector_weights(kpoint_index, neighbours[0], shifts[0], leading_size)
    owned = vectors // ncol
    mats = lax.all_to_all(mats, "col", split_axis=0, concat_axis=2, tiled=True)
    chosen = lax.all_to_all(chosen, "col", split_axis=0, concat_axis=1, tiled=True)
    shell_weights = lax.dynamic_slice_in_dim(shell_weights, cindex * owned, owned)
    count = mats.shape[0]
    cols = mats.shape[2]
    piece = gathered_copies(own, "col", 0)
    block = mats
    real, imag = cprod(
        "rw,bcr->bwc", piece[:, 0], piece[:, 1], block[:, 0], block[:, 1], True, False
    )
    qr = real
    qi = imag
    qr, qi = (qr.astype(bf), qi.astype(bf))
    blocks = cols // ncol
    qbr = qr.reshape(count, width, ncol, blocks)
    qbi = qi.reshape(count, width, ncol, blocks)
    near_r = chosen[:, :, 0].reshape(count, ncol, blocks, width)
    near_i = chosen[:, :, 1].reshape(count, ncol, blocks, width)
    pr, pi = cprod("bwgc,bgcn->bgwn", qbr, qbi, near_r, near_i, False, False)
    mtr = jnp.sum(pr.astype(bf).astype(jnp.float32), 1).astype(bf)
    mti = jnp.sum(pi.astype(bf).astype(jnp.float32), 1).astype(bf)
    vr, vi = cprod("brm,bnm->brn", chosen[:, :, 0], chosen[:, :, 1], mtr, mti, False, True)
    vr = (shell_weights[:, None, None] * vr).astype(bf)
    vi = (shell_weights[:, None, None] * vi).astype(bf)
    block = mats
    real, imag = cprod("bji,bjn->in", block[:, 0], block[:, 1], vr, vi, False, False)
    ysum = sent_and_summed(jnp.concatenate([real, imag], 1).astype(jnp.bfloat16), "col", 0)
    gr, gi, hr, hi, omega = local_terms(mtr, mti, shell_weights, kpts, width)
    gr, gi, hr, hi, omega = tuple(
        (
            part.astype(jnp.float32)
            for part in together(
                (
                    gr.astype(jnp.bfloat16),
                    gi.astype(jnp.bfloat16),
                    hr.astype(jnp.bfloat16),
                    hi.astype(jnp.bfloat16),
                    omega.astype(jnp.bfloat16),
                ),
                "col",
            )
        )
    )
    omega = of_everyone(omega, "ka")
    ur, ui = (own[:, 0].astype(jnp.float32), own[:, 1].astype(jnp.float32))
    uhr, uhi = cprod("rm,mn->rn", ur, ui, hr, hi, False, False, product_precision)
    ugr, ugi = cprod("rm,mn->rn", ur, ui, gr, gi, False, False, product_precision)
    xr = ur + MIXING * (ysum[:, :width] - uhr) + STEP_LENGTH * ugr
    xi = ui + MIXING * (ysum[:, width:] - uhi) + STEP_LENGTH * ugi
    full_r, full_i = tuple(
        (
            part.astype(jnp.float32)
            for part in gather_packed(
                (xr.astype(jnp.bfloat16), xi.astype(jnp.bfloat16)), "col", (0, 0)
            )
        )
    )
    full_r, full_i = newton_schulz(full_r, full_i, gram)
    xr = lax.dynamic_slice_in_dim(full_r, cindex * rows, rows, 0)
    xi = lax.dynamic_slice_in_dim(full_i, cindex * rows, rows, 0)
    share = width // ncol
    grad_r = lax.dynamic_slice_in_dim(gr, cindex * share, share, 0)
    grad_i = lax.dynamic_slice_in_dim(gi, cindex * share, share, 0)
    u_next = jnp.stack([xr, xi], 1)[None]
    gradient = jnp.stack([grad_r, grad_i], 0)[None]
    return (u_next, gradient, omega)


def solution(mesh):
    return jax.shard_map(
        per_device,
        mesh=mesh,
        in_specs=(
            P("ka", None, None, "col", None),
            P("ka", "col", None, None),
            P("ka", None),
            P("ka", None, None),
        ),
        out_specs=(P("ka", "col", None, None), P("ka", None, "col", None), P()),
        check_vma=False,
    )
```

profile of v0, /device:TPU:2, one launch (start us, length us, event | category | flops | bytes accessed | tf_op | source)
XLA Modules:
  0.0 500.4 jit_solution(1954790179767988330)
XLA Ops:
  8.0 4.5 collective-permute-start.15
  12.5 15.4 %collective-permute-start.14 = (bf16[64,2,256]{2,0,1:T(8,128)(2,1)S(1)}, bf16[64,2,256]{2,0,1:T(8,128)(2,1)S(1)}, u32[]{:S(2)}, u32[]{:S(2)}) collective-permute-start(bf16[64,2,256]{2,0,1:T(8,128)(2,1)S(1)} %bitcast.356), channel_id=1, source_target_pairs={{0,136},{8,144},{16,152},{24,160},{32,168},{40,176},{48,184},{56,1... | collective-permute-start | bytes 196616 | tf_op jit(solution)/shard_map/ppermute | solution.py:26
  27.9 5.9 %collective-permute-start.13 = (bf16[64,2,256]{2,0,1:T(8,128)(2,1)S(1)}, bf16[64,2,256]{2,0,1:T(8,128)(2,1)S(1)}, u32[]{:S(2)}, u32[]{:S(2)}) collective-permute-start(bf16[64,2,256]{2,0,1:T(8,128)(2,1)S(1)} %bitcast.357), channel_id=1, source_target_pairs={{0,40},{8,48},{16,56},{24,64},{32,72},{40,80},{48,88},{56,96},{64,... | collective-permute-start | bytes 196616 | tf_op jit(solution)/shard_map/ppermute | solution.py:26
  35.8 15.9 %collective-permute-start.8 = (bf16[64,2,256]{2,0,1:T(8,128)(2,1)S(1)}, bf16[64,2,256]{2,0,1:T(8,128)(2,1)S(1)}, u32[]{:S(2)}, u32[]{:S(2)}) collective-permute-start(bf16[64,2,256]{2,0,1:T(8,128)(2,1)S(1)} %bitcast.359), channel_id=1, source_target_pairs={{0,488},{8,496},{16,504},{24,0},{32,8},{40,16},{48,24},{56,32},{64... | collective-permute-start | bytes 196616 | tf_op jit(solution)/shard_map/ppermute | solution.py:26
  52.6 5.0 %all-to-all-start.2 = ((bf16[8,64,2,256]{3,1,2,0:T(8,128)(2,1)}), bf16[8,64,2,256]{3,1,2,0:T(8,128)(2,1)S(1)}, u32[]{:S(2)}, u32[]{:S(2)}) async-start(bf16[8,64,2,256]{3,1,2,0:T(8,128)(2,1)} %broadcast_in_dim.19), calls=%async_computation.2 | async-start | bytes 1048576 | tf_op jit(solution)/shard_map/all_to_all | solution.py:31
  63.8 6.8 %collective-permute-start.10 = (bf16[64,2,256]{2,0,1:T(8,128)(2,1)S(1)}, bf16[64,2,256]{2,0,1:T(8,128)(2,1)S(1)}, u32[]{:S(2)}, u32[]{:S(2)}) collective-permute-start(bf16[64,2,256]{2,0,1:T(8,128)(2,1)S(1)} %bitcast.363), channel_id=1, source_target_pairs={{0,472},{8,480},{16,488},{24,496},{32,504},{40,0},{48,8},{56,16},{... | collective-permute-start | bytes 196616 | tf_op jit(solution)/shard_map/ppermute | solution.py:26
  70.6 2.9 collective-permute-start.7
  73.5 4.7 collective-permute-start.6
  78.3 9.3 %collective-permute-start.5 = (bf16[64,2,256]{2,0,1:T(8,128)(2,1)S(1)}, bf16[64,2,256]{2,0,1:T(8,128)(2,1)S(1)}, u32[]{:S(2)}, u32[]{:S(2)}) collective-permute-start(bf16[64,2,256]{2,0,1:T(8,128)(2,1)S(1)} %bitcast.366), channel_id=1, source_target_pairs={{0,32},{8,40},{16,48},{24,56},{32,64},{40,72},{48,80},{56,88},{64,... | collective-permute-start | bytes 196616 | tf_op jit(solution)/shard_map/ppermute | solution.py:26
  87.5 5.7 %collective-permute-start.4 = (bf16[64,2,256]{2,0,1:T(8,128)(2,1)S(1)}, bf16[64,2,256]{2,0,1:T(8,128)(2,1)S(1)}, u32[]{:S(2)}, u32[]{:S(2)}) collective-permute-start(bf16[64,2,256]{2,0,1:T(8,128)(2,1)S(1)} %bitcast.367), channel_id=1, source_target_pairs={{0,416},{8,424},{16,432},{24,440},{32,448},{40,456},{48,464},{56,4... | collective-permute-start | bytes 196616 | tf_op jit(solution)/shard_map/ppermute | solution.py:26
  93.2 12.5 %collective-permute-start.3 = (bf16[64,2,256]{2,0,1:T(8,128)(2,1)S(1)}, bf16[64,2,256]{2,0,1:T(8,128)(2,1)S(1)}, u32[]{:S(2)}, u32[]{:S(2)}) collective-permute-start(bf16[64,2,256]{2,0,1:T(8,128)(2,1)S(1)} %bitcast.368), channel_id=1, source_target_pairs={{0,480},{8,488},{16,496},{24,504},{32,0},{40,8},{48,16},{56,24},{6... | collective-permute-start | bytes 196616 | tf_op jit(solution)/shard_map/ppermute | solution.py:26
  110.0 4.8 collective-permute-start
  119.4 27.9 %all_to_all.46 = bf16[8,64,2,256]{3,2,1,0:T(2,128)(2,1)S(1)} all-to-all(bf16[8,64,2,256]{3,2,1,0:T(2,128)(2,1)S(1)} %copy.270), channel_id=1, replica_groups=mesh['ka'=64,'col'=8] {'col'}, dimensions={0} | all-to-all | bytes 1048576 | tf_op jit(solution)/shard_map/all_to_all | solution.py:196
  147.3 14.6 %all-to-all-start.1 = ((bf16[8,2,64,512]{3,2,1,0:T(8,128)(2,1)}), bf16[8,2,64,512]{3,2,1,0:T(8,128)(2,1)S(1)}, u32[]{:S(2)}, u32[]{:S(2)}) async-start(bf16[8,2,64,512]{3,2,1,0:T(8,128)(2,1)} %bitcast.388), calls=%async_computation.1 | async-start | bytes 2097152 | tf_op jit(solution)/shard_map/all_to_all | solution.py:195
  163.5 50.9 %all-to-all-done.1 = bf16[8,2,64,512]{3,2,1,0:T(8,128)(2,1)S(1)} async-done(((bf16[8,2,64,512]{3,2,1,0:T(8,128)(2,1)}), bf16[8,2,64,512]{3,2,1,0:T(8,128)(2,1)S(1)}, u32[]{:S(2)}, u32[]{:S(2)}) %all-to-all-start.1) | async-done | bytes 1048608 | tf_op jit(solution)/shard_map/all_to_all | solution.py:195
  231.8 2.3 gather_fusion.1
  234.2 2.3 gather_fusion
  237.0 2.3 gather_fusion.2
  247.3 122.1 %all-reduce.2.cloned.1.call-done = bf16[262145]{0:T(1024)(128)(2,1)} async-done(((bf16[262145]{0:T(1024)(128)(2,1)}), bf16[262145]{0:T(1024)(128)(2,1)}) %all-reduce.2.cloned.1.call-update) | async-done | bytes 524306 | tf_op jit(solution)/shard_map/psum | solution.py:59
  371.9 10.5 %all-to-all-start.4 = ((f32[64,1,1]{2,1,0:T(1,128)}), f32[64,1,1]{2,1,0:T(1,128)S(1)}, u32[]{:S(2)}, u32[]{:S(2)}) async-start(f32[64,1,1]{2,1,0:T(1,128)} %broadcast_in_dim.24), calls=%async_computation.4 | async-start | bytes 65536 | tf_op jit(solution)/shard_map/all_to_all | solution.py:31
  383.2 14.8 %all-to-all-done.4 = f32[64,1,1]{2,1,0:T(1,128)S(1)} async-done(((f32[64,1,1]{2,1,0:T(1,128)}), f32[64,1,1]{2,1,0:T(1,128)S(1)}, u32[]{:S(2)}, u32[]{:S(2)}) %all-to-all-start.4) | async-done | bytes 288 | tf_op jit(solution)/shard_map/all_to_all | solution.py:31
  398.0 9.0 %all-to-all-start.3 = ((bf16[8,64,512]{2,1,0:T(8,128)(2,1)}), bf16[8,64,512]{2,1,0:T(8,128)(2,1)S(1)}, u32[]{:S(2)}, u32[]{:S(2)}) async-start(bf16[8,64,512]{2,1,0:T(8,128)(2,1)} %pad_maximum_fusion), calls=%async_computation.3 | async-start | bytes 1048576 | tf_op jit(solution)/shard_map/all_to_all | solution.py:53
  409.6 26.2 %all-to-all-done.3 = bf16[8,64,512]{2,1,0:T(8,128)(2,1)S(1)} async-done(((bf16[8,64,512]{2,1,0:T(8,128)(2,1)}), bf16[8,64,512]{2,1,0:T(8,128)(2,1)S(1)}, u32[]{:S(2)}, u32[]{:S(2)}) %all-to-all-start.3) | async-done | bytes 524320 | tf_op jit(solution)/shard_map/all_to_all | solution.py:53
  436.3 48.3 %all-gather = bf16[262144]{0:T(1024)(128)(2,1)S(1)} all-gather(bf16[32768]{0:T(1024)(128)(2,1)S(1)} %pad_maximum_fusion.1), channel_id=2, replica_groups=mesh['ka'=64,'col'=8] {'col'}, dimensions={0}, use_global_device_ids=true | all-gather | bytes 589824 | tf_op jit(solution)/shard_map/all_gather | solution.py:72
  (176 shorter events, 58.6 us)
Async XLA Ops:
  8.0 51.9 %collective-permute-start.15 = (bf16[64,2,256]{2,0,1:T(8,128)(2,1)S(1)}, bf16[64,2,256]{2,0,1:T(8,128)(2,1)S(1)}, u32[]{:S(2)}, u32[]{:S(2)}) collective-permute-start(bf16[64,2,256]{2,0,1:T(8,128)(2,1)S(1)} %bitcast.355), channel_id=1, source_target_pairs={{0,168},{8,176},{16,184},{24,192},{32,200},{40,208},{48,216},{56,2... | collective-permute-start | bytes 196616 | tf_op jit(solution)/shard_map/ppermute | solution.py:26
  12.5 49.4 %collective-permute-start.14 = (bf16[64,2,256]{2,0,1:T(8,128)(2,1)S(1)}, bf16[64,2,256]{2,0,1:T(8,128)(2,1)S(1)}, u32[]{:S(2)}, u32[]{:S(2)}) collective-permute-start(bf16[64,2,256]{2,0,1:T(8,128)(2,1)S(1)} %bitcast.356), channel_id=1, source_target_pairs={{0,136},{8,144},{16,152},{24,160},{32,168},{40,176},{48,184},{56,1... | collective-permute-start | bytes 196616 | tf_op jit(solution)/shard_map/ppermute | solution.py:26
  27.9 35.9 %collective-permute-start.13 = (bf16[64,2,256]{2,0,1:T(8,128)(2,1)S(1)}, bf16[64,2,256]{2,0,1:T(8,128)(2,1)S(1)}, u32[]{:S(2)}, u32[]{:S(2)}) collective-permute-start(bf16[64,2,256]{2,0,1:T(8,128)(2,1)S(1)} %bitcast.357), channel_id=1, source_target_pairs={{0,40},{8,48},{16,56},{24,64},{32,72},{40,80},{48,88},{56,96},{64,... | collective-permute-start | bytes 196616 | tf_op jit(solution)/shard_map/ppermute | solution.py:26
  33.8 36.8 %collective-permute-start.9 = (bf16[64,2,256]{2,0,1:T(8,128)(2,1)S(1)}, bf16[64,2,256]{2,0,1:T(8,128)(2,1)S(1)}, u32[]{:S(2)}, u32[]{:S(2)}) collective-permute-start(bf16[64,2,256]{2,0,1:T(8,128)(2,1)S(1)} %bitcast.358), channel_id=1, source_target_pairs={{0,8},{8,16},{16,24},{24,32},{32,40},{40,48},{48,56},{56,64},{64,7... | collective-permute-start | bytes 196616 | tf_op jit(solution)/shard_map/ppermute | solution.py:26
  35.8 37.7 %collective-permute-start.8 = (bf16[64,2,256]{2,0,1:T(8,128)(2,1)S(1)}, bf16[64,2,256]{2,0,1:T(8,128)(2,1)S(1)}, u32[]{:S(2)}, u32[]{:S(2)}) collective-permute-start(bf16[64,2,256]{2,0,1:T(8,128)(2,1)S(1)} %bitcast.359), channel_id=1, source_target_pairs={{0,488},{8,496},{16,504},{24,0},{32,8},{40,16},{48,24},{56,32},{64... | collective-permute-start | bytes 196616 | tf_op jit(solution)/shard_map/ppermute | solution.py:26
  52.6 66.8 %all-to-all-start.2 = ((bf16[8,64,2,256]{3,1,2,0:T(8,128)(2,1)}), bf16[8,64,2,256]{3,1,2,0:T(8,128)(2,1)S(1)}, u32[]{:S(2)}, u32[]{:S(2)}) async-start(bf16[8,64,2,256]{3,1,2,0:T(8,128)(2,1)} %broadcast_in_dim.19), calls=%async_computation.2 | async-start | bytes 1048576 | tf_op jit(solution)/shard_map/all_to_all | solution.py:31
  59.9 18.3 %collective-permute-start.12 = (bf16[64,2,256]{2,0,1:T(8,128)(2,1)S(1)}, bf16[64,2,256]{2,0,1:T(8,128)(2,1)S(1)}, u32[]{:S(2)}, u32[]{:S(2)}) collective-permute-start(bf16[64,2,256]{2,0,1:T(8,128)(2,1)S(1)} %bitcast.361), channel_id=1, source_target_pairs={{0,344},{8,352},{16,360},{24,368},{32,376},{40,384},{48,392},{56,4... | collective-permute-start | bytes 196616 | tf_op jit(solution)/shard_map/ppermute | solution.py:26
  61.9 25.6 %collective-permute-start.11 = (bf16[64,2,256]{2,0,1:T(8,128)(2,1)S(1)}, bf16[64,2,256]{2,0,1:T(8,128)(2,1)S(1)}, u32[]{:S(2)}, u32[]{:S(2)}) collective-permute-start(bf16[64,2,256]{2,0,1:T(8,128)(2,1)S(1)} %bitcast.362), channel_id=1, source_target_pairs={{0,376},{8,384},{16,392},{24,400},{32,408},{40,416},{48,424},{56,4... | collective-permute-start | bytes 196616 | tf_op jit(solution)/shard_map/ppermute | solution.py:26
  63.8 29.4 %collective-permute-start.10 = (bf16[64,2,256]{2,0,1:T(8,128)(2,1)S(1)}, bf16[64,2,256]{2,0,1:T(8,128)(2,1)S(1)}, u32[]{:S(2)}, u32[]{:S(2)}) collective-permute-start(bf16[64,2,256]{2,0,1:T(8,128)(2,1)S(1)} %bitcast.363), channel_id=1, source_target_pairs={{0,472},{8,480},{16,488},{24,496},{32,504},{40,0},{48,8},{56,16},{... | collective-permute-start | bytes 196616 | tf_op jit(solution)/shard_map/ppermute | solution.py:26
  70.6 35.2 %collective-permute-start.7 = (bf16[64,2,256]{2,0,1:T(8,128)(2,1)S(1)}, bf16[64,2,256]{2,0,1:T(8,128)(2,1)S(1)}, u32[]{:S(2)}, u32[]{:S(2)}) collective-permute-start(bf16[64,2,256]{2,0,1:T(8,128)(2,1)S(1)} %bitcast.364), channel_id=1, source_target_pairs={{0,504},{8,0},{16,8},{24,16},{32,24},{40,32},{48,40},{56,48},{64,5... | collective-permute-start | bytes 196616 | tf_op jit(solution)/shard_map/ppermute | solution.py:26
  73.5 34.2 %collective-permute-start.6 = (bf16[64,2,256]{2,0,1:T(8,128)(2,1)S(1)}, bf16[64,2,256]{2,0,1:T(8,128)(2,1)S(1)}, u32[]{:S(2)}, u32[]{:S(2)}) collective-permute-start(bf16[64,2,256]{2,0,1:T(8,128)(2,1)S(1)} %bitcast.365), channel_id=1, source_target_pairs={{0,24},{8,32},{16,40},{24,48},{32,56},{40,64},{48,72},{56,80},{64,... | collective-permute-start | bytes 196616 | tf_op jit(solution)/shard_map/ppermute | solution.py:26
  78.3 31.7 %collective-permute-start.5 = (bf16[64,2,256]{2,0,1:T(8,128)(2,1)S(1)}, bf16[64,2,256]{2,0,1:T(8,128)(2,1)S(1)}, u32[]{:S(2)}, u32[]{:S(2)}) collective-permute-start(bf16[64,2,256]{2,0,1:T(8,128)(2,1)S(1)} %bitcast.366), channel_id=1, source_target_pairs={{0,32},{8,40},{16,48},{24,56},{32,64},{40,72},{48,80},{56,88},{64,... | collective-permute-start | bytes 196616 | tf_op jit(solution)/shard_map/ppermute | solution.py:26
  87.5 27.3 %collective-permute-start.4 = (bf16[64,2,256]{2,0,1:T(8,128)(2,1)S(1)}, bf16[64,2,256]{2,0,1:T(8,128)(2,1)S(1)}, u32[]{:S(2)}, u32[]{:S(2)}) collective-permute-start(bf16[64,2,256]{2,0,1:T(8,128)(2,1)S(1)} %bitcast.367), channel_id=1, source_target_pairs={{0,416},{8,424},{16,432},{24,440},{32,448},{40,456},{48,464},{56,4... | collective-permute-start | bytes 196616 | tf_op jit(solution)/shard_map/ppermute | solution.py:26
  93.2 21.6 %collective-permute-start.3 = (bf16[64,2,256]{2,0,1:T(8,128)(2,1)S(1)}, bf16[64,2,256]{2,0,1:T(8,128)(2,1)S(1)}, u32[]{:S(2)}, u32[]{:S(2)}) collective-permute-start(bf16[64,2,256]{2,0,1:T(8,128)(2,1)S(1)} %bitcast.368), channel_id=1, source_target_pairs={{0,480},{8,488},{16,496},{24,504},{32,0},{40,8},{48,16},{56,24},{6... | collective-permute-start | bytes 196616 | tf_op jit(solution)/shard_map/ppermute | solution.py:26
  105.8 9.9 %collective-permute-start.2 = (bf16[64,2,256]{2,0,1:T(8,128)(2,1)S(1)}, bf16[64,2,256]{2,0,1:T(8,128)(2,1)S(1)}, u32[]{:S(2)}, u32[]{:S(2)}) collective-permute-start(bf16[64,2,256]{2,0,1:T(8,128)(2,1)S(1)} %bitcast.369), channel_id=1, source_target_pairs={{0,96},{8,104},{16,112},{24,120},{32,128},{40,136},{48,144},{56,15... | collective-permute-start | bytes 196616 | tf_op jit(solution)/shard_map/ppermute | solution.py:26
  107.7 8.1 %collective-permute-start.1 = (bf16[64,2,256]{2,0,1:T(8,128)(2,1)S(1)}, bf16[64,2,256]{2,0,1:T(8,128)(2,1)S(1)}, u32[]{:S(2)}, u32[]{:S(2)}) collective-permute-start(bf16[64,2,256]{2,0,1:T(8,128)(2,1)S(1)} %bitcast.370), channel_id=1, source_target_pairs={{0,128},{8,136},{16,144},{24,152},{32,160},{40,168},{48,176},{56,1... | collective-permute-start | bytes 196616 | tf_op jit(solution)/shard_map/ppermute | solution.py:26
  110.0 6.7 %collective-permute-start = (bf16[64,2,256]{2,0,1:T(8,128)(2,1)S(1)}, bf16[64,2,256]{2,0,1:T(8,128)(2,1)S(1)}, u32[]{:S(2)}, u32[]{:S(2)}) collective-permute-start(bf16[64,2,256]{2,0,1:T(8,128)(2,1)S(1)} %bitcast.371), channel_id=1, source_target_pairs={{0,384},{8,392},{16,400},{24,408},{32,416},{40,424},{48,432},{56,4... | collective-permute-start | bytes 196616 | tf_op jit(solution)/shard_map/ppermute | solution.py:26
  147.3 67.1 %all-to-all-start.1 = ((bf16[8,2,64,512]{3,2,1,0:T(8,128)(2,1)}), bf16[8,2,64,512]{3,2,1,0:T(8,128)(2,1)S(1)}, u32[]{:S(2)}, u32[]{:S(2)}) async-start(bf16[8,2,64,512]{3,2,1,0:T(8,128)(2,1)} %bitcast.388), calls=%async_computation.1 | async-start | bytes 2097152 | tf_op jit(solution)/shard_map/all_to_all | solution.py:195
  161.9 207.5 %all-reduce.2.cloned.1.call-start = ((), (), s32[]{:S(2)}) async-start(), calls=%async_computation.5 | async-start | bytes 1052672 | tf_op jit(solution)/shard_map/psum | solution.py:59
  163.5 52.2 %copy-start = (bf16[1,512,1,256]{3,1,2,0:T(8,128)(2,1)}, bf16[1,512,1,256]{3,1,2,0:T(8,128)(2,1)S(1)}, u32[]{:S(2)}) copy-start(bf16[1,512,1,256]{3,1,2,0:T(8,128)(2,1)S(1)} %get-tuple-element.10) | copy-start | bytes 786436
  219.7 5.7 %copy-start.3 = (f32[512,256]{1,0:T(8,128)S(1)}, f32[512,256]{1,0:T(8,128)}, u32[]{:S(2)}) copy-start(f32[512,256]{1,0:T(8,128)} %convolution_multiply_fusion) | copy-start | bytes 1572868
  369.3 37.7 %copy-start.9 = (bf16[262145]{0:T(1024)(128)(2,1)S(1)}, bf16[262145]{0:T(1024)(128)(2,1)}, u32[]{:S(2)}) copy-start(bf16[262145]{0:T(1024)(128)(2,1)} %all-reduce.2.cloned.1.call-done) | copy-start | bytes 1572874
  371.9 26.1 %all-to-all-start.4 = ((f32[64,1,1]{2,1,0:T(1,128)}), f32[64,1,1]{2,1,0:T(1,128)S(1)}, u32[]{:S(2)}, u32[]{:S(2)}) async-start(f32[64,1,1]{2,1,0:T(1,128)} %broadcast_in_dim.24), calls=%async_computation.4 | async-start | bytes 65536 | tf_op jit(solution)/shard_map/all_to_all | solution.py:31
  398.0 37.8 %all-to-all-start.3 = ((bf16[8,64,512]{2,1,0:T(8,128)(2,1)}), bf16[8,64,512]{2,1,0:T(8,128)(2,1)S(1)}, u32[]{:S(2)}, u32[]{:S(2)}) async-start(bf16[8,64,512]{2,1,0:T(8,128)(2,1)} %pad_maximum_fusion), calls=%async_computation.3 | async-start | bytes 1048576 | tf_op jit(solution)/shard_map/all_to_all | solution.py:53
  (7 other events, 24.1 us)
Sparse Core Ops, SparseCore 0:
  246.1 123.1 all-reduce.1
where the time goes:
time: 502 us; the launch traced here: 500 us
  waiting for transfers between devices  215 us (43%)
  starting transfers between devices  137 us (27%)
  blocking collectives  76.2 us (15%)
  local copies, waits for them, and re-layouts  22.7 us (5%)
  matrix products  21.6 us (4%)
  between operations  17.2 us (3%)
  other arithmetic  10 us (2%)
    psum x1, waiting for transfers between devices, together(): running = lax.psum(vector, axis)  122 us
    ppermute x16, starting transfers between devices, shifted(): lax.ppermute(x, axis, [(i, (i + by) % length) for i in range(length)])  98.3 us
    all_to_all x1, waiting for transfers between devices, per_device(): mats = lax.all_to_all(mats, 'col', split_axis=0, concat_axis=2, tiled=True)  50.9 us
    all_gather x1, blocking collectives, gather_packed(): lines, at, gathered = (lax.all_gather(vector, axis), 0, [])  48.3 us
    all_to_all x1, blocking collectives, per_device(): lax.all_to_all(chosen, 'col', split_axis=0, concat_axis=1, tiled=True)  27.9 us
    all_to_all x1, waiting for transfers between devices, sent_and_summed(): lax.all_to_all(parts, axis, split_axis=0, concat_axis=0, tiled=True)  26.2 us
    dot_general x52, matrix products, cprod(): jnp.einsum(form, p, q, preferred_element_type=jnp.float32, precision=prec...  21.4 us
    all_to_all x2, starting transfers between devices, from_everyone(): lax.all_to_all(jnp.broadcast_to(x[None], (length, *x.shape)), axis, 0, 0,...  15.5 us
  transfers between devices with their start and end apart: 21, of which 7 were waited for; matrix products, arithmetic and copies ran while one was open for 3% of the time, Pallas kernels for 0%

commit v1 on v0

v1 whole, which is shorter than its diff:
```python
import jax
import jax.numpy as jnp
from jax import lax
from jax.experimental import pallas as pl
from jax.experimental.pallas import tpu as pltpu
from jax.sharding import PartitionSpec as P

MIXING = 0.02
STEP_LENGTH = 0.2
SHELL_LIST = [
    (1, 0, 0),
    (-1, 0, 0),
    (0, 1, 0),
    (0, -1, 0),
    (0, 0, 1),
    (0, 0, -1),
    (1, 1, 1),
    (-1, -1, -1),
]
HALVES = [[0, 1, 2, 3], [4, 5, 6, 7]]
F32 = jnp.float32
BF = jnp.bfloat16


def dot(a, b):
    return lax.dot_general(a, b, (((1,), (0,)), ((), ())), preferred_element_type=F32)


def dot_nt(a, b):
    return lax.dot_general(a, b, (((1,), (1,)), ((), ())), preferred_element_type=F32)


def grid_positions(index):
    return jnp.stack([index // 16, index // 4 % 4, index % 4], -1)


def shell_vector_weights(kpoint_index, neighbour_list, shifts):
    grid_sizes = jnp.array([4, 4, 4], F32)
    f = (grid_positions(neighbour_list) - grid_positions(kpoint_index)[..., None, :]).astype(
        F32
    ) / grid_sizes
    f = f + shifts.astype(F32)
    cx = -f[..., 0] + f[..., 1] + f[..., 2]
    cy = f[..., 0] - f[..., 1] + f[..., 2]
    cz = f[..., 0] + f[..., 1] - f[..., 2]
    return 3.0 / (len(SHELL_LIST) * (cx * cx + cy * cy + cz * cz))


def slot_of(dx, dy, dz):
    diagonal = jnp.logical_and(dx != 0, dy != 0)
    pair = jnp.where(diagonal, 3, jnp.where(dx != 0, 0, jnp.where(dy != 0, 1, 2)))
    return 2 * pair + jnp.where(dx + dy + dz < 0, 1, 0)


def sort_kernel(k_ref, near_ref, shift_ref, m_ref, out_ref, sems):
    k = k_ref[0]
    copies = []
    for b in range(8):
        q = near_ref[b]
        dx = q // 16 - k // 16 + 4 * shift_ref[b, 0]
        dy = q // 4 % 4 - k // 4 % 4 + 4 * shift_ref[b, 1]
        dz = q % 4 - k % 4 + 4 * shift_ref[b, 2]
        slot = slot_of(dx, dy, dz)
        copy = pltpu.make_async_copy(m_ref.at[b], out_ref.at[slot], sems.at[b])
        copy.start()
        copies.append(copy)
    for copy in copies:
        copy.wait()


def sorted_by_displacement(kpoint_index, near, shifts, mats):
    smem = pl.BlockSpec(memory_space=pltpu.SMEM)
    hbm = pl.BlockSpec(memory_space=pl.ANY)
    return pl.pallas_call(
        sort_kernel,
        out_shape=jax.ShapeDtypeStruct(mats.shape, mats.dtype),
        in_specs=[smem, smem, smem, hbm],
        out_specs=hbm,
        scratch_shapes=[pltpu.SemaphoreType.DMA((8,))],
        name="sort_mats",
    )(kpoint_index.reshape(1), near, shifts, mats)


def rows_in_order(ref):
    return jnp.concatenate([ref[l, h] for h in range(2) for l in range(4)], 0)


def main_kernel(w_ref, m_ref, u_ref, n_ref, z_ref, g_ref, omega_ref):
    w = w_ref[0]
    a_r = m_ref[:, 0].reshape(512, 512)
    a_i = m_ref[:, 1].reshape(512, 512)
    u = rows_in_order(u_ref)
    n = rows_in_order(n_ref)
    ut = u.T
    p = dot_nt(ut, a_r)
    q = dot_nt(ut, a_i)
    qs = jnp.concatenate([p[:256] + q[256:], q[:256] - p[256:]], 0).astype(BF)
    p = dot(qs, n)
    mt_r = (p[:256, :256] - p[256:, 256:]).astype(BF)
    mt_i = (p[:256, 256:] + p[256:, :256]).astype(BF)
    mts = jnp.concatenate([mt_r, mt_i], 0)
    p = dot_nt(mts, n[:, :256])
    q = dot_nt(mts, n[:, 256:])
    vts = (w * jnp.concatenate([p[:256] + q[256:], q[:256] - p[256:]], 0)).astype(BF)
    p = dot_nt(mts, mts)
    h_r = w * (p[:256, :256] + p[256:, 256:])
    h_i = w * (p[256:, :256] - p[:256, 256:])
    mr, mi = mt_r.astype(F32), mt_i.astype(F32)
    row = lax.broadcasted_iota(jnp.int32, (256, 256), 0)
    col = lax.broadcasted_iota(jnp.int32, (256, 256), 1)
    eye = row == col
    zero = jnp.zeros_like(mr)
    only_r, only_i = jnp.where(eye, mr, zero), jnp.where(eye, mi, zero)
    row_r, row_i = only_r.sum(0, keepdims=True), only_i.sum(0, keepdims=True)
    col_r, col_i = only_r.sum(1, keepdims=True), only_i.sum(1, keepdims=True)
    tr, ti = mr.T, mi.T
    g_r = 2.0 * w * ((mr * row_r + mi * row_i) - (tr * col_r + ti * col_i))
    g_i = 2.0 * w * ((mi * row_r - mr * row_i) + (ti * col_r - tr * col_i))
    square = jnp.where(eye, zero, mr * mr + mi * mi)
    omega = jnp.sum(jnp.sum(square, 0, keepdims=True), 1, keepdims=True)
    omega_ref[...] = jnp.broadcast_to(omega * (w / (64 * 256)), omega_ref.shape)
    for r in range(8):
        g_ref[r, 0] = g_r[32 * r : 32 * r + 32].astype(BF)
        g_ref[r, 1] = g_i[32 * r : 32 * r + 32].astype(BF)
    gt_r = -STEP_LENGTH * g_r - MIXING * h_r
    gt_i = STEP_LENGTH * g_i + MIXING * h_i
    gts = jnp.concatenate([gt_r, gt_i], 0).astype(BF)
    p = dot_nt(gts, u[:, :256])
    q = dot_nt(gts, u[:, 256:])
    zt_r = p[:256] - q[256:]
    zt_i = q[:256] + p[256:]
    p = dot(vts, a_r)
    q = dot(vts, a_i)
    zt_r = (zt_r + MIXING * (p[:256] - q[256:])).astype(BF)
    zt_i = (zt_i + MIXING * (q[:256] + p[256:])).astype(BF)
    z_r, z_i = zt_r.T, zt_i.T
    for h in range(2):
        for l in range(4):
            at = 64 * (4 * h + l)
            z_ref[l, h, :, :256] = z_r[at : at + 64]
            z_ref[l, h, :, 256:] = z_i[at : at + 64]


def main_products(w, mats, full, near):
    vmem = pl.BlockSpec(memory_space=pltpu.VMEM)
    return pl.pallas_call(
        main_kernel,
        out_shape=(
            jax.ShapeDtypeStruct((4, 2, 64, 512), BF),
            jax.ShapeDtypeStruct((8, 2, 32, 256), BF),
            jax.ShapeDtypeStruct((8, 128), F32),
        ),
        in_specs=[pl.BlockSpec(memory_space=pltpu.SMEM), vmem, vmem, vmem],
        out_specs=(vmem, vmem, vmem),
        compiler_params=pltpu.CompilerParams(vmem_limit_bytes=48 << 20),
        name="main_products",
    )(w.reshape(1), mats, full, near)


def cdot(ar, ai, br, bi):
    p = dot(
        jnp.concatenate([ar, ai], 0).astype(BF), jnp.concatenate([br, bi], 1).astype(BF)
    )
    rows, cols = ar.shape[0], br.shape[1]
    return p[:rows, :cols] - p[rows:, cols:], p[:rows, cols:] + p[rows:, :cols]


def orth_kernel(x_ref, own_ref, out_ref):
    x = x_ref[...].reshape(512, 512)
    p = dot(x.T, x)
    s_r = p[:256, :256] + p[256:, 256:]
    s_i = p[:256, 256:] - p[256:, :256]
    row = lax.broadcasted_iota(jnp.int32, (256, 256), 0)
    col = lax.broadcasted_iota(jnp.int32, (256, 256), 1)
    eye = (row == col).astype(F32)
    trace = jnp.sum(jnp.sum(s_r * eye, 0, keepdims=True), 1, keepdims=True)
    square = 256 / (2.0 * trace)
    scale = jnp.sqrt(square)
    d_r = 0.5 * (eye - square * s_r)
    d_i = -0.5 * (square * s_i)
    p_r, p_i = d_r, d_i
    for _ in range(2):
        q_r, q_i = cdot(d_r, d_i, d_r, d_i)
        c_r, c_i = cdot(q_r, q_i, d_r, d_i)
        d_r, d_i = 1.5 * q_r + c_r, 1.5 * q_i + c_i
        e_r, e_i = cdot(p_r, p_i, d_r, d_i)
        p_r, p_i = p_r + d_r + e_r, p_i + d_i + e_i
    own = own_ref[...]
    o_r, o_i = own[:, :256], own[:, 256:]
    e_r, e_i = cdot(o_r, o_i, p_r, p_i)
    out_ref[:, :256] = scale * (o_r + e_r)
    out_ref[:, 256:] = scale * (o_i + e_i)


def orthonormalized(full, own):
    vmem = pl.BlockSpec(memory_space=pltpu.VMEM)
    return pl.pallas_call(
        orth_kernel,
        out_shape=jax.ShapeDtypeStruct((64, 512), F32),
        in_specs=[vmem, vmem],
        out_specs=vmem,
        compiler_params=pltpu.CompilerParams(vmem_limit_bytes=48 << 20),
        name="orthonormalize",
    )(full, own)


def within_half(x):
    return lax.all_to_all(x, "col", 0, 0, tiled=True, axis_index_groups=HALVES)


def other_half(x):
    return lax.ppermute(x, "col", [(i, i ^ 4) for i in range(8)])


def fetch_permutation():
    pairs = []
    for k in range(64):
        for c, d in enumerate(SHELL_LIST):
            g = [(a + b) % 4 for a, b in zip((k // 16, k // 4 % 4, k % 4), d)]
            pairs.append(((g[0] * 16 + g[1] * 4 + g[2]) * 8 + c, k * 8 + c))
    return pairs


def per_device(correlations, gauge, neighbours, shifts):
    kpoint_index = lax.axis_index("ka")
    cindex = lax.axis_index("col")
    low = cindex < 4
    near, shift = neighbours[0], shifts[0]

    own = gauge[0].reshape(64, 512)
    mats = sorted_by_displacement(kpoint_index, near, shift, correlations[0])
    mats = lax.all_to_all(mats, "col", 0, 0, tiled=True)
    other = other_half(own)
    quarter = jnp.where(low, jnp.stack([own, other]), jnp.stack([other, own]))
    full = within_half(jnp.broadcast_to(quarter[None], (4, 2, 64, 512)))
    near_full = lax.ppermute(full, ("ka", "col"), fetch_permutation())

    moved = grid_positions(near) - grid_positions(kpoint_index)[None] + 4 * shift
    slots = slot_of(moved[:, 0], moved[:, 1], moved[:, 2])
    weights = shell_vector_weights(kpoint_index, near, shift)
    weight = jnp.sum(jnp.where(slots == cindex, weights, 0.0))

    z, g, omega = main_products(weight, mats, full, near_full)

    z = within_half(z).astype(F32).sum(0)
    spread = lax.all_to_all(jnp.broadcast_to(omega[:1, :1], (64, 1)), "ka", 0, 0, tiled=True)
    g = lax.all_to_all(g, "col", 0, 0, tiled=True)
    z = z + other_half(z.astype(BF)).astype(F32)
    x = quarter.astype(F32) + z
    full_x = within_half(jnp.broadcast_to(x.astype(BF)[None], (4, 2, 64, 512)))
    own_x = jnp.where(low, x[0], x[1])
    u_next = orthonormalized(full_x, own_x)

    spread = jnp.broadcast_to(spread.sum(0, keepdims=True), (8, 1))
    spread = lax.all_to_all(spread, "col", 0, 0, tiled=True).sum()
    gradient = g.astype(F32).sum(0)[None]
    return (u_next.reshape(1, 64, 2, 256), gradient, spread)


def solution(mesh):
    return jax.shard_map(
        per_device,
        mesh=mesh,
        in_specs=(
            P("ka", None, None, "col", None),
            P("ka", "col", None, None),
            P("ka", None),
            P("ka", None, None),
        ),
        out_specs=(P("ka", "col", None, None), P("ka", None, "col", None), P()),
        check_vma=False,
    )
```

time: 502 us -> 261 us (0.52)
  the two profiles are of different devices: /device:TPU:2 before, /device:TPU:1 now
where the time goes in v1:
time: 261 us; the launch traced here: 260 us
  blocking collectives  83.1 us (32%)
  waiting for transfers between devices  78.4 us (30%)
  starting transfers between devices  47.3 us (18%)
  Pallas kernels  40.5 us (16%)
  local copies, waits for them, and re-layouts  7.14 us (3%)
  other arithmetic  2.97 us (1%)
    all_to_all x1, blocking collectives, per_device(): lax.all_to_all(jnp.broadcast_to(omega[:1, :1], (64, 1)), 'ka', 0, 0, tile...  55.4 us
    all_to_all x1, waiting for transfers between devices, per_device(): mats = lax.all_to_all(mats, 'col', 0, 0, tiled=True)  34.4 us
    pallas_call x1, Pallas kernels, sorted_by_displacement(): pl.pallas_call(sort_kernel, out_shape=jax.ShapeDtypeStruct(mats.shape, ma...  33.7 us
    ppermute x2, waiting for transfers between devices, other_half(): return lax.ppermute(x, 'col', [(i, i ^ 4) for i in range(8)])  22.1 us
    ppermute x2, starting transfers between devices, other_half(): return lax.ppermute(x, 'col', [(i, i ^ 4) for i in range(8)])  16.8 us
    all_to_all x1, blocking collectives, within_half(): return lax.all_to_all(x, 'col', 0, 0, tiled=True, axis_index_groups=HALVES)  16 us
    all_to_all x2, waiting for transfers between devices, within_half(): return lax.all_to_all(x, 'col', 0, 0, tiled=True, axis_index_groups=HALVES)  12.7 us
    all_to_all x2, starting transfers between devices, within_half(): return lax.all_to_all(x, 'col', 0, 0, tiled=True, axis_index_groups=HALVES)  11.9 us
  transfers between devices with their start and end apart: 7, of which 5 were waited for; matrix products, arithmetic and copies ran while one was open for 1% of the time, Pallas kernels for 13%

profile of v1, /device:TPU:1, one launch (start us, length us, event | category | flops | bytes accessed | tf_op | source)
XLA Modules:
  0.0 260.2 jit_solution(8069516427435413109)
XLA Ops:
  0.6 0.9 copy.16
  1.6 9.6 %collective-permute-start = (bf16[64,512]{1,0:T(8,128)(2,1)S(1)}, bf16[64,512]{1,0:T(8,128)(2,1)S(1)}, u32[]{:S(2)}, u32[]{:S(2)}) collective-permute-start(bf16[64,512]{1,0:T(8,128)(2,1)S(1)} %bitcast.126), channel_id=1, source_target_pairs={{0,4},{1,5},{2,6},{3,7},{4,0},{5,1},{6,2},{7,3},{8,12},{9,13},{10,... | collective-permute-start | bytes 196616 | tf_op jit(solution)/shard_map/ppermute | solution.py:212
  11.3 1.6 collective-permute-done
  12.9 0.8 broadcast_in_dim.51
  13.7 8.5 %all-to-all-start.1 = ((bf16[4,2,64,512]{3,2,1,0:T(8,128)(2,1)}), bf16[4,2,64,512]{3,2,1,0:T(8,128)(2,1)S(1)}, u32[]{:S(2)}, u32[]{:S(2)}) async-start(bf16[4,2,64,512]{3,2,1,0:T(8,128)(2,1)} %broadcast_in_dim.51), calls=%async_computation.1 | async-start | bytes 1048576 | tf_op jit(solution)/shard_map/all_to_all | solution.py:208
  22.2 0.7 copy-done.1
  22.9 0.7 copy.10.shift_ref
  23.5 33.7 %sort_mats.1 = bf16[8,2,64,512]{3,2,1,0:T(8,128)(2,1)} custom-call(s32[1]{0:T(128)} %bitcast.12.k_ref, s32[8]{0:T(128)} %bitcast.128, s32[8,3]{1,0:T(8,128)} %copy.10.shift_ref, bf16[8,2,64,512]{3,2,1,0:T(8,128)(2,1)} %bitcast.121), custom_call_target="tpu_custom_call" | custom-call | tf_op jit(solution)/shard_map/sort_mats/pallas_call | solution.py:74
  57.2 10.5 %all-to-all-start = ((bf16[8,2,64,512]{3,2,1,0:T(8,128)(2,1)}), bf16[8,2,64,512]{3,2,1,0:T(8,128)(2,1)S(1)}, u32[]{:S(2)}, u32[]{:S(2)}) async-start(bf16[8,2,64,512]{3,2,1,0:T(8,128)(2,1)} %sort_mats.1), calls=%async_computation | async-start | bytes 2097152 | tf_op jit(solution)/shard_map/all_to_all | solution.py:232
  68.4 4.6 %collective-permute-start.1 = (bf16[4,2,64,512]{3,2,1,0:T(8,128)(2,1)S(1)}, bf16[4,2,64,512]{3,2,1,0:T(8,128)(2,1)S(1)}, u32[]{:S(2)}, u32[]{:S(2)}) collective-permute-start(bf16[4,2,64,512]{3,2,1,0:T(8,128)(2,1)S(1)} %all-to-all-done.1.u_ref), channel_id=1, source_target_pairs={{128,0},{385,1},{34,2},{99,3},{12,4},{29,5},{174,6},{511,7},{136,8... | collective-permute-start | bytes 1572872 | tf_op jit(solution)/shard_map/ppermute | solution.py:236
  73.8 9.2 %collective-permute-done.1.n_ref = bf16[4,2,64,512]{3,2,1,0:T(8,128)(2,1)S(1)} collective-permute-done((bf16[4,2,64,512]{3,2,1,0:T(8,128)(2,1)S(1)}, bf16[4,2,64,512]{3,2,1,0:T(8,128)(2,1)S(1)}, u32[]{:S(2)}, u32[]{:S(2)}) %collective-permute-start.1) | collective-permute-done | bytes 524320 | tf_op jit(solution)/shard_map/ppermute | solution.py:236
  83.0 34.4 %all-to-all-done.m_ref = bf16[8,2,64,512]{3,2,1,0:T(8,128)(2,1)S(1)} async-done(((bf16[8,2,64,512]{3,2,1,0:T(8,128)(2,1)}), bf16[8,2,64,512]{3,2,1,0:T(8,128)(2,1)S(1)}, u32[]{:S(2)}, u32[]{:S(2)}) %all-to-all-start) | async-done | bytes 1048608 | tf_op jit(solution)/shard_map/all_to_all | solution.py:232
  117.4 4.0 %main_products.1 = (bf16[4,2,64,512]{3,2,1,0:T(8,128)(2,1)S(1)}, bf16[8,2,32,256]{3,2,1,0:T(8,128)(2,1)}, f32[8,128]{1,0:T(8,128)S(1)}) custom-call(f32[1]{0:T(128)} %bitcast.11.w_ref, bf16[8,2,64,512]{3,2,1,0:T(8,128)(2,1)S(1)} %all-to-all-done.m_ref, bf16[4,2,64,512]{3,2,1,0:T(8,128)(2,1)S(1)} %all-to-all-done.1.u_ref, ...), custom_call_target="tpu_custom_call" | custom-call | tf_op jit(solution)/shard_map/main_products/pallas_call | solution.py:146
  122.6 55.4 %all_to_all.37 = f32[64,1,1]{2,1,0:T(1,128)S(1)} all-to-all(f32[64,1,1]{2,1,0:T(1,128)S(1)} %broadcast_in_dim.55), channel_id=1, replica_groups=mesh['ka'=64,'col'=8] {'ka'}, dimensions={0} | all-to-all | bytes 512 | tf_op jit(solution)/shard_map/all_to_all | solution.py:246
  179.3 11.6 %all_to_all.38 = f32[8,1,1]{2,1,0:T(1,128)S(1)} all-to-all(f32[8,1,1]{2,1,0:T(1,128)S(1)} %broadcast_in_dim.56), channel_id=1, replica_groups=mesh['ka'=64,'col'=8] {'col'}, dimensions={0} | all-to-all | bytes 64 | tf_op jit(solution)/shard_map/all_to_all | solution.py:255
  191.0 16.0 %all_to_all.39 = bf16[4,2,64,512]{3,2,1,0:T(8,128)(2,1)S(1)} all-to-all(bf16[4,2,64,512]{3,2,1,0:T(8,128)(2,1)S(1)} %get-tuple-element.6), channel_id=1, replica_groups={{0,1,2,3},{4,5,6,7},{8,9,10,11},{12,13,14,15},{16,17,18,19},{20,21,22,2..., dimensions={0} | all-to-all | bytes 1048576 | tf_op jit(solution)/shard_map/all_to_all | solution.py:208
  207.0 3.4 %all-to-all-start.4 = ((bf16[8,2,32,256]{3,2,1,0:T(8,128)(2,1)}), bf16[8,2,32,256]{3,2,1,0:T(8,128)(2,1)S(1)}, u32[]{:S(2)}, u32[]{:S(2)}) async-start(bf16[8,2,32,256]{3,2,1,0:T(8,128)(2,1)} %get-tuple-element.7), calls=%async_computation.4 | async-start | bytes 524288 | tf_op jit(solution)/shard_map/all_to_all | solution.py:247
  210.5 7.2 %collective-permute-start.2 = (bf16[2,64,512]{2,1,0:T(8,128)(2,1)S(1)}, bf16[2,64,512]{2,1,0:T(8,128)(2,1)S(1)}, u32[]{:S(2)}, u32[]{:S(2)}) collective-permute-start(bf16[2,64,512]{2,1,0:T(8,128)(2,1)S(1)} %convert_element_type.28), channel_id=1, source_target_pairs={{0,4},{1,5},{2,6},{3,7},{4,0},{5,1},{6,2},{7,3},{8,12},{9,13},{10,... | collective-permute-start | bytes 393224 | tf_op jit(solution)/shard_map/ppermute | solution.py:212
  217.7 20.5 %collective-permute-done.2 = bf16[2,64,512]{2,1,0:T(8,128)(2,1)S(1)} collective-permute-done((bf16[2,64,512]{2,1,0:T(8,128)(2,1)S(1)}, bf16[2,64,512]{2,1,0:T(8,128)(2,1)S(1)}, u32[]{:S(2)}, u32[]{:S(2)}) %collective-permute-start.2) | collective-permute-done | bytes 131104 | tf_op jit(solution)/shard_map/ppermute | solution.py:212
  238.3 0.8 broadcast_in_dim.52
  239.2 3.5 %all-to-all-start.3 = ((bf16[4,2,64,512]{3,2,1,0:T(8,128)(2,1)}), bf16[4,2,64,512]{3,2,1,0:T(8,128)(2,1)S(1)}, u32[]{:S(2)}, u32[]{:S(2)}) async-start(bf16[4,2,64,512]{3,2,1,0:T(8,128)(2,1)} %broadcast_in_dim.52), calls=%async_computation.3 | async-start | bytes 1048576 | tf_op jit(solution)/shard_map/all_to_all | solution.py:208
  243.9 12.7 %all-to-all-done.3.x_ref = bf16[4,2,64,512]{3,2,1,0:T(8,128)(2,1)S(1)} async-done(((bf16[4,2,64,512]{3,2,1,0:T(8,128)(2,1)}), bf16[4,2,64,512]{3,2,1,0:T(8,128)(2,1)S(1)}, u32[]{:S(2)}, u32[]{:S(2)}) %all-to-all-start.3) | async-done | bytes 524320 | tf_op jit(solution)/shard_map/all_to_all | solution.py:208
  256.6 2.8 %orthonormalize.1 = f32[64,512]{1,0:T(8,128)S(1)} custom-call(bf16[4,2,64,512]{3,2,1,0:T(8,128)(2,1)S(1)} %all-to-all-done.3.x_ref, f32[64,512]{1,0:T(8,128)S(1)} %fusion.own_ref), custom_call_target="tpu_custom_call" | custom-call | tf_op jit(solution)/shard_map/orthonormalize/pallas_call | solution.py:197
  259.5 0.7 reshape.256
  (25 shorter events, 5.4 us)
Async XLA Ops:
  0.6 10.6 %copy-start = (bf16[1,64,2,256]{3,2,1,0:T(2,128)(2,1)S(1)}, bf16[1,64,2,256]{3,2,1,0:T(2,128)(2,1)}, u32[]{:S(2)}) copy-start(bf16[1,64,2,256]{3,2,1,0:T(2,128)(2,1)} %param.6) | copy-start | bytes 196612
  1.6 11.3 %collective-permute-start = (bf16[64,512]{1,0:T(8,128)(2,1)S(1)}, bf16[64,512]{1,0:T(8,128)(2,1)S(1)}, u32[]{:S(2)}, u32[]{:S(2)}) collective-permute-start(bf16[64,512]{1,0:T(8,128)(2,1)S(1)} %bitcast.126), channel_id=1, source_target_pairs={{0,4},{1,5},{2,6},{3,7},{4,0},{5,1},{6,2},{7,3},{8,12},{9,13},{10,... | collective-permute-start | bytes 196616 | tf_op jit(solution)/shard_map/ppermute | solution.py:212
  13.7 43.5 %all-to-all-start.1 = ((bf16[4,2,64,512]{3,2,1,0:T(8,128)(2,1)}), bf16[4,2,64,512]{3,2,1,0:T(8,128)(2,1)S(1)}, u32[]{:S(2)}, u32[]{:S(2)}) async-start(bf16[4,2,64,512]{3,2,1,0:T(8,128)(2,1)} %broadcast_in_dim.51), calls=%async_computation.1 | async-start | bytes 1048576 | tf_op jit(solution)/shard_map/all_to_all | solution.py:208
  22.2 0.7 copy-start.1
  57.2 60.2 %all-to-all-start = ((bf16[8,2,64,512]{3,2,1,0:T(8,128)(2,1)}), bf16[8,2,64,512]{3,2,1,0:T(8,128)(2,1)S(1)}, u32[]{:S(2)}, u32[]{:S(2)}) async-start(bf16[8,2,64,512]{3,2,1,0:T(8,128)(2,1)} %sort_mats.1), calls=%async_computation | async-start | bytes 2097152 | tf_op jit(solution)/shard_map/all_to_all | solution.py:232
  67.8 0.7 copy-start.2
  68.4 14.6 %collective-permute-start.1 = (bf16[4,2,64,512]{3,2,1,0:T(8,128)(2,1)S(1)}, bf16[4,2,64,512]{3,2,1,0:T(8,128)(2,1)S(1)}, u32[]{:S(2)}, u32[]{:S(2)}) collective-permute-start(bf16[4,2,64,512]{3,2,1,0:T(8,128)(2,1)S(1)} %all-to-all-done.1.u_ref), channel_id=1, source_target_pairs={{128,0},{385,1},{34,2},{99,3},{12,4},{29,5},{174,6},{511,7},{136,8... | collective-permute-start | bytes 1572872 | tf_op jit(solution)/shard_map/ppermute | solution.py:236
  207.0 31.3 %all-to-all-start.4 = ((bf16[8,2,32,256]{3,2,1,0:T(8,128)(2,1)}), bf16[8,2,32,256]{3,2,1,0:T(8,128)(2,1)S(1)}, u32[]{:S(2)}, u32[]{:S(2)}) async-start(bf16[8,2,32,256]{3,2,1,0:T(8,128)(2,1)} %get-tuple-element.7), calls=%async_computation.4 | async-start | bytes 524288 | tf_op jit(solution)/shard_map/all_to_all | solution.py:247
  210.5 27.7 %collective-permute-start.2 = (bf16[2,64,512]{2,1,0:T(8,128)(2,1)S(1)}, bf16[2,64,512]{2,1,0:T(8,128)(2,1)S(1)}, u32[]{:S(2)}, u32[]{:S(2)}) collective-permute-start(bf16[2,64,512]{2,1,0:T(8,128)(2,1)S(1)} %convert_element_type.28), channel_id=1, source_target_pairs={{0,4},{1,5},{2,6},{3,7},{4,0},{5,1},{6,2},{7,3},{8,12},{9,13},{10,... | collective-permute-start | bytes 393224 | tf_op jit(solution)/shard_map/ppermute | solution.py:212
  239.2 17.5 %all-to-all-start.3 = ((bf16[4,2,64,512]{3,2,1,0:T(8,128)(2,1)}), bf16[4,2,64,512]{3,2,1,0:T(8,128)(2,1)S(1)}, u32[]{:S(2)}, u32[]{:S(2)}) async-start(bf16[4,2,64,512]{3,2,1,0:T(8,128)(2,1)} %broadcast_in_dim.52), calls=%async_computation.3 | async-start | bytes 1048576 | tf_op jit(solution)/shard_map/all_to_all | solution.py:208

commit v2 on v1

--- a/solution.py
+++ b/solution.py
@@ -4,6 +4,7 @@
 from jax.experimental import pallas as pl
 from jax.experimental.pallas import tpu as pltpu
 from jax.sharding import PartitionSpec as P
+
 
 MIXING = 0.02
 STEP_LENGTH = 0.2
@@ -46,21 +47,53 @@
     return 3.0 / (len(SHELL_LIST) * (cx * cx + cy * cy + cz * cz))
 
 
-def slot_of(dx, dy, dz):
+def owner_of(k, dx, dy, dz):
     diagonal = jnp.logical_and(dx != 0, dy != 0)
-    pair = jnp.where(diagonal, 3, jnp.where(dx != 0, 0, jnp.where(dy != 0, 1, 2)))
-    return 2 * pair + jnp.where(dx + dy + dz < 0, 1, 0)
-
-
-def sort_kernel(k_ref, near_ref, shift_ref, m_ref, out_ref, sems):
+    plus = dx + dy + dz == jnp.where(diagonal, 3, 1)
+    crosses = plus == ((k // 4) % 2 == 1)
+    minus = jnp.where(plus, 0, 1)
+    return jnp.where(
+        diagonal,
+        jnp.where(crosses, 7, 6),
+        jnp.where(
+            dy != 0,
+            jnp.where(crosses, 0, 1),
+            jnp.where(dx != 0, 2 + minus, 4 + minus),
+        ),
+    )
+
+
+def difference(near, k):
+    return (
+        (near // 16 - k // 16 + 4) % 4,
+        (near // 4 % 4 - k // 4 % 4 + 4) % 4,
+        (near % 4 - k % 4 + 4) % 4,
+    )
+
+
+def fetch_permutation():
+    pairs = []
+    for k in range(64):
+        for d in SHELL_LIST:
+            g = [(a + b) % 4 for a, b in zip((k // 16, k // 4 % 4, k % 4), d)]
+            plus = sum(d) > 0
+            crosses = d[1] != 0 and plus == (k // 4 % 2 == 1)
+            if d[0] and d[1]:
+                c = 7 if crosses else 6
+            elif d[1]:
+                c = 0 if crosses else 1
+            else:
+                c = (2 if d[0] else 4) + (0 if plus else 1)
+            source = 7 - c if crosses else c
+            pairs.append(((g[0] * 16 + g[1] * 4 + g[2]) * 8 + source, k * 8 + c))
+    return pairs
+
+
+def sort_kernel(k_ref, near_ref, m_ref, out_ref, sems):
     k = k_ref[0]
     copies = []
     for b in range(8):
-        q = near_ref[b]
-        dx = q // 16 - k // 16 + 4 * shift_ref[b, 0]
-        dy = q // 4 % 4 - k // 4 % 4 + 4 * shift_ref[b, 1]
-        dz = q % 4 - k % 4 + 4 * shift_ref[b, 2]
-        slot = slot_of(dx, dy, dz)
+        slot = owner_of(k, *difference(near_ref[b], k))
         copy = pltpu.make_async_copy(m_ref.at[b], out_ref.at[slot], sems.at[b])
         copy.start()
         copies.append(copy)
@@ -68,29 +101,34 @@
         copy.wait()
 
 
-def sorted_by_displacement(kpoint_index, near, shifts, mats):
+def sorted_by_owner(kpoint_index, near, mats):
     smem = pl.BlockSpec(memory_space=pltpu.SMEM)
-    hbm = pl.BlockSpec(memory_space=pl.ANY)
     return pl.pallas_call(
         sort_kernel,
         out_shape=jax.ShapeDtypeStruct(mats.shape, mats.dtype),
-        in_specs=[smem, smem, smem, hbm],
-        out_specs=hbm,
+        in_specs=[smem, smem, pl.BlockSpec(memory_space=pl.ANY)],
+        out_specs=pl.BlockSpec(memory_space=pltpu.VMEM),
         scratch_shapes=[pltpu.SemaphoreType.DMA((8,))],
         name="sort_mats",
-    )(kpoint_index.reshape(1), near, shifts, mats)
-
-
-def rows_in_order(ref):
-    return jnp.concatenate([ref[l, h] for h in range(2) for l in range(4)], 0)
-
-
-def main_kernel(w_ref, m_ref, u_ref, n_ref, z_ref, g_ref, omega_ref):
+    )(kpoint_index.reshape(1), near, mats)
+
+
+def rows_in_order(ref, holder):
+    blocks = []
+    for r in range(8):
+        d = jnp.bitwise_xor(holder, r)
+        at = 4 * jnp.bitwise_and(d, 1) + jnp.bitwise_and(d, 2) + jnp.right_shift(d, 2)
+        blocks.append(ref[at])
+    return jnp.concatenate(blocks, 0)
+
+
+def main_kernel(w_ref, holder_ref, m_ref, u_ref, n_ref, z_ref, omega_ref):
     w = w_ref[0]
     a_r = m_ref[:, 0].reshape(512, 512)
     a_i = m_ref[:, 1].reshape(512, 512)
-    u = rows_in_order(u_ref)
-    n = rows_in_order(n_ref)
+    u = rows_in_order(u_ref, holder_ref[0])
+    n = rows_in_order(n_ref, holder_ref[1])
+    half = jnp.right_shift(holder_ref[0], 2)
     ut = u.T
     p = dot_nt(ut, a_r)
     q = dot_nt(ut, a_i)
@@ -119,9 +157,7 @@
     square = jnp.where(eye, zero, mr * mr + mi * mi)
     omega = jnp.sum(jnp.sum(square, 0, keepdims=True), 1, keepdims=True)
     omega_ref[...] = jnp.broadcast_to(omega * (w / (64 * 256)), omega_ref.shape)
-    for r in range(8):
-        g_ref[r, 0] = g_r[32 * r : 32 * r + 32].astype(BF)
-        g_ref[r, 1] = g_i[32 * r : 32 * r + 32].astype(BF)
+    b_r, b_i = g_r.astype(BF), g_i.astype(BF)
     gt_r = -STEP_LENGTH * g_r - MIXING * h_r
     gt_i = STEP_LENGTH * g_i + MIXING * h_i
     gts = jnp.concatenate([gt_r, gt_i], 0).astype(BF)
@@ -136,25 +172,29 @@
     z_r, z_i = zt_r.T, zt_i.T
     for h in range(2):
         for l in range(4):
+            to = jnp.bitwise_xor(half, h)
             at = 64 * (4 * h + l)
-            z_ref[l, h, :, :256] = z_r[at : at + 64]
-            z_ref[l, h, :, 256:] = z_i[at : at + 64]
-
-
-def main_products(w, mats, full, near):
+            z_ref[l, to, :64, :256] = z_r[at : at + 64]
+            z_ref[l, to, :64, 256:] = z_i[at : at + 64]
+            at = 32 * (4 * h + l)
+            z_ref[l, to, 64:, :256] = b_r[at : at + 32]
+            z_ref[l, to, 64:, 256:] = b_i[at : at + 32]
+
+
+def main_products(w, holders, mats, full, near):
     vmem = pl.BlockSpec(memory_space=pltpu.VMEM)
+    smem = pl.BlockSpec(memory_space=pltpu.SMEM)
     return pl.pallas_call(
         main_kernel,
         out_shape=(
-            jax.ShapeDtypeStruct((4, 2, 64, 512), BF),
-            jax.ShapeDtypeStruct((8, 2, 32, 256), BF),
+            jax.ShapeDtypeStruct((4, 2, 96, 512), BF),
             jax.ShapeDtypeStruct((8, 128), F32),
         ),
-        in_specs=[pl.BlockSpec(memory_space=pltpu.SMEM), vmem, vmem, vmem],
-        out_specs=(vmem, vmem, vmem),
+        in_specs=[smem, smem, vmem, vmem, vmem],
+        out_specs=(vmem, vmem),
         compiler_params=pltpu.CompilerParams(vmem_limit_bytes=48 << 20),
         name="main_products",
-    )(w.reshape(1), mats, full, near)
+    )(w.reshape(1), holders, mats, full, near)
 
 
 def cdot(ar, ai, br, bi):
@@ -166,7 +206,7 @@
 
 
 def orth_kernel(x_ref, own_ref, out_ref):
-    x = x_ref[...].reshape(512, 512)
+    x = x_ref[...]
     p = dot(x.T, x)
     s_r = p[:256, :256] + p[256:, 256:]
     s_i = p[:256, 256:] - p[256:, :256]
@@ -208,53 +248,61 @@
     return lax.all_to_all(x, "col", 0, 0, tiled=True, axis_index_groups=HALVES)
 
 
-def other_half(x):
-    return lax.ppermute(x, "col", [(i, i ^ 4) for i in range(8)])
-
-
-def fetch_permutation():
-    pairs = []
-    for k in range(64):
-        for c, d in enumerate(SHELL_LIST):
-            g = [(a + b) % 4 for a, b in zip((k // 16, k // 4 % 4, k % 4), d)]
-            pairs.append(((g[0] * 16 + g[1] * 4 + g[2]) * 8 + c, k * 8 + c))
-    return pairs
+def partner(x, axis, bit):
+    length = lax.axis_size(axis)
+    return lax.ppermute(x, axis, [(i, i ^ bit) for i in range(length)])
 
 
 def per_device(correlations, gauge, neighbours, shifts):
     kpoint_index = lax.axis_index("ka")
     cindex = lax.axis_index("col")
-    low = cindex < 4
     near, shift = neighbours[0], shifts[0]
 
     own = gauge[0].reshape(64, 512)
-    mats = sorted_by_displacement(kpoint_index, near, shift, correlations[0])
+    mats = sorted_by_owner(kpoint_index, near, correlations[0])
     mats = lax.all_to_all(mats, "col", 0, 0, tiled=True)
-    other = other_half(own)
-    quarter = jnp.where(low, jnp.stack([own, other]), jnp.stack([other, own]))
-    full = within_half(jnp.broadcast_to(quarter[None], (4, 2, 64, 512)))
+    pair = jnp.stack([own, partner(own, "col", 4)])
+    full = jnp.stack([pair, partner(pair, "col", 2)])
+    full = jnp.stack([full, partner(full, "col", 1)]).reshape(8, 64, 512)
     near_full = lax.ppermute(full, ("ka", "col"), fetch_permutation())
-
-    moved = grid_positions(near) - grid_positions(kpoint_index)[None] + 4 * shift
-    slots = slot_of(moved[:, 0], moved[:, 1], moved[:, 2])
+    outer = jnp.logical_or(cindex == 0, cindex == 7)
+    holders = jnp.stack([cindex, jnp.where(outer, 7 - cindex, cindex)])
+
+    owners = owner_of(kpoint_index, *difference(near, kpoint_index))
     weights = shell_vector_weights(kpoint_index, near, shift)
-    weight = jnp.sum(jnp.where(slots == cindex, weights, 0.0))
-
-    z, g, omega = main_products(weight, mats, full, near_full)
-
-    z = within_half(z).astype(F32).sum(0)
-    spread = lax.all_to_all(jnp.broadcast_to(omega[:1, :1], (64, 1)), "ka", 0, 0, tiled=True)
-    g = lax.all_to_all(g, "col", 0, 0, tiled=True)
-    z = z + other_half(z.astype(BF)).astype(F32)
-    x = quarter.astype(F32) + z
-    full_x = within_half(jnp.broadcast_to(x.astype(BF)[None], (4, 2, 64, 512)))
-    own_x = jnp.where(low, x[0], x[1])
+    weight = jnp.sum(jnp.where(owners == cindex, weights, 0.0))
+
+    z, spread = main_products(weight, holders, mats, full, near_full)
+
+    z = within_half(z)
+    for bit in (1, 2, 4, 16):
+        spread = spread + partner(spread, "ka", bit)
+    z = z.astype(F32).sum(0)
+    arrived = jnp.concatenate([z[0, :64], z[1]], 0).astype(BF)
+    arrived = partner(arrived, "col", 4).astype(F32)
+    spread = spread + partner(spread, "ka", 32)
+    groups = [
+        [8 * (16 * y + 8 * h + x) + c for h in range(2) for c in range(8)]
+        for y in range(4)
+        for x in range(8)
+    ]
+    spread = lax.all_to_all(
+        jnp.concatenate([spread, spread], 0),
+        ("ka", "col"),
+        0,
+        0,
+        tiled=True,
+        axis_index_groups=groups,
+    ).sum(0)
+    x = pair.astype(F32) + jnp.stack([z[0, :64] + arrived[64:128], z[1, :64] + arrived[:64]])
+    g = z[0, 64:] + arrived[128:]
+    full_x = x.astype(BF).reshape(128, 512)
+    for bit in (2, 1):
+        full_x = jnp.concatenate([full_x, partner(full_x, "col", bit)], 0)
+    own_x = x[0]
     u_next = orthonormalized(full_x, own_x)
-
-    spread = jnp.broadcast_to(spread.sum(0, keepdims=True), (8, 1))
-    spread = lax.all_to_all(spread, "col", 0, 0, tiled=True).sum()
-    gradient = g.astype(F32).sum(0)[None]
-    return (u_next.reshape(1, 64, 2, 256), gradient, spread)
+    gradient = jnp.stack([g[:, :256], g[:, 256:]])[None]
+    return (u_next.reshape(1, 64, 2, 256), gradient, spread[0])
 
 
 def solution(mesh):

time: 261 us -> 211 us (0.81)
  the two profiles are of different devices: /device:TPU:1 before, /device:TPU:2 now
where the time goes in v2:
time: 211 us; the launch traced here: 210 us
  waiting for transfers between devices  114 us (54%)
  starting transfers between devices  61.4 us (29%)
  blocking collectives  19.5 us (9%)
  Pallas kernels  11.2 us (5%)
  other arithmetic  2.49 us (1%)
    ppermute x11, waiting for transfers between devices, partner(): return lax.ppermute(x, axis, [(i, i ^ bit) for i in range(length)])  87 us
    ppermute x11, starting transfers between devices, partner(): return lax.ppermute(x, axis, [(i, i ^ bit) for i in range(length)])  39.3 us
    all_to_all x1, blocking collectives, per_device(): lax.all_to_all(jnp.concatenate([spread, spread], 0), ('ka', 'col'), 0, 0,...  19.5 us
    all_to_all x1, waiting for transfers between devices, within_half(): return lax.all_to_all(x, 'col', 0, 0, tiled=True, axis_index_groups=HALVES)  17 us
    all_to_all x1, starting transfers between devices, per_device(): mats = lax.all_to_all(mats, 'col', 0, 0, tiled=True)  12.7 us
    ppermute x1, waiting for transfers between devices, per_device(): near_full = lax.ppermute(full, ('ka', 'col'), fetch_permutation())  9.9 us
    ppermute x1, starting transfers between devices, per_device(): near_full = lax.ppermute(full, ('ka', 'col'), fetch_permutation())  5.91 us
    pallas_call x1, Pallas kernels, main_products(): pl.pallas_call(main_kernel, out_shape=(jax.ShapeDtypeStruct((4, 2, 96, 51...  5.32 us
  transfers between devices with their start and end apart: 14, of which 11 were waited for; matrix products, arithmetic and copies ran while one was open for 1% of the time, Pallas kernels for 0%

profile of v2, /device:TPU:2, one launch (start us, length us, event | category | flops | bytes accessed | tf_op | source)
XLA Modules:
  0.0 210.4 jit_solution(7180417147942164588)
XLA Ops:
  0.6 3.1 %sort_mats.1 = bf16[8,2,64,512]{3,2,1,0:T(8,128)(2,1)} custom-call(s32[1]{0:T(128)} %bitcast.12.k_ref, s32[8]{0:T(128)} %bitcast.141, bf16[8,2,64,512]{3,2,1,0:T(8,128)(2,1)} %bitcast.133), custom_call_target="tpu_custom_call" | custom-call | tf_op jit(solution)/shard_map/sort_mats/pallas_call | solution.py:106
  3.7 12.7 %all-to-all-start = ((bf16[8,2,64,512]{3,2,1,0:T(8,128)(2,1)}), bf16[8,2,64,512]{3,2,1,0:T(8,128)(2,1)S(1)}, u32[]{:S(2)}, u32[]{:S(2)}) async-start(bf16[8,2,64,512]{3,2,1,0:T(8,128)(2,1)} %sort_mats.1), calls=%async_computation | async-start | bytes 2097152 | tf_op jit(solution)/shard_map/all_to_all | solution.py:263
  16.4 7.8 %collective-permute-start = (bf16[64,512]{1,0:T(8,128)(2,1)S(1)}, bf16[64,512]{1,0:T(8,128)(2,1)S(1)}, u32[]{:S(2)}, u32[]{:S(2)}) collective-permute-start(bf16[64,512]{1,0:T(8,128)(2,1)S(1)} %bitcast.139), channel_id=1, source_target_pairs={{0,4},{1,5},{2,6},{3,7},{4,0},{5,1},{6,2},{7,3},{8,12},{9,13},{10,... | collective-permute-start | bytes 196616 | tf_op jit(solution)/shard_map/ppermute | solution.py:253
  24.3 48.9 %collective-permute-done = bf16[64,512]{1,0:T(8,128)(2,1)S(1)} collective-permute-done((bf16[64,512]{1,0:T(8,128)(2,1)S(1)}, bf16[64,512]{1,0:T(8,128)(2,1)S(1)}, u32[]{:S(2)}, u32[]{:S(2)}) %collective-permute-start) | collective-permute-done | bytes 65568 | tf_op jit(solution)/shard_map/ppermute | solution.py:253
  75.2 5.8 %collective-permute-done.1 = bf16[2,64,512]{2,1,0:T(8,128)(2,1)S(1)} collective-permute-done((bf16[2,64,512]{2,1,0:T(8,128)(2,1)S(1)}, bf16[2,64,512]{2,1,0:T(8,128)(2,1)S(1)}, u32[]{:S(2)}, u32[]{:S(2)}) %collective-permute-start.1) | collective-permute-done | bytes 131104 | tf_op jit(solution)/shard_map/ppermute | solution.py:253
  83.3 6.1 %collective-permute-done.2 = bf16[2,2,64,512]{3,2,1,0:T(8,128)(2,1)S(1)} collective-permute-done((bf16[2,2,64,512]{3,2,1,0:T(8,128)(2,1)S(1)}, bf16[2,2,64,512]{3,2,1,0:T(8,128)(2,1)S(1)}, u32[]{:S(2)}, u32[]{:S(2)}) %collective-permute-start.2) | collective-permute-done | bytes 262176 | tf_op jit(solution)/shard_map/ppermute | solution.py:253
  89.4 5.9 %collective-permute-start.3 = (bf16[8,64,512]{2,1,0:T(8,128)(2,1)S(1)}, bf16[8,64,512]{2,1,0:T(8,128)(2,1)S(1)}, u32[]{:S(2)}, u32[]{:S(2)}) collective-permute-start(bf16[8,64,512]{2,1,0:T(8,128)(2,1)S(1)} %bitcast.128), channel_id=1, source_target_pairs={{130,2},{387,3},{33,1},{103,0},{12,4},{29,5},{174,6},{504,7},{138,... | collective-permute-start | bytes 1572872 | tf_op jit(solution)/shard_map/ppermute | solution.py:267
  96.1 9.9 %collective-permute-done.3.n_ref = bf16[8,64,512]{2,1,0:T(8,128)(2,1)S(1)} collective-permute-done((bf16[8,64,512]{2,1,0:T(8,128)(2,1)S(1)}, bf16[8,64,512]{2,1,0:T(8,128)(2,1)S(1)}, u32[]{:S(2)}, u32[]{:S(2)}) %collective-permute-start.3) | collective-permute-done | bytes 524320 | tf_op jit(solution)/shard_map/ppermute | solution.py:267
  106.0 5.3 %main_products.1 = (bf16[4,2,96,512]{3,2,1,0:T(8,128)(2,1)}, f32[8,128]{1,0:T(8,128)S(1)}) custom-call(f32[1]{0:T(128)} %bitcast.9.w_ref, s32[2]{0:T(128)S(1)} %pad_add_fusion.1.holder_ref, bf16[8,2,64,512]{3,2,1,0:T(8,128)(2,1)S(1)} %all-to-all-done.m_ref, bf16[8,64,512]{2,1,0:T(8,128)(2,1)S(1)} %bitcast.129, ...), custom_call_target="tpu_custom_call" | custom-call | tf_op jit(solution)/shard_map/main_products/pallas_call | solution.py:187
  111.3 3.5 %all-to-all-start.1 = ((bf16[4,2,96,512]{3,2,1,0:T(8,128)(2,1)}), bf16[4,2,96,512]{3,2,1,0:T(8,128)(2,1)S(1)}, u32[]{:S(2)}, u32[]{:S(2)}) async-start(bf16[4,2,96,512]{3,2,1,0:T(8,128)(2,1)} %get-tuple-element.5), calls=%async_computation.1 | async-start | bytes 1572864 | tf_op jit(solution)/shard_map/all_to_all | solution.py:248
  114.8 3.7 %collective-permute-start.7 = (f32[8,128]{1,0:T(8,128)S(1)}, f32[8,128]{1,0:T(8,128)S(1)}, u32[]{:S(2)}, u32[]{:S(2)}) collective-permute-start(f32[8,128]{1,0:T(8,128)S(1)} %get-tuple-element.6), channel_id=1, source_target_pairs={{0,8},{8,0},{16,24},{24,16},{32,40},{40,32},{48,56},{56,48},{64,72... | collective-permute-start | bytes 12296 | tf_op jit(solution)/shard_map/ppermute | solution.py:253
  118.5 17.0 %all-to-all-done.1 = bf16[4,2,96,512]{3,2,1,0:T(8,128)(2,1)S(1)} async-done(((bf16[4,2,96,512]{3,2,1,0:T(8,128)(2,1)}), bf16[4,2,96,512]{3,2,1,0:T(8,128)(2,1)S(1)}, u32[]{:S(2)}, u32[]{:S(2)}) %all-to-all-start.1) | async-done | bytes 786464 | tf_op jit(solution)/shard_map/all_to_all | solution.py:248
  135.7 8.5 %collective-permute-start.4 = (bf16[160,512]{1,0:T(8,128)(2,1)S(1)}, bf16[160,512]{1,0:T(8,128)(2,1)S(1)}, u32[]{:S(2)}, u32[]{:S(2)}) collective-permute-start(bf16[160,512]{1,0:T(8,128)(2,1)S(1)} %pad_maximum_fusion.4), channel_id=1, source_target_pairs={{0,4},{1,5},{2,6},{3,7},{4,0},{5,1},{6,2},{7,3},{8,12},{9,13},{10,... | collective-permute-start | bytes 491528 | tf_op jit(solution)/shard_map/ppermute | solution.py:253
  144.1 3.4 %collective-permute-start.8 = (f32[8,128]{1,0:T(8,128)S(1)}, f32[8,128]{1,0:T(8,128)S(1)}, u32[]{:S(2)}, u32[]{:S(2)}) collective-permute-start(f32[8,128]{1,0:T(8,128)S(1)} %add.173), channel_id=1, source_target_pairs={{0,16},{8,24},{16,0},{24,8},{32,48},{40,56},{48,32},{56,40},{64,80... | collective-permute-start | bytes 12296 | tf_op jit(solution)/shard_map/ppermute | solution.py:253
  151.6 5.1 %collective-permute-done.9 = f32[8,128]{1,0:T(8,128)S(1)} collective-permute-done((f32[8,128]{1,0:T(8,128)S(1)}, f32[8,128]{1,0:T(8,128)S(1)}, u32[]{:S(2)}, u32[]{:S(2)}) %collective-permute-start.9) | collective-permute-done | bytes 4128 | tf_op jit(solution)/shard_map/ppermute | solution.py:253
  158.6 3.6 %collective-permute-done.10 = f32[8,128]{1,0:T(8,128)S(1)} collective-permute-done((f32[8,128]{1,0:T(8,128)S(1)}, f32[8,128]{1,0:T(8,128)S(1)}, u32[]{:S(2)}, u32[]{:S(2)}) %collective-permute-start.10) | collective-permute-done | bytes 4128 | tf_op jit(solution)/shard_map/ppermute | solution.py:253
  162.1 3.3 %collective-permute-start.11 = (f32[8,128]{1,0:T(8,128)S(1)}, f32[8,128]{1,0:T(8,128)S(1)}, u32[]{:S(2)}, u32[]{:S(2)}) collective-permute-start(f32[8,128]{1,0:T(8,128)S(1)} %add.176), channel_id=1, source_target_pairs={{0,256},{8,264},{16,272},{24,280},{32,288},{40,296},{48,304},{56,3... | collective-permute-start | bytes 12296 | tf_op jit(solution)/shard_map/ppermute | solution.py:253
  165.4 3.7 %collective-permute-done.11 = f32[8,128]{1,0:T(8,128)S(1)} collective-permute-done((f32[8,128]{1,0:T(8,128)S(1)}, f32[8,128]{1,0:T(8,128)S(1)}, u32[]{:S(2)}, u32[]{:S(2)}) %collective-permute-start.11) | collective-permute-done | bytes 4128 | tf_op jit(solution)/shard_map/ppermute | solution.py:253
  169.1 19.5 %all_to_all.19 = f32[16,1,128]{2,1,0:T(1,128)S(1)} all-to-all(f32[16,1,128]{2,1,0:T(1,128)S(1)} %bitcast.140), channel_id=1, replica_groups={{0,1,2,3,4,5,6,7,64,65,66,67,68,69,70,71},{8,9,10,11,12,13,14,15,72,73,..., dimensions={0} | all-to-all | bytes 16384 | tf_op jit(solution)/shard_map/all_to_all | solution.py:289
  189.3 2.5 %collective-permute-start.5 = (bf16[128,512]{1,0:T(8,128)(2,1)S(1)}, bf16[128,512]{1,0:T(8,128)(2,1)S(1)}, u32[]{:S(2)}, u32[]{:S(2)}) collective-permute-start(bf16[128,512]{1,0:T(8,128)(2,1)S(1)} %bitcast.130), channel_id=1, source_target_pairs={{0,2},{1,3},{2,0},{3,1},{4,6},{5,7},{6,4},{7,5},{8,10},{9,11},{10,... | collective-permute-start | bytes 393224 | tf_op jit(solution)/shard_map/ppermute | solution.py:253
  191.9 6.6 %collective-permute-done.5 = bf16[128,512]{1,0:T(8,128)(2,1)S(1)} collective-permute-done((bf16[128,512]{1,0:T(8,128)(2,1)S(1)}, bf16[128,512]{1,0:T(8,128)(2,1)S(1)}, u32[]{:S(2)}, u32[]{:S(2)}) %collective-permute-start.5) | collective-permute-done | bytes 131104 | tf_op jit(solution)/shard_map/ppermute | solution.py:253
  198.5 2.5 %collective-permute-start.6 = (bf16[256,512]{1,0:T(8,128)(2,1)S(1)}, bf16[256,512]{1,0:T(8,128)(2,1)S(1)}, u32[]{:S(2)}, u32[]{:S(2)}) collective-permute-start(bf16[256,512]{1,0:T(8,128)(2,1)S(1)} %pad_maximum_fusion.3), channel_id=1, source_target_pairs={{0,1},{1,0},{2,3},{3,2},{4,5},{5,4},{6,7},{7,6},{8,9},{9,8},{10,11... | collective-permute-start | bytes 786440 | tf_op jit(solution)/shard_map/ppermute | solution.py:253
  201.6 5.1 %collective-permute-done.6 = bf16[256,512]{1,0:T(8,128)(2,1)S(1)} collective-permute-done((bf16[256,512]{1,0:T(8,128)(2,1)S(1)}, bf16[256,512]{1,0:T(8,128)(2,1)S(1)}, u32[]{:S(2)}, u32[]{:S(2)}) %collective-permute-start.6) | collective-permute-done | bytes 262176 | tf_op jit(solution)/shard_map/ppermute | solution.py:253
  206.8 2.8 %orthonormalize.1 = f32[64,512]{1,0:T(8,128)S(1)} custom-call(bf16[512,512]{1,0:T(8,128)(2,1)S(1)} %pad_maximum_fusion.1.x_ref, f32[64,512]{1,0:T(8,128)S(1)} %slice_bitcast_fusion.own_ref), custom_call_target="tpu_custom_call" | custom-call | tf_op jit(solution)/shard_map/orthonormalize/pallas_call | solution.py:237
  (46 shorter events, 13.1 us)
Async XLA Ops:
  3.7 12.7 %copy-start = (bf16[1,64,2,256]{3,2,1,0:T(2,128)(2,1)S(1)}, bf16[1,64,2,256]{3,2,1,0:T(2,128)(2,1)}, u32[]{:S(2)}) copy-start(bf16[1,64,2,256]{3,2,1,0:T(2,128)(2,1)} %param.6) | copy-start | bytes 196612
  3.7 102.2 %all-to-all-start = ((bf16[8,2,64,512]{3,2,1,0:T(8,128)(2,1)}), bf16[8,2,64,512]{3,2,1,0:T(8,128)(2,1)S(1)}, u32[]{:S(2)}, u32[]{:S(2)}) async-start(bf16[8,2,64,512]{3,2,1,0:T(8,128)(2,1)} %sort_mats.1), calls=%async_computation | async-start | bytes 2097152 | tf_op jit(solution)/shard_map/all_to_all | solution.py:263
  16.4 66.6 %copy-start.2 = (s32[1,8,3]{1,0,2:T(1,128)S(1)}, s32[1,8,3]{1,0,2:T(1,128)}, u32[]{:S(2)}) copy-start(s32[1,8,3]{1,0,2:T(1,128)} %param.8) | copy-start | bytes 292
  16.4 56.8 %collective-permute-start = (bf16[64,512]{1,0:T(8,128)(2,1)S(1)}, bf16[64,512]{1,0:T(8,128)(2,1)S(1)}, u32[]{:S(2)}, u32[]{:S(2)}) collective-permute-start(bf16[64,512]{1,0:T(8,128)(2,1)S(1)} %bitcast.139), channel_id=1, source_target_pairs={{0,4},{1,5},{2,6},{3,7},{4,0},{5,1},{6,2},{7,3},{8,12},{9,13},{10,... | collective-permute-start | bytes 196616 | tf_op jit(solution)/shard_map/ppermute | solution.py:253
  73.3 22.1 %copy-start.1 = (s32[1,8]{1,0:T(1,128)S(1)}, s32[1,8]{1,0:T(1,128)}, u32[]{:S(2)}) copy-start(s32[1,8]{1,0:T(1,128)} %param.7) | copy-start | bytes 100
  73.3 7.8 %collective-permute-start.1 = (bf16[2,64,512]{2,1,0:T(8,128)(2,1)S(1)}, bf16[2,64,512]{2,1,0:T(8,128)(2,1)S(1)}, u32[]{:S(2)}, u32[]{:S(2)}) collective-permute-start(bf16[2,64,512]{2,1,0:T(8,128)(2,1)S(1)} %get-tuple-element.14), channel_id=1, source_target_pairs={{0,2},{1,3},{2,0},{3,1},{4,6},{5,7},{6,4},{7,5},{8,10},{9,11},{10,... | collective-permute-start | bytes 393224 | tf_op jit(solution)/shard_map/ppermute | solution.py:253
  81.1 8.3 %collective-permute-start.2 = (bf16[2,2,64,512]{3,2,1,0:T(8,128)(2,1)S(1)}, bf16[2,2,64,512]{3,2,1,0:T(8,128)(2,1)S(1)}, u32[]{:S(2)}, u32[]{:S(2)}) collective-permute-start(bf16[2,2,64,512]{3,2,1,0:T(8,128)(2,1)S(1)} %get-tuple-element.12), channel_id=1, source_target_pairs={{0,1},{1,0},{2,3},{3,2},{4,5},{5,4},{6,7},{7,6},{8,9},{9,8},{10,11... | collective-permute-start | bytes 786440 | tf_op jit(solution)/shard_map/ppermute | solution.py:253
  89.4 16.6 %collective-permute-start.3 = (bf16[8,64,512]{2,1,0:T(8,128)(2,1)S(1)}, bf16[8,64,512]{2,1,0:T(8,128)(2,1)S(1)}, u32[]{:S(2)}, u32[]{:S(2)}) collective-permute-start(bf16[8,64,512]{2,1,0:T(8,128)(2,1)S(1)} %bitcast.128), channel_id=1, source_target_pairs={{130,2},{387,3},{33,1},{103,0},{12,4},{29,5},{174,6},{504,7},{138,... | collective-permute-start | bytes 1572872 | tf_op jit(solution)/shard_map/ppermute | solution.py:267
  111.3 24.2 %all-to-all-start.1 = ((bf16[4,2,96,512]{3,2,1,0:T(8,128)(2,1)}), bf16[4,2,96,512]{3,2,1,0:T(8,128)(2,1)S(1)}, u32[]{:S(2)}, u32[]{:S(2)}) async-start(bf16[4,2,96,512]{3,2,1,0:T(8,128)(2,1)} %get-tuple-element.5), calls=%async_computation.1 | async-start | bytes 1572864 | tf_op jit(solution)/shard_map/all_to_all | solution.py:248
  114.8 29.3 %collective-permute-start.7 = (f32[8,128]{1,0:T(8,128)S(1)}, f32[8,128]{1,0:T(8,128)S(1)}, u32[]{:S(2)}, u32[]{:S(2)}) collective-permute-start(f32[8,128]{1,0:T(8,128)S(1)} %get-tuple-element.6), channel_id=1, source_target_pairs={{0,8},{8,0},{16,24},{24,16},{32,40},{40,32},{48,56},{56,48},{64,72... | collective-permute-start | bytes 12296 | tf_op jit(solution)/shard_map/ppermute | solution.py:253
  135.7 53.5 %collective-permute-start.4 = (bf16[160,512]{1,0:T(8,128)(2,1)S(1)}, bf16[160,512]{1,0:T(8,128)(2,1)S(1)}, u32[]{:S(2)}, u32[]{:S(2)}) collective-permute-start(bf16[160,512]{1,0:T(8,128)(2,1)S(1)} %pad_maximum_fusion.4), channel_id=1, source_target_pairs={{0,4},{1,5},{2,6},{3,7},{4,0},{5,1},{6,2},{7,3},{8,12},{9,13},{10,... | collective-permute-start | bytes 491528 | tf_op jit(solution)/shard_map/ppermute | solution.py:253
  144.1 5.5 %collective-permute-start.8 = (f32[8,128]{1,0:T(8,128)S(1)}, f32[8,128]{1,0:T(8,128)S(1)}, u32[]{:S(2)}, u32[]{:S(2)}) collective-permute-start(f32[8,128]{1,0:T(8,128)S(1)} %add.173), channel_id=1, source_target_pairs={{0,16},{8,24},{16,0},{24,8},{32,48},{40,56},{48,32},{56,40},{64,80... | collective-permute-start | bytes 12296 | tf_op jit(solution)/shard_map/ppermute | solution.py:253
  149.6 7.0 %collective-permute-start.9 = (f32[8,128]{1,0:T(8,128)S(1)}, f32[8,128]{1,0:T(8,128)S(1)}, u32[]{:S(2)}, u32[]{:S(2)}) collective-permute-start(f32[8,128]{1,0:T(8,128)S(1)} %add.174), channel_id=1, source_target_pairs={{0,32},{8,40},{16,48},{24,56},{32,0},{40,8},{48,16},{56,24},{64,96... | collective-permute-start | bytes 12296 | tf_op jit(solution)/shard_map/ppermute | solution.py:253
  156.6 5.5 %collective-permute-start.10 = (f32[8,128]{1,0:T(8,128)S(1)}, f32[8,128]{1,0:T(8,128)S(1)}, u32[]{:S(2)}, u32[]{:S(2)}) collective-permute-start(f32[8,128]{1,0:T(8,128)S(1)} %add.175), channel_id=1, source_target_pairs={{0,128},{8,136},{16,144},{24,152},{32,160},{40,168},{48,176},{56,1... | collective-permute-start | bytes 12296 | tf_op jit(solution)/shard_map/ppermute | solution.py:253
  162.1 7.0 %collective-permute-start.11 = (f32[8,128]{1,0:T(8,128)S(1)}, f32[8,128]{1,0:T(8,128)S(1)}, u32[]{:S(2)}, u32[]{:S(2)}) collective-permute-start(f32[8,128]{1,0:T(8,128)S(1)} %add.176), channel_id=1, source_target_pairs={{0,256},{8,264},{16,272},{24,280},{32,288},{40,296},{48,304},{56,3... | collective-permute-start | bytes 12296 | tf_op jit(solution)/shard_map/ppermute | solution.py:253
  189.3 9.2 %collective-permute-start.5 = (bf16[128,512]{1,0:T(8,128)(2,1)S(1)}, bf16[128,512]{1,0:T(8,128)(2,1)S(1)}, u32[]{:S(2)}, u32[]{:S(2)}) collective-permute-start(bf16[128,512]{1,0:T(8,128)(2,1)S(1)} %bitcast.130), channel_id=1, source_target_pairs={{0,2},{1,3},{2,0},{3,1},{4,6},{5,7},{6,4},{7,5},{8,10},{9,11},{10,... | collective-permute-start | bytes 393224 | tf_op jit(solution)/shard_map/ppermute | solution.py:253
  198.5 8.3 %collective-permute-start.6 = (bf16[256,512]{1,0:T(8,128)(2,1)S(1)}, bf16[256,512]{1,0:T(8,128)(2,1)S(1)}, u32[]{:S(2)}, u32[]{:S(2)}) collective-permute-start(bf16[256,512]{1,0:T(8,128)(2,1)S(1)} %pad_maximum_fusion.3), channel_id=1, source_target_pairs={{0,1},{1,0},{2,3},{3,2},{4,5},{5,4},{6,7},{7,6},{8,9},{9,8},{10,11... | collective-permute-start | bytes 786440 | tf_op jit(solution)/shard_map/ppermute | solution.py:253

commit v3 on v2

--- a/solution.py
+++ b/solution.py
@@ -89,26 +89,38 @@
     return pairs
 
 
-def sort_kernel(k_ref, near_ref, m_ref, out_ref, sems):
+EARLY = 16
+
+
+def sort_kernel(k_ref, near_ref, m_ref, early_ref, late_ref, sems):
     k = k_ref[0]
     copies = []
     for b in range(8):
         slot = owner_of(k, *difference(near_ref[b], k))
-        copy = pltpu.make_async_copy(m_ref.at[b], out_ref.at[slot], sems.at[b])
-        copy.start()
-        copies.append(copy)
+        for part, (out_ref, rows) in enumerate(
+            ((early_ref, pl.ds(0, EARLY)), (late_ref, pl.ds(EARLY, 64 - EARLY)))
+        ):
+            copy = pltpu.make_async_copy(
+                m_ref.at[b, :, rows], out_ref.at[slot], sems.at[part, b]
+            )
+            copy.start()
+            copies.append(copy)
     for copy in copies:
         copy.wait()
 
 
 def sorted_by_owner(kpoint_index, near, mats):
     smem = pl.BlockSpec(memory_space=pltpu.SMEM)
+    vmem = pl.BlockSpec(memory_space=pltpu.VMEM)
     return pl.pallas_call(
         sort_kernel,
-        out_shape=jax.ShapeDtypeStruct(mats.shape, mats.dtype),
+        out_shape=(
+            jax.ShapeDtypeStruct((8, 2, EARLY, 512), BF),
+            jax.ShapeDtypeStruct((8, 2, 64 - EARLY, 512), BF),
+        ),
         in_specs=[smem, smem, pl.BlockSpec(memory_space=pl.ANY)],
-        out_specs=pl.BlockSpec(memory_space=pltpu.VMEM),
-        scratch_shapes=[pltpu.SemaphoreType.DMA((8,))],
+        out_specs=(vmem, vmem),
+        scratch_shapes=[pltpu.SemaphoreType.DMA((2, 8))],
         name="sort_mats",
     )(kpoint_index.reshape(1), near, mats)
 
@@ -122,10 +134,12 @@
     return jnp.concatenate(blocks, 0)
 
 
-def main_kernel(w_ref, holder_ref, m_ref, u_ref, n_ref, z_ref, omega_ref):
+def main_kernel(w_ref, holder_ref, early_ref, late_ref, u_ref, n_ref, z_ref):
     w = w_ref[0]
-    a_r = m_ref[:, 0].reshape(512, 512)
-    a_i = m_ref[:, 1].reshape(512, 512)
+    a_r, a_i = (
+        jnp.concatenate([ref[r, p] for r in range(8) for ref in (early_ref, late_ref)], 0)
+        for p in range(2)
+    )
     u = rows_in_order(u_ref, holder_ref[0])
     n = rows_in_order(n_ref, holder_ref[1])
     half = jnp.right_shift(holder_ref[0], 2)
@@ -156,8 +170,9 @@
     g_i = 2.0 * w * ((mi * row_r - mr * row_i) + (ti * col_r - tr * col_i))
     square = jnp.where(eye, zero, mr * mr + mi * mi)
     omega = jnp.sum(jnp.sum(square, 0, keepdims=True), 1, keepdims=True)
-    omega_ref[...] = jnp.broadcast_to(omega * (w / (64 * 256)), omega_ref.shape)
-    b_r, b_i = g_r.astype(BF), g_i.astype(BF)
+    omega = omega * (w / (64 * 256))
+    b_r = jnp.where(eye & (row % 32 == 0), omega, g_r).astype(BF)
+    b_i = g_i.astype(BF)
     gt_r = -STEP_LENGTH * g_r - MIXING * h_r
     gt_i = STEP_LENGTH * g_i + MIXING * h_i
     gts = jnp.concatenate([gt_r, gt_i], 0).astype(BF)
@@ -181,20 +196,17 @@
             z_ref[l, to, 64:, 256:] = b_i[at : at + 32]
 
 
-def main_products(w, holders, mats, full, near):
+def main_products(w, holders, early, late, full, near):
     vmem = pl.BlockSpec(memory_space=pltpu.VMEM)
     smem = pl.BlockSpec(memory_space=pltpu.SMEM)
     return pl.pallas_call(
         main_kernel,
-        out_shape=(
-            jax.ShapeDtypeStruct((4, 2, 96, 512), BF),
-            jax.ShapeDtypeStruct((8, 128), F32),
-        ),
-        in_specs=[smem, smem, vmem, vmem, vmem],
-        out_specs=(vmem, vmem),
+        out_shape=jax.ShapeDtypeStruct((4, 2, 96, 512), BF),
+        in_specs=[smem, smem, vmem, vmem, vmem, vmem],
+        out_specs=vmem,
         compiler_params=pltpu.CompilerParams(vmem_limit_bytes=48 << 20),
         name="main_products",
-    )(w.reshape(1), holders, mats, full, near)
+    )(w.reshape(1), holders, early, late, full, near)
 
 
 def cdot(ar, ai, br, bi):
@@ -228,15 +240,15 @@
     own = own_ref[...]
     o_r, o_i = own[:, :256], own[:, 256:]
     e_r, e_i = cdot(o_r, o_i, p_r, p_i)
-    out_ref[:, :256] = scale * (o_r + e_r)
-    out_ref[:, 256:] = scale * (o_i + e_i)
+    out_ref[:, 0] = scale * (o_r + e_r)
+    out_ref[:, 1] = scale * (o_i + e_i)
 
 
 def orthonormalized(full, own):
     vmem = pl.BlockSpec(memory_space=pltpu.VMEM)
     return pl.pallas_call(
         orth_kernel,
-        out_shape=jax.ShapeDtypeStruct((64, 512), F32),
+        out_shape=jax.ShapeDtypeStruct((64, 2, 256), F32),
         in_specs=[vmem, vmem],
         out_specs=vmem,
         compiler_params=pltpu.CompilerParams(vmem_limit_bytes=48 << 20),
@@ -253,14 +265,23 @@
     return lax.ppermute(x, axis, [(i, i ^ bit) for i in range(length)])
 
 
+def half_ring_permutation():
+    pairs = []
+    for k in range(64):
+        for c in range(8):
+            pairs.append((8 * k + c, 8 * (k ^ 8) + (c ^ 4)))
+    return pairs
+
+
 def per_device(correlations, gauge, neighbours, shifts):
     kpoint_index = lax.axis_index("ka")
     cindex = lax.axis_index("col")
     near, shift = neighbours[0], shifts[0]
 
     own = gauge[0].reshape(64, 512)
-    mats = sorted_by_owner(kpoint_index, near, correlations[0])
-    mats = lax.all_to_all(mats, "col", 0, 0, tiled=True)
+    early, late = sorted_by_owner(kpoint_index, near, correlations[0])
+    early = lax.all_to_all(early, "col", 0, 0, tiled=True)
+    late = lax.all_to_all(late, "col", 0, 0, tiled=True)
     pair = jnp.stack([own, partner(own, "col", 4)])
     full = jnp.stack([pair, partner(pair, "col", 2)])
     full = jnp.stack([full, partner(full, "col", 1)]).reshape(8, 64, 512)
@@ -272,37 +293,27 @@
     weights = shell_vector_weights(kpoint_index, near, shift)
     weight = jnp.sum(jnp.where(owners == cindex, weights, 0.0))
 
-    z, spread = main_products(weight, holders, mats, full, near_full)
-
-    z = within_half(z)
-    for bit in (1, 2, 4, 16):
-        spread = spread + partner(spread, "ka", bit)
-    z = z.astype(F32).sum(0)
+    z = main_products(weight, holders, early, late, full, near_full)
+
+    z = within_half(z).astype(F32).sum(0)
     arrived = jnp.concatenate([z[0, :64], z[1]], 0).astype(BF)
     arrived = partner(arrived, "col", 4).astype(F32)
-    spread = spread + partner(spread, "ka", 32)
-    groups = [
-        [8 * (16 * y + 8 * h + x) + c for h in range(2) for c in range(8)]
-        for y in range(4)
-        for x in range(8)
-    ]
-    spread = lax.all_to_all(
-        jnp.concatenate([spread, spread], 0),
-        ("ka", "col"),
-        0,
-        0,
-        tiled=True,
-        axis_index_groups=groups,
-    ).sum(0)
-    x = pair.astype(F32) + jnp.stack([z[0, :64] + arrived[64:128], z[1, :64] + arrived[:64]])
-    g = z[0, 64:] + arrived[128:]
+    x = pair.astype(F32) + z[:, :64] + jnp.stack([arrived[64:128], arrived[:64]])
     full_x = x.astype(BF).reshape(128, 512)
     for bit in (2, 1):
         full_x = jnp.concatenate([full_x, partner(full_x, "col", bit)], 0)
-    own_x = x[0]
-    u_next = orthonormalized(full_x, own_x)
-    gradient = jnp.stack([g[:, :256], g[:, 256:]])[None]
-    return (u_next.reshape(1, 64, 2, 256), gradient, spread[0])
+    carries = jnp.arange(256)[None] == 32 * cindex
+    groups = [[16 * y + 8 * z_hi + x for y in range(4) for x in range(8)] for z_hi in range(2)]
+    spread = jnp.broadcast_to(jnp.where(carries, z[0, 64:65, :256], 0.0), (32, 256))
+    spread = lax.all_to_all(spread, "ka", 0, 0, tiled=True, axis_index_groups=groups)
+    spread = jnp.broadcast_to(spread.sum(0, keepdims=True), (8, 256))
+    spread = spread + partner(spread, "col", 4)
+    spread = spread + lax.ppermute(spread, ("ka", "col"), half_ring_permutation())
+    u_next = orthonormalized(full_x, x[0])
+    g = z[0, 64:] + arrived[128:]
+    first = jnp.logical_and(carries, jnp.arange(32)[:, None] == 0)
+    gradient = jnp.stack([jnp.where(first, 0.0, g[:, :256]), g[:, 256:]])[None]
+    return (u_next[None], gradient, jnp.sum(spread[0]))
 
 
 def solution(mesh):

time: 211 us -> 209 us (level)
  the two profiles are of different devices: /device:TPU:2 before, /device:TPU:1 now
where the time goes in v3:
time: 209 us; the launch traced here: 208 us
  waiting for transfers between devices  106 us (51%)
  starting transfers between devices  59.6 us (29%)
  blocking collectives  25.5 us (12%)
  Pallas kernels  12.2 us (6%)
  other arithmetic  2.76 us (1%)
    ppermute x7, waiting for transfers between devices, partner(): return lax.ppermute(x, axis, [(i, i ^ bit) for i in range(length)])  69.1 us
    all_to_all x1, blocking collectives, per_device(): early = lax.all_to_all(early, 'col', 0, 0, tiled=True)  25.5 us
    ppermute x7, starting transfers between devices, partner(): return lax.ppermute(x, axis, [(i, i ^ bit) for i in range(length)])  24.2 us
    all_to_all x1, waiting for transfers between devices, within_half(): return lax.all_to_all(x, 'col', 0, 0, tiled=True, axis_index_groups=HALVES)  20.2 us
    ppermute x1, starting transfers between devices, per_device(): near_full = lax.ppermute(full, ('ka', 'col'), fetch_permutation())  10.8 us
    all_to_all x1, starting transfers between devices, per_device(): late = lax.all_to_all(late, 'col', 0, 0, tiled=True)  9.14 us
    ppermute x1, waiting for transfers between devices, per_device(): near_full = lax.ppermute(full, ('ka', 'col'), fetch_permutation())  8.29 us
    all_to_all x1, waiting for transfers between devices, per_device(): lax.all_to_all(spread, 'ka', 0, 0, tiled=True, axis_index_groups=groups)  7.24 us
  transfers between devices with their start and end apart: 12, of which 10 were waited for; matrix products, arithmetic and copies ran while one was open for 1% of the time, Pallas kernels for 0%

profile of v3, /device:TPU:1, one launch (start us, length us, event | category | flops | bytes accessed | tf_op | source)
XLA Modules:
  0.0 207.8 jit_solution(14124950551630969490)
XLA Ops:
  0.6 3.2 %sort_mats.1 = (bf16[8,2,16,512]{3,2,1,0:T(8,128)(2,1)}, bf16[8,2,48,512]{3,2,1,0:T(8,128)(2,1)}) custom-call(s32[1]{0:T(128)} %bitcast.12.k_ref, s32[8]{0:T(128)} %bitcast.130, bf16[8,2,64,512]{3,2,1,0:T(8,128)(2,1)} %bitcast.122), custom_call_target="tpu_custom_call" | custom-call | tf_op jit(solution)/shard_map/sort_mats/pallas_call | solution.py:115
  3.8 25.5 %all_to_all.21.early_ref = bf16[8,2,16,512]{3,2,1,0:T(8,128)(2,1)S(1)} all-to-all(bf16[8,2,16,512]{3,2,1,0:T(8,128)(2,1)} %get-tuple-element.5), channel_id=1, replica_groups=mesh['ka'=64,'col'=8] {'col'}, dimensions={0} | all-to-all | bytes 524288 | tf_op jit(solution)/shard_map/all_to_all | solution.py:283
  29.3 9.1 %all-to-all-start.1 = ((bf16[8,2,48,512]{3,2,1,0:T(8,128)(2,1)}), bf16[8,2,48,512]{3,2,1,0:T(8,128)(2,1)S(1)}, u32[]{:S(2)}, u32[]{:S(2)}) async-start(bf16[8,2,48,512]{3,2,1,0:T(8,128)(2,1)} %get-tuple-element.6), calls=%async_computation.1 | async-start | bytes 1572864 | tf_op jit(solution)/shard_map/all_to_all | solution.py:284
  38.5 7.3 %collective-permute-start = (bf16[64,512]{1,0:T(8,128)(2,1)S(1)}, bf16[64,512]{1,0:T(8,128)(2,1)S(1)}, u32[]{:S(2)}, u32[]{:S(2)}) collective-permute-start(bf16[64,512]{1,0:T(8,128)(2,1)S(1)} %bitcast.129), channel_id=1, source_target_pairs={{0,4},{1,5},{2,6},{3,7},{4,0},{5,1},{6,2},{7,3},{8,12},{9,13},{10,... | collective-permute-start | bytes 196616 | tf_op jit(solution)/shard_map/ppermute | solution.py:265
  45.8 36.7 %collective-permute-done = bf16[64,512]{1,0:T(8,128)(2,1)S(1)} collective-permute-done((bf16[64,512]{1,0:T(8,128)(2,1)S(1)}, bf16[64,512]{1,0:T(8,128)(2,1)S(1)}, u32[]{:S(2)}, u32[]{:S(2)}) %collective-permute-start) | collective-permute-done | bytes 65568 | tf_op jit(solution)/shard_map/ppermute | solution.py:265
  82.5 1.9 collective-permute-start.1
  84.5 6.1 %collective-permute-done.1 = bf16[2,64,512]{2,1,0:T(8,128)(2,1)S(1)} collective-permute-done((bf16[2,64,512]{2,1,0:T(8,128)(2,1)S(1)}, bf16[2,64,512]{2,1,0:T(8,128)(2,1)S(1)}, u32[]{:S(2)}, u32[]{:S(2)}) %collective-permute-start.1) | collective-permute-done | bytes 131104 | tf_op jit(solution)/shard_map/ppermute | solution.py:265
  90.6 1.9 collective-permute-start.2
  92.8 5.3 %collective-permute-done.2 = bf16[2,2,64,512]{3,2,1,0:T(8,128)(2,1)S(1)} collective-permute-done((bf16[2,2,64,512]{3,2,1,0:T(8,128)(2,1)S(1)}, bf16[2,2,64,512]{3,2,1,0:T(8,128)(2,1)S(1)}, u32[]{:S(2)}, u32[]{:S(2)}) %collective-permute-start.2) | collective-permute-done | bytes 262176 | tf_op jit(solution)/shard_map/ppermute | solution.py:265
  98.2 10.8 %collective-permute-start.3 = (bf16[8,64,512]{2,1,0:T(8,128)(2,1)S(1)}, bf16[8,64,512]{2,1,0:T(8,128)(2,1)S(1)}, u32[]{:S(2)}, u32[]{:S(2)}) collective-permute-start(bf16[8,64,512]{2,1,0:T(8,128)(2,1)S(1)} %bitcast.117), channel_id=1, source_target_pairs={{130,2},{387,3},{33,1},{103,0},{12,4},{29,5},{174,6},{504,7},{138,... | collective-permute-start | bytes 1572872 | tf_op jit(solution)/shard_map/ppermute | solution.py:288
  109.8 8.3 %collective-permute-done.3.n_ref = bf16[8,64,512]{2,1,0:T(8,128)(2,1)S(1)} collective-permute-done((bf16[8,64,512]{2,1,0:T(8,128)(2,1)S(1)}, bf16[8,64,512]{2,1,0:T(8,128)(2,1)S(1)}, u32[]{:S(2)}, u32[]{:S(2)}) %collective-permute-start.3) | collective-permute-done | bytes 524320 | tf_op jit(solution)/shard_map/ppermute | solution.py:288
  118.1 5.5 %main_products.1 = bf16[4,2,96,512]{3,2,1,0:T(8,128)(2,1)} custom-call(f32[1]{0:T(128)} %bitcast.9.w_ref, s32[2]{0:T(128)S(1)} %pad_add_fusion.1.holder_ref, bf16[8,2,16,512]{3,2,1,0:T(8,128)(2,1)S(1)} %all_to_all.21.early_ref, bf16[8,2,48,512]{3,2,1,0:T(8,128)(2,1)S(1)} %all-to-all-done.1.late_ref, bf16[8,64,512]{2,1,0:T(8,128)(2,1)S(1)} %bitcast.118, ...), custom_call_target="tpu_custom_call" | custom-call | tf_op jit(solution)/shard_map/main_products/pallas_call | solution.py:202
  123.6 3.5 %all-to-all-start.2 = ((bf16[4,2,96,512]{3,2,1,0:T(8,128)(2,1)}), bf16[4,2,96,512]{3,2,1,0:T(8,128)(2,1)S(1)}, u32[]{:S(2)}, u32[]{:S(2)}) async-start(bf16[4,2,96,512]{3,2,1,0:T(8,128)(2,1)} %main_products.1), calls=%async_computation.2 | async-start | bytes 1572864 | tf_op jit(solution)/shard_map/all_to_all | solution.py:260
  127.1 20.2 %all-to-all-done.2 = bf16[4,2,96,512]{3,2,1,0:T(8,128)(2,1)S(1)} async-done(((bf16[4,2,96,512]{3,2,1,0:T(8,128)(2,1)}), bf16[4,2,96,512]{3,2,1,0:T(8,128)(2,1)S(1)}, u32[]{:S(2)}, u32[]{:S(2)}) %all-to-all-start.2) | async-done | bytes 786464 | tf_op jit(solution)/shard_map/all_to_all | solution.py:260
  148.2 4.8 %all-to-all-start.3 = ((f32[32,1,256]{2,1,0:T(1,128)}), f32[32,1,256]{2,1,0:T(1,128)S(1)}, u32[]{:S(2)}, u32[]{:S(2)}) async-start(f32[32,1,256]{2,1,0:T(1,128)} %broadcast_in_dim.54), calls=%async_computation.3 | async-start | bytes 65536 | tf_op jit(solution)/shard_map/all_to_all | solution.py:308
  153.0 7.2 %all-to-all-done.3 = f32[32,1,256]{2,1,0:T(1,128)S(1)} async-done(((f32[32,1,256]{2,1,0:T(1,128)}), f32[32,1,256]{2,1,0:T(1,128)S(1)}, u32[]{:S(2)}, u32[]{:S(2)}) %all-to-all-start.3) | async-done | bytes 32800 | tf_op jit(solution)/shard_map/all_to_all | solution.py:308
  160.3 7.3 %collective-permute-start.7 = (f32[8,256]{1,0:T(8,128)S(1)}, f32[8,256]{1,0:T(8,128)S(1)}, u32[]{:S(2)}, u32[]{:S(2)}) collective-permute-start(f32[8,256]{1,0:T(8,128)S(1)} %broadcast_in_dim.55), channel_id=1, source_target_pairs={{0,4},{1,5},{2,6},{3,7},{4,0},{5,1},{6,2},{7,3},{8,12},{9,13},{10,... | collective-permute-start | bytes 24584 | tf_op jit(solution)/shard_map/ppermute | solution.py:265
  167.7 1.9 collective-permute-start.4
  169.6 7.1 %collective-permute-start.8 = (f32[8,256]{1,0:T(8,128)S(1)}, f32[8,256]{1,0:T(8,128)S(1)}, u32[]{:S(2)}, u32[]{:S(2)}) collective-permute-start(f32[8,256]{1,0:T(8,128)S(1)} %broadcast_add_fusion), channel_id=1, source_target_pairs={{0,68},{1,69},{2,70},{3,71},{4,64},{5,65},{6,66},{7,67},{8,76},{9,... | collective-permute-start | bytes 24584 | tf_op jit(solution)/shard_map/ppermute | solution.py:311
  178.5 9.8 %collective-permute-done.4 = bf16[160,512]{1,0:T(8,128)(2,1)S(1)} collective-permute-done((bf16[160,512]{1,0:T(8,128)(2,1)S(1)}, bf16[160,512]{1,0:T(8,128)(2,1)S(1)}, u32[]{:S(2)}, u32[]{:S(2)}) %collective-permute-start.4) | collective-permute-done | bytes 163872 | tf_op jit(solution)/shard_map/ppermute | solution.py:265
  190.5 5.3 %collective-permute-done.5 = bf16[128,512]{1,0:T(8,128)(2,1)S(1)} collective-permute-done((bf16[128,512]{1,0:T(8,128)(2,1)S(1)}, bf16[128,512]{1,0:T(8,128)(2,1)S(1)}, u32[]{:S(2)}, u32[]{:S(2)}) %collective-permute-start.5) | collective-permute-done | bytes 131104 | tf_op jit(solution)/shard_map/ppermute | solution.py:265
  195.8 1.9 collective-permute-start.6
  198.4 5.8 %collective-permute-done.6 = bf16[256,512]{1,0:T(8,128)(2,1)S(1)} collective-permute-done((bf16[256,512]{1,0:T(8,128)(2,1)S(1)}, bf16[256,512]{1,0:T(8,128)(2,1)S(1)}, u32[]{:S(2)}, u32[]{:S(2)}) %collective-permute-start.6) | collective-permute-done | bytes 262176 | tf_op jit(solution)/shard_map/ppermute | solution.py:265
  204.3 3.5 %orthonormalize.1 = f32[64,2,256]{2,1,0:T(2,128)} custom-call(bf16[512,512]{1,0:T(8,128)(2,1)S(1)} %pad_maximum_fusion.1.x_ref, f32[64,512]{1,0:T(8,128)S(1)} %slice_bitcast_fusion.own_ref), custom_call_target="tpu_custom_call" | custom-call | tf_op jit(solution)/shard_map/orthonormalize/pallas_call | solution.py:249
  (44 shorter events, 6.6 us)
Async XLA Ops:
  3.8 34.6 %copy-start = (bf16[1,64,2,256]{3,2,1,0:T(2,128)(2,1)S(1)}, bf16[1,64,2,256]{3,2,1,0:T(2,128)(2,1)}, u32[]{:S(2)}) copy-start(bf16[1,64,2,256]{3,2,1,0:T(2,128)(2,1)} %param.6) | copy-start | bytes 196612
  29.3 88.8 %all-to-all-start.1 = ((bf16[8,2,48,512]{3,2,1,0:T(8,128)(2,1)}), bf16[8,2,48,512]{3,2,1,0:T(8,128)(2,1)S(1)}, u32[]{:S(2)}, u32[]{:S(2)}) async-start(bf16[8,2,48,512]{3,2,1,0:T(8,128)(2,1)} %get-tuple-element.6), calls=%async_computation.1 | async-start | bytes 1572864 | tf_op jit(solution)/shard_map/all_to_all | solution.py:284
  38.4 54.1 %copy-start.2 = (s32[1,8,3]{1,0,2:T(1,128)S(1)}, s32[1,8,3]{1,0,2:T(1,128)}, u32[]{:S(2)}) copy-start(s32[1,8,3]{1,0,2:T(1,128)} %param.8) | copy-start | bytes 292
  38.5 44.0 %collective-permute-start = (bf16[64,512]{1,0:T(8,128)(2,1)S(1)}, bf16[64,512]{1,0:T(8,128)(2,1)S(1)}, u32[]{:S(2)}, u32[]{:S(2)}) collective-permute-start(bf16[64,512]{1,0:T(8,128)(2,1)S(1)} %bitcast.129), channel_id=1, source_target_pairs={{0,4},{1,5},{2,6},{3,7},{4,0},{5,1},{6,2},{7,3},{8,12},{9,13},{10,... | collective-permute-start | bytes 196616 | tf_op jit(solution)/shard_map/ppermute | solution.py:265
  82.5 26.5 %copy-start.1 = (s32[1,8]{1,0:T(1,128)S(1)}, s32[1,8]{1,0:T(1,128)}, u32[]{:S(2)}) copy-start(s32[1,8]{1,0:T(1,128)} %param.7) | copy-start | bytes 100
  82.5 8.0 %collective-permute-start.1 = (bf16[2,64,512]{2,1,0:T(8,128)(2,1)S(1)}, bf16[2,64,512]{2,1,0:T(8,128)(2,1)S(1)}, u32[]{:S(2)}, u32[]{:S(2)}) collective-permute-start(bf16[2,64,512]{2,1,0:T(8,128)(2,1)S(1)} %get-tuple-element.14), channel_id=1, source_target_pairs={{0,2},{1,3},{2,0},{3,1},{4,6},{5,7},{6,4},{7,5},{8,10},{9,11},{10,... | collective-permute-start | bytes 393224 | tf_op jit(solution)/shard_map/ppermute | solution.py:265
  90.6 7.5 %collective-permute-start.2 = (bf16[2,2,64,512]{3,2,1,0:T(8,128)(2,1)S(1)}, bf16[2,2,64,512]{3,2,1,0:T(8,128)(2,1)S(1)}, u32[]{:S(2)}, u32[]{:S(2)}) collective-permute-start(bf16[2,2,64,512]{3,2,1,0:T(8,128)(2,1)S(1)} %get-tuple-element.12), channel_id=1, source_target_pairs={{0,1},{1,0},{2,3},{3,2},{4,5},{5,4},{6,7},{7,6},{8,9},{9,8},{10,11... | collective-permute-start | bytes 786440 | tf_op jit(solution)/shard_map/ppermute | solution.py:265
  98.2 19.9 %collective-permute-start.3 = (bf16[8,64,512]{2,1,0:T(8,128)(2,1)S(1)}, bf16[8,64,512]{2,1,0:T(8,128)(2,1)S(1)}, u32[]{:S(2)}, u32[]{:S(2)}) collective-permute-start(bf16[8,64,512]{2,1,0:T(8,128)(2,1)S(1)} %bitcast.117), channel_id=1, source_target_pairs={{130,2},{387,3},{33,1},{103,0},{12,4},{29,5},{174,6},{504,7},{138,... | collective-permute-start | bytes 1572872 | tf_op jit(solution)/shard_map/ppermute | solution.py:288
  123.6 23.8 %all-to-all-start.2 = ((bf16[4,2,96,512]{3,2,1,0:T(8,128)(2,1)}), bf16[4,2,96,512]{3,2,1,0:T(8,128)(2,1)S(1)}, u32[]{:S(2)}, u32[]{:S(2)}) async-start(bf16[4,2,96,512]{3,2,1,0:T(8,128)(2,1)} %main_products.1), calls=%async_computation.2 | async-start | bytes 1572864 | tf_op jit(solution)/shard_map/all_to_all | solution.py:260
  148.2 12.1 %all-to-all-start.3 = ((f32[32,1,256]{2,1,0:T(1,128)}), f32[32,1,256]{2,1,0:T(1,128)S(1)}, u32[]{:S(2)}, u32[]{:S(2)}) async-start(f32[32,1,256]{2,1,0:T(1,128)} %broadcast_in_dim.54), calls=%async_computation.3 | async-start | bytes 65536 | tf_op jit(solution)/shard_map/all_to_all | solution.py:308
  160.3 9.3 %collective-permute-start.7 = (f32[8,256]{1,0:T(8,128)S(1)}, f32[8,256]{1,0:T(8,128)S(1)}, u32[]{:S(2)}, u32[]{:S(2)}) collective-permute-start(f32[8,256]{1,0:T(8,128)S(1)} %broadcast_in_dim.55), channel_id=1, source_target_pairs={{0,4},{1,5},{2,6},{3,7},{4,0},{5,1},{6,2},{7,3},{8,12},{9,13},{10,... | collective-permute-start | bytes 24584 | tf_op jit(solution)/shard_map/ppermute | solution.py:265
  167.7 20.6 %collective-permute-start.4 = (bf16[160,512]{1,0:T(8,128)(2,1)S(1)}, bf16[160,512]{1,0:T(8,128)(2,1)S(1)}, u32[]{:S(2)}, u32[]{:S(2)}) collective-permute-start(bf16[160,512]{1,0:T(8,128)(2,1)S(1)} %pad_maximum_fusion.4), channel_id=1, source_target_pairs={{0,4},{1,5},{2,6},{3,7},{4,0},{5,1},{6,2},{7,3},{8,12},{9,13},{10,... | collective-permute-start | bytes 491528 | tf_op jit(solution)/shard_map/ppermute | solution.py:265
  169.6 8.3 %collective-permute-start.8 = (f32[8,256]{1,0:T(8,128)S(1)}, f32[8,256]{1,0:T(8,128)S(1)}, u32[]{:S(2)}, u32[]{:S(2)}) collective-permute-start(f32[8,256]{1,0:T(8,128)S(1)} %broadcast_add_fusion), channel_id=1, source_target_pairs={{0,68},{1,69},{2,70},{3,71},{4,64},{5,65},{6,66},{7,67},{8,76},{9,... | collective-permute-start | bytes 24584 | tf_op jit(solution)/shard_map/ppermute | solution.py:311
  188.5 7.4 %collective-permute-start.5 = (bf16[128,512]{1,0:T(8,128)(2,1)S(1)}, bf16[128,512]{1,0:T(8,128)(2,1)S(1)}, u32[]{:S(2)}, u32[]{:S(2)}) collective-permute-start(bf16[128,512]{1,0:T(8,128)(2,1)S(1)} %bitcast.119), channel_id=1, source_target_pairs={{0,2},{1,3},{2,0},{3,1},{4,6},{5,7},{6,4},{7,5},{8,10},{9,11},{10,... | collective-permute-start | bytes 393224 | tf_op jit(solution)/shard_map/ppermute | solution.py:265
  195.8 8.4 %collective-permute-start.6 = (bf16[256,512]{1,0:T(8,128)(2,1)S(1)}, bf16[256,512]{1,0:T(8,128)(2,1)S(1)}, u32[]{:S(2)}, u32[]{:S(2)}) collective-permute-start(bf16[256,512]{1,0:T(8,128)(2,1)S(1)} %pad_maximum_fusion.3), channel_id=1, source_target_pairs={{0,1},{1,0},{2,3},{3,2},{4,5},{5,4},{6,7},{7,6},{8,9},{9,8},{10,11... | collective-permute-start | bytes 786440 | tf_op jit(solution)/shard_map/ppermute | solution.py:265

commit v4 on v3

--- a/solution.py
+++ b/solution.py
@@ -1,3 +1,5 @@
+import functools
+
 import jax
 import jax.numpy as jnp
 from jax import lax
@@ -89,71 +91,101 @@
     return pairs
 
 
-EARLY = 16
-
-
-def sort_kernel(k_ref, near_ref, m_ref, early_ref, late_ref, sems):
+EARLY = 32
+
+
+def sort_kernel(k_ref, near_ref, m_ref, out_ref, sems, *, start):
     k = k_ref[0]
     copies = []
     for b in range(8):
         slot = owner_of(k, *difference(near_ref[b], k))
-        for part, (out_ref, rows) in enumerate(
-            ((early_ref, pl.ds(0, EARLY)), (late_ref, pl.ds(EARLY, 64 - EARLY)))
-        ):
-            copy = pltpu.make_async_copy(
-                m_ref.at[b, :, rows], out_ref.at[slot], sems.at[part, b]
-            )
-            copy.start()
-            copies.append(copy)
+        rows = pl.ds(start, out_ref.shape[2])
+        copy = pltpu.make_async_copy(m_ref.at[b, :, rows], out_ref.at[slot], sems.at[b])
+        copy.start()
+        copies.append(copy)
     for copy in copies:
         copy.wait()
 
 
-def sorted_by_owner(kpoint_index, near, mats):
+def sorted_by_owner(kpoint_index, near, mats, start, rows):
     smem = pl.BlockSpec(memory_space=pltpu.SMEM)
-    vmem = pl.BlockSpec(memory_space=pltpu.VMEM)
     return pl.pallas_call(
-        sort_kernel,
-        out_shape=(
-            jax.ShapeDtypeStruct((8, 2, EARLY, 512), BF),
-            jax.ShapeDtypeStruct((8, 2, 64 - EARLY, 512), BF),
-        ),
+        functools.partial(sort_kernel, start=start),
+        out_shape=jax.ShapeDtypeStruct((8, 2, rows, 512), BF),
         in_specs=[smem, smem, pl.BlockSpec(memory_space=pl.ANY)],
-        out_specs=(vmem, vmem),
-        scratch_shapes=[pltpu.SemaphoreType.DMA((2, 8))],
+        out_specs=pl.BlockSpec(memory_space=pltpu.VMEM),
+        scratch_shapes=[pltpu.SemaphoreType.DMA((8,))],
         name="sort_mats",
     )(kpoint_index.reshape(1), near, mats)
 
 
-def rows_in_order(ref, holder):
+def blocks_in_order(ref, holder):
     blocks = []
     for r in range(8):
         d = jnp.bitwise_xor(holder, r)
         at = 4 * jnp.bitwise_and(d, 1) + jnp.bitwise_and(d, 2) + jnp.right_shift(d, 2)
         blocks.append(ref[at])
-    return jnp.concatenate(blocks, 0)
-
-
-def main_kernel(w_ref, holder_ref, early_ref, late_ref, u_ref, n_ref, z_ref):
+    return blocks
+
+
+def part(ref, p):
+    return ref[:, p].reshape(8 * ref.shape[2], 512)
+
+
+def conj_left(p, q):
+    return jnp.concatenate([p[:256] + q[256:], q[:256] - p[256:]], 0)
+
+
+def overlap(ut, mats_ref, near):
+    qs = conj_left(dot_nt(ut, part(mats_ref, 0)), dot_nt(ut, part(mats_ref, 1))).astype(BF)
+    p = dot(qs, near)
+    return p[:256, :256] - p[256:, 256:], p[:256, 256:] + p[256:, :256]
+
+
+def prep_kernel(holder_ref, early_ref, u_ref, n_ref, ut_ref, near_e_ref, near_l_ref, mt_ref):
+    ut = jnp.concatenate(blocks_in_order(u_ref, holder_ref[0]), 0).T
+    ut_ref[...] = ut
+    blocks = blocks_in_order(n_ref, holder_ref[1])
+    near_e = jnp.concatenate([block[:EARLY] for block in blocks], 0)
+    near_e_ref[...] = near_e
+    near_l_ref[...] = jnp.concatenate([block[EARLY:] for block in blocks], 0)
+    mt_ref[0], mt_ref[1] = overlap(ut, early_ref, near_e)
+
+
+def prepared(holders, early, full, near):
+    vmem = pl.BlockSpec(memory_space=pltpu.VMEM)
+    smem = pl.BlockSpec(memory_space=pltpu.SMEM)
+    return pl.pallas_call(
+        prep_kernel,
+        out_shape=(
+            jax.ShapeDtypeStruct((512, 512), BF),
+            jax.ShapeDtypeStruct((8 * EARLY, 512), BF),
+            jax.ShapeDtypeStruct((512 - 8 * EARLY, 512), BF),
+            jax.ShapeDtypeStruct((2, 256, 256), F32),
+        ),
+        in_specs=[smem, vmem, vmem, vmem],
+        out_specs=(vmem, vmem, vmem, vmem),
+        compiler_params=pltpu.CompilerParams(vmem_limit_bytes=48 << 20),
+        name="prep",
+    )(holders, early, full, near)
+
+
+def main_kernel(
+    w_ref, holder_ref, early_ref, late_ref, ut_ref, near_e_ref, near_l_ref, mt_ref,
+    z_ref, scratch_ref, sems,
+):
     w = w_ref[0]
-    a_r, a_i = (
-        jnp.concatenate([ref[r, p] for r in range(8) for ref in (early_ref, late_ref)], 0)
-        for p in range(2)
-    )
-    u = rows_in_order(u_ref, holder_ref[0])
-    n = rows_in_order(n_ref, holder_ref[1])
     half = jnp.right_shift(holder_ref[0], 2)
-    ut = u.T
-    p = dot_nt(ut, a_r)
-    q = dot_nt(ut, a_i)
-    qs = jnp.concatenate([p[:256] + q[256:], q[:256] - p[256:]], 0).astype(BF)
-    p = dot(qs, n)
-    mt_r = (p[:256, :256] - p[256:, 256:]).astype(BF)
-    mt_i = (p[:256, 256:] + p[256:, :256]).astype(BF)
+    ut = ut_ref[...]
+    near_e, near_l = near_e_ref[...], near_l_ref[...]
+    mt_r, mt_i = overlap(ut, late_ref, near_l)
+    mt_r = (mt_ref[0] + mt_r).astype(BF)
+    mt_i = (mt_ref[1] + mt_i).astype(BF)
     mts = jnp.concatenate([mt_r, mt_i], 0)
-    p = dot_nt(mts, n[:, :256])
-    q = dot_nt(mts, n[:, 256:])
-    vts = (w * jnp.concatenate([p[:256] + q[256:], q[:256] - p[256:]], 0)).astype(BF)
+    vts_e, vts_l = (
+        (w * conj_left(dot_nt(mts, near[:, :256]), dot_nt(mts, near[:, 256:]))).astype(BF)
+        for near in (near_e, near_l)
+    )
     p = dot_nt(mts, mts)
     h_r = w * (p[:256, :256] + p[256:, 256:])
     h_i = w * (p[256:, :256] - p[:256, 256:])
@@ -173,40 +205,57 @@
     omega = omega * (w / (64 * 256))
     b_r = jnp.where(eye & (row % 32 == 0), omega, g_r).astype(BF)
     b_i = g_i.astype(BF)
+    copies = []
+
+    def send(rows, lanes):
+        piece = (slice(None), slice(None), rows, lanes)
+        copy = pltpu.make_async_copy(
+            scratch_ref.at[piece], z_ref.at[piece], sems.at[len(copies)]
+        )
+        copy.start()
+        copies.append(copy)
+
+    def store(value, rows, lanes):
+        size = value.shape[0] // 8
+        for h in range(2):
+            to = jnp.bitwise_xor(half, h)
+            for l in range(4):
+                at = size * (4 * h + l)
+                scratch_ref[l, to, rows, lanes] = value[at : at + size]
+
+    low, high = pl.ds(0, 256), pl.ds(256, 256)
+    store(b_r, pl.ds(64, 32), low)
+    store(b_i, pl.ds(64, 32), high)
+    send(pl.ds(64, 32), pl.ds(0, 512))
     gt_r = -STEP_LENGTH * g_r - MIXING * h_r
     gt_i = STEP_LENGTH * g_i + MIXING * h_i
     gts = jnp.concatenate([gt_r, gt_i], 0).astype(BF)
-    p = dot_nt(gts, u[:, :256])
-    q = dot_nt(gts, u[:, 256:])
-    zt_r = p[:256] - q[256:]
-    zt_i = q[:256] + p[256:]
-    p = dot(vts, a_r)
-    q = dot(vts, a_i)
-    zt_r = (zt_r + MIXING * (p[:256] - q[256:])).astype(BF)
-    zt_i = (zt_i + MIXING * (q[:256] + p[256:])).astype(BF)
-    z_r, z_i = zt_r.T, zt_i.T
-    for h in range(2):
-        for l in range(4):
-            to = jnp.bitwise_xor(half, h)
-            at = 64 * (4 * h + l)
-            z_ref[l, to, :64, :256] = z_r[at : at + 64]
-            z_ref[l, to, :64, 256:] = z_i[at : at + 64]
-            at = 32 * (4 * h + l)
-            z_ref[l, to, 64:, :256] = b_r[at : at + 32]
-            z_ref[l, to, 64:, 256:] = b_i[at : at + 32]
-
-
-def main_products(w, holders, early, late, full, near):
+    p = dot(gts, ut[:256])
+    q = dot(gts, ut[256:])
+    y_p = dot(vts_e, part(early_ref, 0)) + dot(vts_l, part(late_ref, 0))
+    y_q = dot(vts_e, part(early_ref, 1)) + dot(vts_l, part(late_ref, 1))
+    z_r = (p[:256] - q[256:] + MIXING * (y_p[:256] - y_q[256:])).astype(BF)
+    store(z_r.T, pl.ds(0, 64), low)
+    send(pl.ds(0, 64), low)
+    z_i = (q[:256] + p[256:] + MIXING * (y_q[:256] + y_p[256:])).astype(BF)
+    store(z_i.T, pl.ds(0, 64), high)
+    send(pl.ds(0, 64), high)
+    for copy in copies:
+        copy.wait()
+
+
+def main_products(w, holders, early, late, prep):
     vmem = pl.BlockSpec(memory_space=pltpu.VMEM)
     smem = pl.BlockSpec(memory_space=pltpu.SMEM)
     return pl.pallas_call(
         main_kernel,
         out_shape=jax.ShapeDtypeStruct((4, 2, 96, 512), BF),
-        in_specs=[smem, smem, vmem, vmem, vmem, vmem],
-        out_specs=vmem,
+        in_specs=[smem, smem] + [vmem] * 6,
+        out_specs=pl.BlockSpec(memory_space=pl.ANY),
+        scratch_shapes=[pltpu.VMEM((4, 2, 96, 512), BF), pltpu.SemaphoreType.DMA((3,))],
         compiler_params=pltpu.CompilerParams(vmem_limit_bytes=48 << 20),
         name="main_products",
-    )(w.reshape(1), holders, early, late, full, near)
+    )(w.reshape(1), holders, early, late, *prep)
 
 
 def cdot(ar, ai, br, bi):
@@ -279,7 +328,8 @@
     near, shift = neighbours[0], shifts[0]
 
     own = gauge[0].reshape(64, 512)
-    early, late = sorted_by_owner(kpoint_index, near, correlations[0])
+    early = sorted_by_owner(kpoint_index, near, correlations[0], 0, EARLY)
+    late = sorted_by_owner(kpoint_index, near, correlations[0], EARLY, 64 - EARLY)
     early = lax.all_to_all(early, "col", 0, 0, tiled=True)
     late = lax.all_to_all(late, "col", 0, 0, tiled=True)
     pair = jnp.stack([own, partner(own, "col", 4)])
@@ -293,7 +343,8 @@
     weights = shell_vector_weights(kpoint_index, near, shift)
     weight = jnp.sum(jnp.where(owners == cindex, weights, 0.0))
 
-    z = main_products(weight, holders, early, late, full, near_full)
+    prep = prepared(holders, early, full, near_full)
+    z = main_products(weight, holders, early, late, prep)
 
     z = within_half(z).astype(F32).sum(0)
     arrived = jnp.concatenate([z[0, :64], z[1]], 0).astype(BF)

time: 209 us -> 209 us (level)
  blocking collectives: 25.5 us -> 0 us
  starting transfers between devices: 59.6 us -> 76.7 us
  waiting for transfers between devices: 106 us -> 112 us
  Pallas kernels: 12.2 us -> 15 us
    all_to_all x1 -> x0, blocking collectives: 25.5 us -> none  [per_device(): early = lax.all_to_all(early, 'col', 0, 0, tiled=True)]
    all_to_all x0 -> x1, waiting for transfers between devices: none -> 18.1 us  [per_device(): early = lax.all_to_all(early, 'col', 0, 0, tiled=True)]
    all_to_all x0 -> x1, starting transfers between devices: none -> 13.1 us  [per_device(): early = lax.all_to_all(early, 'col', 0, 0, tiled=True)]
    ppermute x7, waiting for transfers between devices: 69.1 us -> 56.8 us  [partner(): return lax.ppermute(x, axis, [(i, i ^ bit) for i in range(length)])]
    pallas_call x1 -> x3, Pallas kernels: 3.18 us -> 6.93 us  [the longest x2 5.47 us: sorted_by_owner(): pl.pallas_call(functools.partial(sort_kernel, start=start), out_shape=jax...]
    all_to_all x1, starting transfers between devices: 9.14 us -> 11.7 us  [per_device(): late = lax.all_to_all(late, 'col', 0, 0, tiled=True)]
  transfers between devices with their start and end apart: 12 -> 13, of which waited for: 10 -> 11; matrix products, arithmetic and copies ran while one was open for 1% -> 1% of each run, Pallas kernels for 0% -> 2%
where the time goes in v4:
time: 209 us; the launch traced here: 208 us
  waiting for transfers between devices  112 us (54%)
  starting transfers between devices  76.7 us (37%)
  Pallas kernels  15 us (7%)
  other arithmetic  2.68 us (1%)
    ppermute x7, waiting for transfers between devices, partner(): return lax.ppermute(x, axis, [(i, i ^ bit) for i in range(length)])  56.8 us
    ppermute x7, starting transfers between devices, partner(): return lax.ppermute(x, axis, [(i, i ^ bit) for i in range(length)])  24.1 us
    all_to_all x1, waiting for transfers between devices, within_half(): return lax.all_to_all(x, 'col', 0, 0, tiled=True, axis_index_groups=HALVES)  19.5 us
    all_to_all x1, waiting for transfers between devices, per_device(): early = lax.all_to_all(early, 'col', 0, 0, tiled=True)  18.1 us
    all_to_all x1, starting transfers between devices, per_device(): early = lax.all_to_all(early, 'col', 0, 0, tiled=True)  13.1 us
    ppermute x1, starting transfers between devices, per_device(): near_full = lax.ppermute(full, ('ka', 'col'), fetch_permutation())  12.1 us
    all_to_all x1, starting transfers between devices, per_device(): late = lax.all_to_all(late, 'col', 0, 0, tiled=True)  11.7 us
    ppermute x1, waiting for transfers between devices, per_device(): near_full = lax.ppermute(full, ('ka', 'col'), fetch_permutation())  9.28 us
  transfers between devices with their start and end apart: 13, of which 11 were waited for; matrix products, arithmetic and copies ran while one was open for 1% of the time, Pallas kernels for 2%

profile of v4, /device:TPU:1, one launch (start us, length us, event | category | flops | bytes accessed | tf_op | source)
XLA Modules:
  0.0 208.4 jit_solution(2364232696059965321)
XLA Ops:
  0.6 2.7 %sort_mats.2 = bf16[8,2,32,512]{3,2,1,0:T(8,128)(2,1)} custom-call(s32[1]{0:T(128)} %bitcast.12.k_ref, s32[8]{0:T(128)} %bitcast.131, bf16[8,2,64,512]{3,2,1,0:T(8,128)(2,1)} %bitcast.119), custom_call_target="tpu_custom_call" | custom-call | tf_op jit(solution)/shard_map/sort_mats/pallas_call | solution.py:112
  3.3 13.1 %all-to-all-start = ((bf16[8,2,32,512]{3,2,1,0:T(8,128)(2,1)}), bf16[8,2,32,512]{3,2,1,0:T(8,128)(2,1)S(1)}, u32[]{:S(2)}, u32[]{:S(2)}) async-start(bf16[8,2,32,512]{3,2,1,0:T(8,128)(2,1)} %sort_mats.2), calls=%async_computation | async-start | bytes 1048576 | tf_op jit(solution)/shard_map/all_to_all | solution.py:333
  16.4 2.8 %sort_mats.3 = bf16[8,2,32,512]{3,2,1,0:T(8,128)(2,1)} custom-call(s32[1]{0:T(128)} %bitcast.12.k_ref, s32[8]{0:T(128)} %bitcast.132, bf16[8,2,64,512]{3,2,1,0:T(8,128)(2,1)} %bitcast.120), custom_call_target="tpu_custom_call" | custom-call | tf_op jit(solution)/shard_map/sort_mats/pallas_call | solution.py:112
  19.2 18.1 %all-to-all-done.early_ref = bf16[8,2,32,512]{3,2,1,0:T(8,128)(2,1)S(1)} async-done(((bf16[8,2,32,512]{3,2,1,0:T(8,128)(2,1)}), bf16[8,2,32,512]{3,2,1,0:T(8,128)(2,1)S(1)}, u32[]{:S(2)}, u32[]{:S(2)}) %all-to-all-start) | async-done | bytes 524320 | tf_op jit(solution)/shard_map/all_to_all | solution.py:333
  37.3 11.7 %all-to-all-start.1 = ((bf16[8,2,32,512]{3,2,1,0:T(8,128)(2,1)}), bf16[8,2,32,512]{3,2,1,0:T(8,128)(2,1)S(1)}, u32[]{:S(2)}, u32[]{:S(2)}) async-start(bf16[8,2,32,512]{3,2,1,0:T(8,128)(2,1)} %sort_mats.3), calls=%async_computation.1 | async-start | bytes 1048576 | tf_op jit(solution)/shard_map/all_to_all | solution.py:334
  49.1 7.3 %collective-permute-start = (bf16[64,512]{1,0:T(8,128)(2,1)S(1)}, bf16[64,512]{1,0:T(8,128)(2,1)S(1)}, u32[]{:S(2)}, u32[]{:S(2)}) collective-permute-start(bf16[64,512]{1,0:T(8,128)(2,1)S(1)} %bitcast.130), channel_id=1, source_target_pairs={{0,4},{1,5},{2,6},{3,7},{4,0},{5,1},{6,2},{7,3},{8,12},{9,13},{10,... | collective-permute-start | bytes 196616 | tf_op jit(solution)/shard_map/ppermute | solution.py:314
  56.4 25.6 %collective-permute-done = bf16[64,512]{1,0:T(8,128)(2,1)S(1)} collective-permute-done((bf16[64,512]{1,0:T(8,128)(2,1)S(1)}, bf16[64,512]{1,0:T(8,128)(2,1)S(1)}, u32[]{:S(2)}, u32[]{:S(2)}) %collective-permute-start) | collective-permute-done | bytes 65568 | tf_op jit(solution)/shard_map/ppermute | solution.py:314
  82.0 1.9 collective-permute-start.1
  83.9 6.1 %collective-permute-done.1 = bf16[2,64,512]{2,1,0:T(8,128)(2,1)S(1)} collective-permute-done((bf16[2,64,512]{2,1,0:T(8,128)(2,1)S(1)}, bf16[2,64,512]{2,1,0:T(8,128)(2,1)S(1)}, u32[]{:S(2)}, u32[]{:S(2)}) %collective-permute-start.1) | collective-permute-done | bytes 131104 | tf_op jit(solution)/shard_map/ppermute | solution.py:314
  92.2 5.4 %collective-permute-done.2 = bf16[2,2,64,512]{3,2,1,0:T(8,128)(2,1)S(1)} collective-permute-done((bf16[2,2,64,512]{3,2,1,0:T(8,128)(2,1)S(1)}, bf16[2,2,64,512]{3,2,1,0:T(8,128)(2,1)S(1)}, u32[]{:S(2)}, u32[]{:S(2)}) %collective-permute-start.2) | collective-permute-done | bytes 262176 | tf_op jit(solution)/shard_map/ppermute | solution.py:314
  97.7 12.1 %collective-permute-start.3 = (bf16[8,64,512]{2,1,0:T(8,128)(2,1)S(1)}, bf16[8,64,512]{2,1,0:T(8,128)(2,1)S(1)}, u32[]{:S(2)}, u32[]{:S(2)}) collective-permute-start(bf16[8,64,512]{2,1,0:T(8,128)(2,1)S(1)} %bitcast.117), channel_id=1, source_target_pairs={{130,2},{387,3},{33,1},{103,0},{12,4},{29,5},{174,6},{504,7},{138,... | collective-permute-start | bytes 1572872 | tf_op jit(solution)/shard_map/ppermute | solution.py:338
  110.5 9.3 %collective-permute-done.3.n_ref = bf16[8,64,512]{2,1,0:T(8,128)(2,1)S(1)} collective-permute-done((bf16[8,64,512]{2,1,0:T(8,128)(2,1)S(1)}, bf16[8,64,512]{2,1,0:T(8,128)(2,1)S(1)}, u32[]{:S(2)}, u32[]{:S(2)}) %collective-permute-start.3) | collective-permute-done | bytes 524320 | tf_op jit(solution)/shard_map/ppermute | solution.py:338
  121.3 4.6 %main_products.1 = bf16[4,2,96,512]{3,2,1,0:T(8,128)(2,1)} custom-call(f32[1]{0:T(128)} %bitcast.9.w_ref, s32[2]{0:T(128)S(1)} %pad_add_fusion.1.holder_ref, bf16[8,2,32,512]{3,2,1,0:T(8,128)(2,1)S(1)} %all-to-all-done.early_ref, bf16[8,2,32,512]{3,2,1,0:T(8,128)(2,1)S(1)} %all-to-all-done.1.late_ref, bf16[512,512]{1,0:T(8,128)(2,1)S(1)} %get-tuple-element.7.ut_ref, ...), custom_call_target="tpu_custom_call" | custom-call | tf_op jit(solution)/shard_map/main_products/pallas_call | solution.py:250
  125.9 3.5 %all-to-all-start.2 = ((bf16[4,2,96,512]{3,2,1,0:T(8,128)(2,1)}), bf16[4,2,96,512]{3,2,1,0:T(8,128)(2,1)S(1)}, u32[]{:S(2)}, u32[]{:S(2)}) async-start(bf16[4,2,96,512]{3,2,1,0:T(8,128)(2,1)} %main_products.1), calls=%async_computation.2 | async-start | bytes 1572864 | tf_op jit(solution)/shard_map/all_to_all | solution.py:309
  129.4 19.5 %all-to-all-done.2 = bf16[4,2,96,512]{3,2,1,0:T(8,128)(2,1)S(1)} async-done(((bf16[4,2,96,512]{3,2,1,0:T(8,128)(2,1)}), bf16[4,2,96,512]{3,2,1,0:T(8,128)(2,1)S(1)}, u32[]{:S(2)}, u32[]{:S(2)}) %all-to-all-start.2) | async-done | bytes 786464 | tf_op jit(solution)/shard_map/all_to_all | solution.py:309
  149.7 5.3 %all-to-all-start.3 = ((f32[32,1,256]{2,1,0:T(1,128)}), f32[32,1,256]{2,1,0:T(1,128)S(1)}, u32[]{:S(2)}, u32[]{:S(2)}) async-start(f32[32,1,256]{2,1,0:T(1,128)} %broadcast_in_dim.54), calls=%async_computation.3 | async-start | bytes 65536 | tf_op jit(solution)/shard_map/all_to_all | solution.py:359
  155.0 7.2 %all-to-all-done.3 = f32[32,1,256]{2,1,0:T(1,128)S(1)} async-done(((f32[32,1,256]{2,1,0:T(1,128)}), f32[32,1,256]{2,1,0:T(1,128)S(1)}, u32[]{:S(2)}, u32[]{:S(2)}) %all-to-all-start.3) | async-done | bytes 32800 | tf_op jit(solution)/shard_map/all_to_all | solution.py:359
  162.3 6.1 %collective-permute-start.7 = (f32[8,256]{1,0:T(8,128)S(1)}, f32[8,256]{1,0:T(8,128)S(1)}, u32[]{:S(2)}, u32[]{:S(2)}) collective-permute-start(f32[8,256]{1,0:T(8,128)S(1)} %broadcast_in_dim.55), channel_id=1, source_target_pairs={{0,4},{1,5},{2,6},{3,7},{4,0},{5,1},{6,2},{7,3},{8,12},{9,13},{10,... | collective-permute-start | bytes 24584 | tf_op jit(solution)/shard_map/ppermute | solution.py:314
  168.4 3.1 %collective-permute-start.4 = (bf16[160,512]{1,0:T(8,128)(2,1)S(1)}, bf16[160,512]{1,0:T(8,128)(2,1)S(1)}, u32[]{:S(2)}, u32[]{:S(2)}) collective-permute-start(bf16[160,512]{1,0:T(8,128)(2,1)S(1)} %pad_maximum_fusion.4), channel_id=1, source_target_pairs={{0,4},{1,5},{2,6},{3,7},{4,0},{5,1},{6,2},{7,3},{8,12},{9,13},{10,... | collective-permute-start | bytes 491528 | tf_op jit(solution)/shard_map/ppermute | solution.py:314
  171.5 6.9 %collective-permute-start.8 = (f32[8,256]{1,0:T(8,128)S(1)}, f32[8,256]{1,0:T(8,128)S(1)}, u32[]{:S(2)}, u32[]{:S(2)}) collective-permute-start(f32[8,256]{1,0:T(8,128)S(1)} %broadcast_add_fusion), channel_id=1, source_target_pairs={{0,68},{1,69},{2,70},{3,71},{4,64},{5,65},{6,66},{7,67},{8,76},{9,... | collective-permute-start | bytes 24584 | tf_op jit(solution)/shard_map/ppermute | solution.py:362
  180.4 8.6 %collective-permute-done.4 = bf16[160,512]{1,0:T(8,128)(2,1)S(1)} collective-permute-done((bf16[160,512]{1,0:T(8,128)(2,1)S(1)}, bf16[160,512]{1,0:T(8,128)(2,1)S(1)}, u32[]{:S(2)}, u32[]{:S(2)}) %collective-permute-start.4) | collective-permute-done | bytes 163872 | tf_op jit(solution)/shard_map/ppermute | solution.py:314
  191.2 5.3 %collective-permute-done.5 = bf16[128,512]{1,0:T(8,128)(2,1)S(1)} collective-permute-done((bf16[128,512]{1,0:T(8,128)(2,1)S(1)}, bf16[128,512]{1,0:T(8,128)(2,1)S(1)}, u32[]{:S(2)}, u32[]{:S(2)}) %collective-permute-start.5) | collective-permute-done | bytes 131104 | tf_op jit(solution)/shard_map/ppermute | solution.py:314
  199.1 5.8 %collective-permute-done.6 = bf16[256,512]{1,0:T(8,128)(2,1)S(1)} collective-permute-done((bf16[256,512]{1,0:T(8,128)(2,1)S(1)}, bf16[256,512]{1,0:T(8,128)(2,1)S(1)}, u32[]{:S(2)}, u32[]{:S(2)}) %collective-permute-start.6) | collective-permute-done | bytes 262176 | tf_op jit(solution)/shard_map/ppermute | solution.py:314
  204.9 3.5 %orthonormalize.1 = f32[64,2,256]{2,1,0:T(2,128)} custom-call(bf16[512,512]{1,0:T(8,128)(2,1)S(1)} %pad_maximum_fusion.1.x_ref, f32[64,512]{1,0:T(8,128)S(1)} %slice_bitcast_fusion.own_ref), custom_call_target="tpu_custom_call" | custom-call | tf_op jit(solution)/shard_map/orthonormalize/pallas_call | solution.py:298
  (47 shorter events, 12.0 us)
Async XLA Ops:
  3.3 34.0 %all-to-all-start = ((bf16[8,2,32,512]{3,2,1,0:T(8,128)(2,1)}), bf16[8,2,32,512]{3,2,1,0:T(8,128)(2,1)S(1)}, u32[]{:S(2)}, u32[]{:S(2)}) async-start(bf16[8,2,32,512]{3,2,1,0:T(8,128)(2,1)} %sort_mats.2), calls=%async_computation | async-start | bytes 1048576 | tf_op jit(solution)/shard_map/all_to_all | solution.py:333
  16.4 32.7 %copy-start = (bf16[1,64,2,256]{3,2,1,0:T(2,128)(2,1)S(1)}, bf16[1,64,2,256]{3,2,1,0:T(2,128)(2,1)}, u32[]{:S(2)}) copy-start(bf16[1,64,2,256]{3,2,1,0:T(2,128)(2,1)} %param.6) | copy-start | bytes 196612
  19.2 72.8 %copy-start.2 = (s32[1,8,3]{1,0,2:T(1,128)S(1)}, s32[1,8,3]{1,0,2:T(1,128)}, u32[]{:S(2)}) copy-start(s32[1,8,3]{1,0,2:T(1,128)} %param.8) | copy-start | bytes 292
  37.3 83.9 %all-to-all-start.1 = ((bf16[8,2,32,512]{3,2,1,0:T(8,128)(2,1)}), bf16[8,2,32,512]{3,2,1,0:T(8,128)(2,1)S(1)}, u32[]{:S(2)}, u32[]{:S(2)}) async-start(bf16[8,2,32,512]{3,2,1,0:T(8,128)(2,1)} %sort_mats.3), calls=%async_computation.1 | async-start | bytes 1048576 | tf_op jit(solution)/shard_map/all_to_all | solution.py:334
  49.1 32.9 %collective-permute-start = (bf16[64,512]{1,0:T(8,128)(2,1)S(1)}, bf16[64,512]{1,0:T(8,128)(2,1)S(1)}, u32[]{:S(2)}, u32[]{:S(2)}) collective-permute-start(bf16[64,512]{1,0:T(8,128)(2,1)S(1)} %bitcast.130), channel_id=1, source_target_pairs={{0,4},{1,5},{2,6},{3,7},{4,0},{5,1},{6,2},{7,3},{8,12},{9,13},{10,... | collective-permute-start | bytes 196616 | tf_op jit(solution)/shard_map/ppermute | solution.py:314
  82.0 27.8 %copy-start.1 = (s32[1,8]{1,0:T(1,128)S(1)}, s32[1,8]{1,0:T(1,128)}, u32[]{:S(2)}) copy-start(s32[1,8]{1,0:T(1,128)} %param.7) | copy-start | bytes 100
  82.0 8.0 %collective-permute-start.1 = (bf16[2,64,512]{2,1,0:T(8,128)(2,1)S(1)}, bf16[2,64,512]{2,1,0:T(8,128)(2,1)S(1)}, u32[]{:S(2)}, u32[]{:S(2)}) collective-permute-start(bf16[2,64,512]{2,1,0:T(8,128)(2,1)S(1)} %get-tuple-element.18), channel_id=1, source_target_pairs={{0,2},{1,3},{2,0},{3,1},{4,6},{5,7},{6,4},{7,5},{8,10},{9,11},{10,... | collective-permute-start | bytes 393224 | tf_op jit(solution)/shard_map/ppermute | solution.py:314
  90.1 7.6 %collective-permute-start.2 = (bf16[2,2,64,512]{3,2,1,0:T(8,128)(2,1)S(1)}, bf16[2,2,64,512]{3,2,1,0:T(8,128)(2,1)S(1)}, u32[]{:S(2)}, u32[]{:S(2)}) collective-permute-start(bf16[2,2,64,512]{3,2,1,0:T(8,128)(2,1)S(1)} %get-tuple-element.16), channel_id=1, source_target_pairs={{0,1},{1,0},{2,3},{3,2},{4,5},{5,4},{6,7},{7,6},{8,9},{9,8},{10,11... | collective-permute-start | bytes 786440 | tf_op jit(solution)/shard_map/ppermute | solution.py:314
  97.7 22.1 %collective-permute-start.3 = (bf16[8,64,512]{2,1,0:T(8,128)(2,1)S(1)}, bf16[8,64,512]{2,1,0:T(8,128)(2,1)S(1)}, u32[]{:S(2)}, u32[]{:S(2)}) collective-permute-start(bf16[8,64,512]{2,1,0:T(8,128)(2,1)S(1)} %bitcast.117), channel_id=1, source_target_pairs={{130,2},{387,3},{33,1},{103,0},{12,4},{29,5},{174,6},{504,7},{138,... | collective-permute-start | bytes 1572872 | tf_op jit(solution)/shard_map/ppermute | solution.py:338
  125.9 23.0 %all-to-all-start.2 = ((bf16[4,2,96,512]{3,2,1,0:T(8,128)(2,1)}), bf16[4,2,96,512]{3,2,1,0:T(8,128)(2,1)S(1)}, u32[]{:S(2)}, u32[]{:S(2)}) async-start(bf16[4,2,96,512]{3,2,1,0:T(8,128)(2,1)} %main_products.1), calls=%async_computation.2 | async-start | bytes 1572864 | tf_op jit(solution)/shard_map/all_to_all | solution.py:309
  149.7 12.5 %all-to-all-start.3 = ((f32[32,1,256]{2,1,0:T(1,128)}), f32[32,1,256]{2,1,0:T(1,128)S(1)}, u32[]{:S(2)}, u32[]{:S(2)}) async-start(f32[32,1,256]{2,1,0:T(1,128)} %broadcast_in_dim.54), calls=%async_computation.3 | async-start | bytes 65536 | tf_op jit(solution)/shard_map/all_to_all | solution.py:359
  162.3 9.2 %collective-permute-start.7 = (f32[8,256]{1,0:T(8,128)S(1)}, f32[8,256]{1,0:T(8,128)S(1)}, u32[]{:S(2)}, u32[]{:S(2)}) collective-permute-start(f32[8,256]{1,0:T(8,128)S(1)} %broadcast_in_dim.55), channel_id=1, source_target_pairs={{0,4},{1,5},{2,6},{3,7},{4,0},{5,1},{6,2},{7,3},{8,12},{9,13},{10,... | collective-permute-start | bytes 24584 | tf_op jit(solution)/shard_map/ppermute | solution.py:314
  168.4 20.7 %collective-permute-start.4 = (bf16[160,512]{1,0:T(8,128)(2,1)S(1)}, bf16[160,512]{1,0:T(8,128)(2,1)S(1)}, u32[]{:S(2)}, u32[]{:S(2)}) collective-permute-start(bf16[160,512]{1,0:T(8,128)(2,1)S(1)} %pad_maximum_fusion.4), channel_id=1, source_target_pairs={{0,4},{1,5},{2,6},{3,7},{4,0},{5,1},{6,2},{7,3},{8,12},{9,13},{10,... | collective-permute-start | bytes 491528 | tf_op jit(solution)/shard_map/ppermute | solution.py:314
  171.5 8.3 %collective-permute-start.8 = (f32[8,256]{1,0:T(8,128)S(1)}, f32[8,256]{1,0:T(8,128)S(1)}, u32[]{:S(2)}, u32[]{:S(2)}) collective-permute-start(f32[8,256]{1,0:T(8,128)S(1)} %broadcast_add_fusion), channel_id=1, source_target_pairs={{0,68},{1,69},{2,70},{3,71},{4,64},{5,65},{6,66},{7,67},{8,76},{9,... | collective-permute-start | bytes 24584 | tf_op jit(solution)/shard_map/ppermute | solution.py:362
  189.2 7.3 %collective-permute-start.5 = (bf16[128,512]{1,0:T(8,128)(2,1)S(1)}, bf16[128,512]{1,0:T(8,128)(2,1)S(1)}, u32[]{:S(2)}, u32[]{:S(2)}) collective-permute-start(bf16[128,512]{1,0:T(8,128)(2,1)S(1)} %bitcast.121), channel_id=1, source_target_pairs={{0,2},{1,3},{2,0},{3,1},{4,6},{5,7},{6,4},{7,5},{8,10},{9,11},{10,... | collective-permute-start | bytes 393224 | tf_op jit(solution)/shard_map/ppermute | solution.py:314
  196.5 8.3 %collective-permute-start.6 = (bf16[256,512]{1,0:T(8,128)(2,1)S(1)}, bf16[256,512]{1,0:T(8,128)(2,1)S(1)}, u32[]{:S(2)}, u32[]{:S(2)}) collective-permute-start(bf16[256,512]{1,0:T(8,128)(2,1)S(1)} %pad_maximum_fusion.3), channel_id=1, source_target_pairs={{0,1},{1,0},{2,3},{3,2},{4,5},{5,4},{6,7},{7,6},{8,9},{9,8},{10,11... | collective-permute-start | bytes 786440 | tf_op jit(solution)/shard_map/ppermute | solution.py:314

commit v5 on v4

--- a/solution.py
+++ b/solution.py
@@ -279,18 +279,17 @@
     scale = jnp.sqrt(square)
     d_r = 0.5 * (eye - square * s_r)
     d_i = -0.5 * (square * s_i)
-    p_r, p_i = d_r, d_i
-    for _ in range(2):
-        q_r, q_i = cdot(d_r, d_i, d_r, d_i)
-        c_r, c_i = cdot(q_r, q_i, d_r, d_i)
-        d_r, d_i = 1.5 * q_r + c_r, 1.5 * q_i + c_i
-        e_r, e_i = cdot(p_r, p_i, d_r, d_i)
-        p_r, p_i = p_r + d_r + e_r, p_i + d_i + e_i
     own = own_ref[...]
-    o_r, o_i = own[:, :256], own[:, 256:]
-    e_r, e_i = cdot(o_r, o_i, p_r, p_i)
-    out_ref[:, 0] = scale * (o_r + e_r)
-    out_ref[:, 1] = scale * (o_i + e_i)
+    y_r, y_i = own[:, :256], own[:, 256:]
+    for turn in range(3):
+        if turn:
+            q_r, q_i = cdot(d_r, d_i, d_r, d_i)
+            c_r, c_i = cdot(q_r, q_i, d_r, d_i)
+            d_r, d_i = 1.5 * q_r + c_r, 1.5 * q_i + c_i
+        e_r, e_i = cdot(y_r, y_i, d_r, d_i)
+        y_r, y_i = y_r + e_r, y_i + e_i
+    out_ref[:, 0] = scale * y_r
+    out_ref[:, 1] = scale * y_i
 
 
 def orthonormalized(full, own):
@@ -327,7 +326,7 @@
     cindex = lax.axis_index("col")
     near, shift = neighbours[0], shifts[0]
 
-    own = gauge[0].reshape(64, 512)
+    own = lax.optimization_barrier(gauge[0].reshape(64, 512))
     early = sorted_by_owner(kpoint_index, near, correlations[0], 0, EARLY)
     late = sorted_by_owner(kpoint_index, near, correlations[0], EARLY, 64 - EARLY)
     early = lax.all_to_all(early, "col", 0, 0, tiled=True)

time: 209 us -> 209 us (level)
  no operation moved by 1% of the time
where the time goes in v5:
time: 209 us; the launch traced here: 208 us
  waiting for transfers between devices  112 us (54%)
  starting transfers between devices  76.7 us (37%)
  Pallas kernels  14.8 us (7%)
  other arithmetic  2.68 us (1%)
    ppermute x7, waiting for transfers between devices, partner(): return lax.ppermute(x, axis, [(i, i ^ bit) for i in range(length)])  56.8 us
    ppermute x7, starting transfers between devices, partner(): return lax.ppermute(x, axis, [(i, i ^ bit) for i in range(length)])  24.1 us
    all_to_all x1, waiting for transfers between devices, within_half(): return lax.all_to_all(x, 'col', 0, 0, tiled=True, axis_index_groups=HALVES)  19.5 us
    all_to_all x1, waiting for transfers between devices, per_device(): early = lax.all_to_all(early, 'col', 0, 0, tiled=True)  18.1 us
    all_to_all x1, starting transfers between devices, per_device(): early = lax.all_to_all(early, 'col', 0, 0, tiled=True)  13.1 us
    ppermute x1, starting transfers between devices, per_device(): near_full = lax.ppermute(full, ('ka', 'col'), fetch_permutation())  12.1 us
    all_to_all x1, starting transfers between devices, per_device(): late = lax.all_to_all(late, 'col', 0, 0, tiled=True)  11.7 us
    ppermute x1, waiting for transfers between devices, per_device(): near_full = lax.ppermute(full, ('ka', 'col'), fetch_permutation())  9.28 us
  transfers between devices with their start and end apart: 13, of which 11 were waited for; matrix products, arithmetic and copies ran while one was open for 1% of the time, Pallas kernels for 2%

profile of v5, /device:TPU:1, one launch (start us, length us, event | category | flops | bytes accessed | tf_op | source)
XLA Modules:
  0.0 208.2 jit_solution(15673428559574957725)
XLA Ops:
  0.6 2.7 %sort_mats.2 = bf16[8,2,32,512]{3,2,1,0:T(8,128)(2,1)} custom-call(s32[1]{0:T(128)} %bitcast.13.k_ref, s32[8]{0:T(128)} %bitcast.134, bf16[8,2,64,512]{3,2,1,0:T(8,128)(2,1)} %bitcast.120), custom_call_target="tpu_custom_call" | custom-call | tf_op jit(solution)/shard_map/sort_mats/pallas_call | solution.py:112
  3.3 13.1 %all-to-all-start = ((bf16[8,2,32,512]{3,2,1,0:T(8,128)(2,1)}), bf16[8,2,32,512]{3,2,1,0:T(8,128)(2,1)S(1)}, u32[]{:S(2)}, u32[]{:S(2)}) async-start(bf16[8,2,32,512]{3,2,1,0:T(8,128)(2,1)} %sort_mats.2), calls=%async_computation | async-start | bytes 1048576 | tf_op jit(solution)/shard_map/all_to_all | solution.py:332
  16.4 2.8 %sort_mats.3 = bf16[8,2,32,512]{3,2,1,0:T(8,128)(2,1)} custom-call(s32[1]{0:T(128)} %bitcast.13.k_ref, s32[8]{0:T(128)} %bitcast.135, bf16[8,2,64,512]{3,2,1,0:T(8,128)(2,1)} %bitcast.121), custom_call_target="tpu_custom_call" | custom-call | tf_op jit(solution)/shard_map/sort_mats/pallas_call | solution.py:112
  19.2 18.1 %all-to-all-done.early_ref = bf16[8,2,32,512]{3,2,1,0:T(8,128)(2,1)S(1)} async-done(((bf16[8,2,32,512]{3,2,1,0:T(8,128)(2,1)}), bf16[8,2,32,512]{3,2,1,0:T(8,128)(2,1)S(1)}, u32[]{:S(2)}, u32[]{:S(2)}) %all-to-all-start) | async-done | bytes 524320 | tf_op jit(solution)/shard_map/all_to_all | solution.py:332
  37.3 11.7 %all-to-all-start.1 = ((bf16[8,2,32,512]{3,2,1,0:T(8,128)(2,1)}), bf16[8,2,32,512]{3,2,1,0:T(8,128)(2,1)S(1)}, u32[]{:S(2)}, u32[]{:S(2)}) async-start(bf16[8,2,32,512]{3,2,1,0:T(8,128)(2,1)} %sort_mats.3), calls=%async_computation.1 | async-start | bytes 1048576 | tf_op jit(solution)/shard_map/all_to_all | solution.py:333
  49.1 7.3 %collective-permute-start = (bf16[64,512]{1,0:T(8,128)(2,1)S(1)}, bf16[64,512]{1,0:T(8,128)(2,1)S(1)}, u32[]{:S(2)}, u32[]{:S(2)}) collective-permute-start(bf16[64,512]{1,0:T(8,128)(2,1)S(1)} %bitcast.125), channel_id=1, source_target_pairs={{0,4},{1,5},{2,6},{3,7},{4,0},{5,1},{6,2},{7,3},{8,12},{9,13},{10,... | collective-permute-start | bytes 196616 | tf_op jit(solution)/shard_map/ppermute | solution.py:313
  56.4 25.6 %collective-permute-done = bf16[64,512]{1,0:T(8,128)(2,1)S(1)} collective-permute-done((bf16[64,512]{1,0:T(8,128)(2,1)S(1)}, bf16[64,512]{1,0:T(8,128)(2,1)S(1)}, u32[]{:S(2)}, u32[]{:S(2)}) %collective-permute-start) | collective-permute-done | bytes 65568 | tf_op jit(solution)/shard_map/ppermute | solution.py:313
  82.0 1.9 collective-permute-start.1
  83.9 6.1 %collective-permute-done.1 = bf16[2,64,512]{2,1,0:T(8,128)(2,1)S(1)} collective-permute-done((bf16[2,64,512]{2,1,0:T(8,128)(2,1)S(1)}, bf16[2,64,512]{2,1,0:T(8,128)(2,1)S(1)}, u32[]{:S(2)}, u32[]{:S(2)}) %collective-permute-start.1) | collective-permute-done | bytes 131104 | tf_op jit(solution)/shard_map/ppermute | solution.py:313
  92.2 5.4 %collective-permute-done.2 = bf16[2,2,64,512]{3,2,1,0:T(8,128)(2,1)S(1)} collective-permute-done((bf16[2,2,64,512]{3,2,1,0:T(8,128)(2,1)S(1)}, bf16[2,2,64,512]{3,2,1,0:T(8,128)(2,1)S(1)}, u32[]{:S(2)}, u32[]{:S(2)}) %collective-permute-start.2) | collective-permute-done | bytes 262176 | tf_op jit(solution)/shard_map/ppermute | solution.py:313
  97.7 12.1 %collective-permute-start.3 = (bf16[8,64,512]{2,1,0:T(8,128)(2,1)S(1)}, bf16[8,64,512]{2,1,0:T(8,128)(2,1)S(1)}, u32[]{:S(2)}, u32[]{:S(2)}) collective-permute-start(bf16[8,64,512]{2,1,0:T(8,128)(2,1)S(1)} %bitcast.118), channel_id=1, source_target_pairs={{130,2},{387,3},{33,1},{103,0},{12,4},{29,5},{174,6},{504,7},{138,... | collective-permute-start | bytes 1572872 | tf_op jit(solution)/shard_map/ppermute | solution.py:337
  110.5 9.3 %collective-permute-done.3.n_ref = bf16[8,64,512]{2,1,0:T(8,128)(2,1)S(1)} collective-permute-done((bf16[8,64,512]{2,1,0:T(8,128)(2,1)S(1)}, bf16[8,64,512]{2,1,0:T(8,128)(2,1)S(1)}, u32[]{:S(2)}, u32[]{:S(2)}) %collective-permute-start.3) | collective-permute-done | bytes 524320 | tf_op jit(solution)/shard_map/ppermute | solution.py:337
  121.3 4.6 %main_products.1 = bf16[4,2,96,512]{3,2,1,0:T(8,128)(2,1)} custom-call(f32[1]{0:T(128)} %bitcast.10.w_ref, s32[2]{0:T(128)S(1)} %pad_add_fusion.1.holder_ref, bf16[8,2,32,512]{3,2,1,0:T(8,128)(2,1)S(1)} %all-to-all-done.early_ref, bf16[8,2,32,512]{3,2,1,0:T(8,128)(2,1)S(1)} %all-to-all-done.1.late_ref, bf16[512,512]{1,0:T(8,128)(2,1)S(1)} %get-tuple-element.7.ut_ref, ...), custom_call_target="tpu_custom_call" | custom-call | tf_op jit(solution)/shard_map/main_products/pallas_call | solution.py:250
  125.9 3.5 %all-to-all-start.2 = ((bf16[4,2,96,512]{3,2,1,0:T(8,128)(2,1)}), bf16[4,2,96,512]{3,2,1,0:T(8,128)(2,1)S(1)}, u32[]{:S(2)}, u32[]{:S(2)}) async-start(bf16[4,2,96,512]{3,2,1,0:T(8,128)(2,1)} %main_products.1), calls=%async_computation.2 | async-start | bytes 1572864 | tf_op jit(solution)/shard_map/all_to_all | solution.py:308
  129.4 19.5 %all-to-all-done.2 = bf16[4,2,96,512]{3,2,1,0:T(8,128)(2,1)S(1)} async-done(((bf16[4,2,96,512]{3,2,1,0:T(8,128)(2,1)}), bf16[4,2,96,512]{3,2,1,0:T(8,128)(2,1)S(1)}, u32[]{:S(2)}, u32[]{:S(2)}) %all-to-all-start.2) | async-done | bytes 786464 | tf_op jit(solution)/shard_map/all_to_all | solution.py:308
  149.7 5.3 %all-to-all-start.3 = ((f32[32,1,256]{2,1,0:T(1,128)}), f32[32,1,256]{2,1,0:T(1,128)S(1)}, u32[]{:S(2)}, u32[]{:S(2)}) async-start(f32[32,1,256]{2,1,0:T(1,128)} %broadcast_in_dim.54), calls=%async_computation.3 | async-start | bytes 65536 | tf_op jit(solution)/shard_map/all_to_all | solution.py:358
  155.0 7.2 %all-to-all-done.3 = f32[32,1,256]{2,1,0:T(1,128)S(1)} async-done(((f32[32,1,256]{2,1,0:T(1,128)}), f32[32,1,256]{2,1,0:T(1,128)S(1)}, u32[]{:S(2)}, u32[]{:S(2)}) %all-to-all-start.3) | async-done | bytes 32800 | tf_op jit(solution)/shard_map/all_to_all | solution.py:358
  162.3 6.1 %collective-permute-start.7 = (f32[8,256]{1,0:T(8,128)S(1)}, f32[8,256]{1,0:T(8,128)S(1)}, u32[]{:S(2)}, u32[]{:S(2)}) collective-permute-start(f32[8,256]{1,0:T(8,128)S(1)} %broadcast_in_dim.55), channel_id=1, source_target_pairs={{0,4},{1,5},{2,6},{3,7},{4,0},{5,1},{6,2},{7,3},{8,12},{9,13},{10,... | collective-permute-start | bytes 24584 | tf_op jit(solution)/shard_map/ppermute | solution.py:313
  168.4 3.1 %collective-permute-start.4 = (bf16[160,512]{1,0:T(8,128)(2,1)S(1)}, bf16[160,512]{1,0:T(8,128)(2,1)S(1)}, u32[]{:S(2)}, u32[]{:S(2)}) collective-permute-start(bf16[160,512]{1,0:T(8,128)(2,1)S(1)} %pad_maximum_fusion.4), channel_id=1, source_target_pairs={{0,4},{1,5},{2,6},{3,7},{4,0},{5,1},{6,2},{7,3},{8,12},{9,13},{10,... | collective-permute-start | bytes 491528 | tf_op jit(solution)/shard_map/ppermute | solution.py:313
  171.5 6.9 %collective-permute-start.8 = (f32[8,256]{1,0:T(8,128)S(1)}, f32[8,256]{1,0:T(8,128)S(1)}, u32[]{:S(2)}, u32[]{:S(2)}) collective-permute-start(f32[8,256]{1,0:T(8,128)S(1)} %broadcast_add_fusion), channel_id=1, source_target_pairs={{0,68},{1,69},{2,70},{3,71},{4,64},{5,65},{6,66},{7,67},{8,76},{9,... | collective-permute-start | bytes 24584 | tf_op jit(solution)/shard_map/ppermute | solution.py:361
  180.4 8.6 %collective-permute-done.4 = bf16[160,512]{1,0:T(8,128)(2,1)S(1)} collective-permute-done((bf16[160,512]{1,0:T(8,128)(2,1)S(1)}, bf16[160,512]{1,0:T(8,128)(2,1)S(1)}, u32[]{:S(2)}, u32[]{:S(2)}) %collective-permute-start.4) | collective-permute-done | bytes 163872 | tf_op jit(solution)/shard_map/ppermute | solution.py:313
  191.2 5.3 %collective-permute-done.5 = bf16[128,512]{1,0:T(8,128)(2,1)S(1)} collective-permute-done((bf16[128,512]{1,0:T(8,128)(2,1)S(1)}, bf16[128,512]{1,0:T(8,128)(2,1)S(1)}, u32[]{:S(2)}, u32[]{:S(2)}) %collective-permute-start.5) | collective-permute-done | bytes 131104 | tf_op jit(solution)/shard_map/ppermute | solution.py:313
  199.1 5.8 %collective-permute-done.6 = bf16[256,512]{1,0:T(8,128)(2,1)S(1)} collective-permute-done((bf16[256,512]{1,0:T(8,128)(2,1)S(1)}, bf16[256,512]{1,0:T(8,128)(2,1)S(1)}, u32[]{:S(2)}, u32[]{:S(2)}) %collective-permute-start.6) | collective-permute-done | bytes 262176 | tf_op jit(solution)/shard_map/ppermute | solution.py:313
  204.9 3.3 %orthonormalize.1 = f32[64,2,256]{2,1,0:T(2,128)} custom-call(bf16[512,512]{1,0:T(8,128)(2,1)S(1)} %pad_maximum_fusion.1.x_ref, f32[64,512]{1,0:T(8,128)S(1)} %slice_bitcast_fusion.own_ref), custom_call_target="tpu_custom_call" | custom-call | tf_op jit(solution)/shard_map/orthonormalize/pallas_call | solution.py:297
  (46 shorter events, 12.0 us)
Async XLA Ops:
  3.3 34.0 %all-to-all-start = ((bf16[8,2,32,512]{3,2,1,0:T(8,128)(2,1)}), bf16[8,2,32,512]{3,2,1,0:T(8,128)(2,1)S(1)}, u32[]{:S(2)}, u32[]{:S(2)}) async-start(bf16[8,2,32,512]{3,2,1,0:T(8,128)(2,1)} %sort_mats.2), calls=%async_computation | async-start | bytes 1048576 | tf_op jit(solution)/shard_map/all_to_all | solution.py:332
  16.4 32.7 %copy-start = (bf16[1,64,2,256]{3,2,1,0:T(2,128)(2,1)S(1)}, bf16[1,64,2,256]{3,2,1,0:T(2,128)(2,1)}, u32[]{:S(2)}) copy-start(bf16[1,64,2,256]{3,2,1,0:T(2,128)(2,1)} %param.6) | copy-start | bytes 196612
  19.2 72.8 %copy-start.2 = (s32[1,8,3]{1,0,2:T(1,128)S(1)}, s32[1,8,3]{1,0,2:T(1,128)}, u32[]{:S(2)}) copy-start(s32[1,8,3]{1,0,2:T(1,128)} %param.8) | copy-start | bytes 292
  37.3 83.9 %all-to-all-start.1 = ((bf16[8,2,32,512]{3,2,1,0:T(8,128)(2,1)}), bf16[8,2,32,512]{3,2,1,0:T(8,128)(2,1)S(1)}, u32[]{:S(2)}, u32[]{:S(2)}) async-start(bf16[8,2,32,512]{3,2,1,0:T(8,128)(2,1)} %sort_mats.3), calls=%async_computation.1 | async-start | bytes 1048576 | tf_op jit(solution)/shard_map/all_to_all | solution.py:333
  49.1 32.9 %collective-permute-start = (bf16[64,512]{1,0:T(8,128)(2,1)S(1)}, bf16[64,512]{1,0:T(8,128)(2,1)S(1)}, u32[]{:S(2)}, u32[]{:S(2)}) collective-permute-start(bf16[64,512]{1,0:T(8,128)(2,1)S(1)} %bitcast.125), channel_id=1, source_target_pairs={{0,4},{1,5},{2,6},{3,7},{4,0},{5,1},{6,2},{7,3},{8,12},{9,13},{10,... | collective-permute-start | bytes 196616 | tf_op jit(solution)/shard_map/ppermute | solution.py:313
  82.0 27.8 %copy-start.1 = (s32[1,8]{1,0:T(1,128)S(1)}, s32[1,8]{1,0:T(1,128)}, u32[]{:S(2)}) copy-start(s32[1,8]{1,0:T(1,128)} %param.7) | copy-start | bytes 100
  82.0 8.0 %collective-permute-start.1 = (bf16[2,64,512]{2,1,0:T(8,128)(2,1)S(1)}, bf16[2,64,512]{2,1,0:T(8,128)(2,1)S(1)}, u32[]{:S(2)}, u32[]{:S(2)}) collective-permute-start(bf16[2,64,512]{2,1,0:T(8,128)(2,1)S(1)} %get-tuple-element.18), channel_id=1, source_target_pairs={{0,2},{1,3},{2,0},{3,1},{4,6},{5,7},{6,4},{7,5},{8,10},{9,11},{10,... | collective-permute-start | bytes 393224 | tf_op jit(solution)/shard_map/ppermute | solution.py:313
  90.1 7.6 %collective-permute-start.2 = (bf16[2,2,64,512]{3,2,1,0:T(8,128)(2,1)S(1)}, bf16[2,2,64,512]{3,2,1,0:T(8,128)(2,1)S(1)}, u32[]{:S(2)}, u32[]{:S(2)}) collective-permute-start(bf16[2,2,64,512]{3,2,1,0:T(8,128)(2,1)S(1)} %get-tuple-element.16), channel_id=1, source_target_pairs={{0,1},{1,0},{2,3},{3,2},{4,5},{5,4},{6,7},{7,6},{8,9},{9,8},{10,11... | collective-permute-start | bytes 786440 | tf_op jit(solution)/shard_map/ppermute | solution.py:313
  97.7 22.1 %collective-permute-start.3 = (bf16[8,64,512]{2,1,0:T(8,128)(2,1)S(1)}, bf16[8,64,512]{2,1,0:T(8,128)(2,1)S(1)}, u32[]{:S(2)}, u32[]{:S(2)}) collective-permute-start(bf16[8,64,512]{2,1,0:T(8,128)(2,1)S(1)} %bitcast.118), channel_id=1, source_target_pairs={{130,2},{387,3},{33,1},{103,0},{12,4},{29,5},{174,6},{504,7},{138,... | collective-permute-start | bytes 1572872 | tf_op jit(solution)/shard_map/ppermute | solution.py:337
  125.9 23.0 %all-to-all-start.2 = ((bf16[4,2,96,512]{3,2,1,0:T(8,128)(2,1)}), bf16[4,2,96,512]{3,2,1,0:T(8,128)(2,1)S(1)}, u32[]{:S(2)}, u32[]{:S(2)}) async-start(bf16[4,2,96,512]{3,2,1,0:T(8,128)(2,1)} %main_products.1), calls=%async_computation.2 | async-start | bytes 1572864 | tf_op jit(solution)/shard_map/all_to_all | solution.py:308
  149.7 12.5 %all-to-all-start.3 = ((f32[32,1,256]{2,1,0:T(1,128)}), f32[32,1,256]{2,1,0:T(1,128)S(1)}, u32[]{:S(2)}, u32[]{:S(2)}) async-start(f32[32,1,256]{2,1,0:T(1,128)} %broadcast_in_dim.54), calls=%async_computation.3 | async-start | bytes 65536 | tf_op jit(solution)/shard_map/all_to_all | solution.py:358
  162.3 9.2 %collective-permute-start.7 = (f32[8,256]{1,0:T(8,128)S(1)}, f32[8,256]{1,0:T(8,128)S(1)}, u32[]{:S(2)}, u32[]{:S(2)}) collective-permute-start(f32[8,256]{1,0:T(8,128)S(1)} %broadcast_in_dim.55), channel_id=1, source_target_pairs={{0,4},{1,5},{2,6},{3,7},{4,0},{5,1},{6,2},{7,3},{8,12},{9,13},{10,... | collective-permute-start | bytes 24584 | tf_op jit(solution)/shard_map/ppermute | solution.py:313
  168.4 20.7 %collective-permute-start.4 = (bf16[160,512]{1,0:T(8,128)(2,1)S(1)}, bf16[160,512]{1,0:T(8,128)(2,1)S(1)}, u32[]{:S(2)}, u32[]{:S(2)}) collective-permute-start(bf16[160,512]{1,0:T(8,128)(2,1)S(1)} %pad_maximum_fusion.4), channel_id=1, source_target_pairs={{0,4},{1,5},{2,6},{3,7},{4,0},{5,1},{6,2},{7,3},{8,12},{9,13},{10,... | collective-permute-start | bytes 491528 | tf_op jit(solution)/shard_map/ppermute | solution.py:313
  171.5 8.3 %collective-permute-start.8 = (f32[8,256]{1,0:T(8,128)S(1)}, f32[8,256]{1,0:T(8,128)S(1)}, u32[]{:S(2)}, u32[]{:S(2)}) collective-permute-start(f32[8,256]{1,0:T(8,128)S(1)} %broadcast_add_fusion), channel_id=1, source_target_pairs={{0,68},{1,69},{2,70},{3,71},{4,64},{5,65},{6,66},{7,67},{8,76},{9,... | collective-permute-start | bytes 24584 | tf_op jit(solution)/shard_map/ppermute | solution.py:361
  189.2 7.3 %collective-permute-start.5 = (bf16[128,512]{1,0:T(8,128)(2,1)S(1)}, bf16[128,512]{1,0:T(8,128)(2,1)S(1)}, u32[]{:S(2)}, u32[]{:S(2)}) collective-permute-start(bf16[128,512]{1,0:T(8,128)(2,1)S(1)} %bitcast.122), channel_id=1, source_target_pairs={{0,2},{1,3},{2,0},{3,1},{4,6},{5,7},{6,4},{7,5},{8,10},{9,11},{10,... | collective-permute-start | bytes 393224 | tf_op jit(solution)/shard_map/ppermute | solution.py:313
  196.5 8.3 %collective-permute-start.6 = (bf16[256,512]{1,0:T(8,128)(2,1)S(1)}, bf16[256,512]{1,0:T(8,128)(2,1)S(1)}, u32[]{:S(2)}, u32[]{:S(2)}) collective-permute-start(bf16[256,512]{1,0:T(8,128)(2,1)S(1)} %pad_maximum_fusion.3), channel_id=1, source_target_pairs={{0,1},{1,0},{2,3},{3,2},{4,5},{5,4},{6,7},{7,6},{8,9},{9,8},{10,11... | collective-permute-start | bytes 786440 | tf_op jit(solution)/shard_map/ppermute | solution.py:313

commit v6 on v5

--- a/solution.py
+++ b/solution.py
@@ -56,10 +56,10 @@
     minus = jnp.where(plus, 0, 1)
     return jnp.where(
         diagonal,
-        jnp.where(crosses, 7, 6),
+        jnp.where(crosses, 0, 1),
         jnp.where(
             dy != 0,
-            jnp.where(crosses, 0, 1),
+            jnp.where(crosses, 7, 6),
             jnp.where(dx != 0, 2 + minus, 4 + minus),
         ),
     )
@@ -81,9 +81,9 @@
             plus = sum(d) > 0
             crosses = d[1] != 0 and plus == (k // 4 % 2 == 1)
             if d[0] and d[1]:
+                c = 0 if crosses else 1
+            elif d[1]:
                 c = 7 if crosses else 6
-            elif d[1]:
-                c = 0 if crosses else 1
             else:
                 c = (2 if d[0] else 4) + (0 if plus else 1)
             source = 7 - c if crosses else c
@@ -94,16 +94,21 @@
 EARLY = 32
 
 
-def sort_kernel(k_ref, near_ref, m_ref, out_ref, sems, *, start):
+def sort_kernel(k_ref, near_ref, m_ref, out_ref, block_ref, in_sems, out_sems, *, start):
     k = k_ref[0]
-    copies = []
+    arriving, leaving = [], []
+    for b in range(8):
+        rows = pl.ds(start, out_ref.shape[2])
+        copy = pltpu.make_async_copy(m_ref.at[b, :, rows], block_ref.at[b], in_sems.at[b])
+        copy.start()
+        arriving.append(copy)
     for b in range(8):
         slot = owner_of(k, *difference(near_ref[b], k))
-        rows = pl.ds(start, out_ref.shape[2])
-        copy = pltpu.make_async_copy(m_ref.at[b, :, rows], out_ref.at[slot], sems.at[b])
+        arriving[b].wait()
+        copy = pltpu.make_async_copy(block_ref.at[b], out_ref.at[slot], out_sems.at[b])
         copy.start()
-        copies.append(copy)
-    for copy in copies:
+        leaving.append(copy)
+    for copy in leaving:
         copy.wait()
 
 
@@ -113,8 +118,12 @@
         functools.partial(sort_kernel, start=start),
         out_shape=jax.ShapeDtypeStruct((8, 2, rows, 512), BF),
         in_specs=[smem, smem, pl.BlockSpec(memory_space=pl.ANY)],
-        out_specs=pl.BlockSpec(memory_space=pltpu.VMEM),
-        scratch_shapes=[pltpu.SemaphoreType.DMA((8,))],
+        out_specs=pl.BlockSpec(memory_space=pl.ANY),
+        scratch_shapes=[
+            pltpu.VMEM((8, 2, rows, 512), BF),
+            pltpu.SemaphoreType.DMA((8,)),
+            pltpu.SemaphoreType.DMA((8,)),
+        ],
         name="sort_mats",
     )(kpoint_index.reshape(1), near, mats)
 

time: 209 us -> 212 us (1.014)
  the two profiles are of different devices: /device:TPU:1 before, /device:TPU:2 now
where the time goes in v6:
time: 212 us; the launch traced here: 211 us
  waiting for transfers between devices  134 us (63%)
  starting transfers between devices  58.5 us (28%)
  Pallas kernels  14.5 us (7%)
  other arithmetic  2.68 us (1%)
    ppermute x7, waiting for transfers between devices, partner(): return lax.ppermute(x, axis, [(i, i ^ bit) for i in range(length)])  59.6 us
    all_to_all x1, waiting for transfers between devices, per_device(): early = lax.all_to_all(early, 'col', 0, 0, tiled=True)  26.1 us
    ppermute x7, starting transfers between devices, partner(): return lax.ppermute(x, axis, [(i, i ^ bit) for i in range(length)])  25.3 us
    all_to_all x1, waiting for transfers between devices, within_half(): return lax.all_to_all(x, 'col', 0, 0, tiled=True, axis_index_groups=HALVES)  21.2 us
    ppermute x1, waiting for transfers between devices, per_device(): near_full = lax.ppermute(full, ('ka', 'col'), fetch_permutation())  13.2 us
    all_to_all x1, starting transfers between devices, per_device(): early = lax.all_to_all(early, 'col', 0, 0, tiled=True)  12.5 us
    ppermute x1, waiting for transfers between devices, per_device(): lax.ppermute(spread, ('ka', 'col'), half_ring_permutation())  7.6 us
    all_to_all x1, waiting for transfers between devices, per_device(): lax.all_to_all(spread, 'ka', 0, 0, tiled=True, axis_index_groups=groups)  6.29 us
  transfers between devices with their start and end apart: 13, of which 11 were waited for; matrix products, arithmetic and copies ran while one was open for 1% of the time, Pallas kernels for 2%

profile of v6, /device:TPU:2, one launch (start us, length us, event | category | flops | bytes accessed | tf_op | source)
XLA Modules:
  0.0 211.5 jit_solution(8018669709359216075)
XLA Ops:
  0.6 2.5 %sort_mats.2 = bf16[8,2,32,512]{3,2,1,0:T(8,128)(2,1)} custom-call(s32[1]{0:T(128)} %bitcast.13.k_ref, s32[8]{0:T(128)} %bitcast.134, bf16[8,2,64,512]{3,2,1,0:T(8,128)(2,1)} %bitcast.120), custom_call_target="tpu_custom_call" | custom-call | tf_op jit(solution)/shard_map/sort_mats/pallas_call | solution.py:117
  3.1 12.5 %all-to-all-start = ((bf16[8,2,32,512]{3,2,1,0:T(8,128)(2,1)}), bf16[8,2,32,512]{3,2,1,0:T(8,128)(2,1)S(1)}, u32[]{:S(2)}, u32[]{:S(2)}) async-start(bf16[8,2,32,512]{3,2,1,0:T(8,128)(2,1)} %sort_mats.2), calls=%async_computation | async-start | bytes 1048576 | tf_op jit(solution)/shard_map/all_to_all | solution.py:341
  15.7 2.6 %sort_mats.3 = bf16[8,2,32,512]{3,2,1,0:T(8,128)(2,1)} custom-call(s32[1]{0:T(128)} %bitcast.13.k_ref, s32[8]{0:T(128)} %bitcast.135, bf16[8,2,64,512]{3,2,1,0:T(8,128)(2,1)} %bitcast.121), custom_call_target="tpu_custom_call" | custom-call | tf_op jit(solution)/shard_map/sort_mats/pallas_call | solution.py:117
  18.3 26.1 %all-to-all-done.early_ref = bf16[8,2,32,512]{3,2,1,0:T(8,128)(2,1)S(1)} async-done(((bf16[8,2,32,512]{3,2,1,0:T(8,128)(2,1)}), bf16[8,2,32,512]{3,2,1,0:T(8,128)(2,1)S(1)}, u32[]{:S(2)}, u32[]{:S(2)}) %all-to-all-start) | async-done | bytes 524320 | tf_op jit(solution)/shard_map/all_to_all | solution.py:341
  44.4 4.3 %all-to-all-start.1 = ((bf16[8,2,32,512]{3,2,1,0:T(8,128)(2,1)}), bf16[8,2,32,512]{3,2,1,0:T(8,128)(2,1)S(1)}, u32[]{:S(2)}, u32[]{:S(2)}) async-start(bf16[8,2,32,512]{3,2,1,0:T(8,128)(2,1)} %sort_mats.3), calls=%async_computation.1 | async-start | bytes 1048576 | tf_op jit(solution)/shard_map/all_to_all | solution.py:342
  48.7 7.8 %collective-permute-start = (bf16[64,512]{1,0:T(8,128)(2,1)S(1)}, bf16[64,512]{1,0:T(8,128)(2,1)S(1)}, u32[]{:S(2)}, u32[]{:S(2)}) collective-permute-start(bf16[64,512]{1,0:T(8,128)(2,1)S(1)} %bitcast.125), channel_id=1, source_target_pairs={{0,4},{1,5},{2,6},{3,7},{4,0},{5,1},{6,2},{7,3},{8,12},{9,13},{10,... | collective-permute-start | bytes 196616 | tf_op jit(solution)/shard_map/ppermute | solution.py:322
  56.5 26.2 %collective-permute-done = bf16[64,512]{1,0:T(8,128)(2,1)S(1)} collective-permute-done((bf16[64,512]{1,0:T(8,128)(2,1)S(1)}, bf16[64,512]{1,0:T(8,128)(2,1)S(1)}, u32[]{:S(2)}, u32[]{:S(2)}) %collective-permute-start) | collective-permute-done | bytes 65568 | tf_op jit(solution)/shard_map/ppermute | solution.py:322
  82.7 1.9 collective-permute-start.1
  84.6 5.8 %collective-permute-done.1 = bf16[2,64,512]{2,1,0:T(8,128)(2,1)S(1)} collective-permute-done((bf16[2,64,512]{2,1,0:T(8,128)(2,1)S(1)}, bf16[2,64,512]{2,1,0:T(8,128)(2,1)S(1)}, u32[]{:S(2)}, u32[]{:S(2)}) %collective-permute-start.1) | collective-permute-done | bytes 131104 | tf_op jit(solution)/shard_map/ppermute | solution.py:322
  90.5 1.9 collective-permute-start.2
  92.7 6.3 %collective-permute-done.2 = bf16[2,2,64,512]{3,2,1,0:T(8,128)(2,1)S(1)} collective-permute-done((bf16[2,2,64,512]{3,2,1,0:T(8,128)(2,1)S(1)}, bf16[2,2,64,512]{3,2,1,0:T(8,128)(2,1)S(1)}, u32[]{:S(2)}, u32[]{:S(2)}) %collective-permute-start.2) | collective-permute-done | bytes 262176 | tf_op jit(solution)/shard_map/ppermute | solution.py:322
  99.1 6.1 %collective-permute-start.3 = (bf16[8,64,512]{2,1,0:T(8,128)(2,1)S(1)}, bf16[8,64,512]{2,1,0:T(8,128)(2,1)S(1)}, u32[]{:S(2)}, u32[]{:S(2)}) collective-permute-start(bf16[8,64,512]{2,1,0:T(8,128)(2,1)S(1)} %bitcast.118), channel_id=1, source_target_pairs={{130,2},{387,3},{38,6},{96,7},{12,4},{29,5},{169,1},{511,0},{138,1... | collective-permute-start | bytes 1572872 | tf_op jit(solution)/shard_map/ppermute | solution.py:346
  105.9 13.2 %collective-permute-done.3.n_ref = bf16[8,64,512]{2,1,0:T(8,128)(2,1)S(1)} collective-permute-done((bf16[8,64,512]{2,1,0:T(8,128)(2,1)S(1)}, bf16[8,64,512]{2,1,0:T(8,128)(2,1)S(1)}, u32[]{:S(2)}, u32[]{:S(2)}) %collective-permute-start.3) | collective-permute-done | bytes 524320 | tf_op jit(solution)/shard_map/ppermute | solution.py:346
  120.5 4.6 %main_products.1 = bf16[4,2,96,512]{3,2,1,0:T(8,128)(2,1)} custom-call(f32[1]{0:T(128)} %bitcast.10.w_ref, s32[2]{0:T(128)S(1)} %pad_add_fusion.1.holder_ref, bf16[8,2,32,512]{3,2,1,0:T(8,128)(2,1)S(1)} %all-to-all-done.early_ref, bf16[8,2,32,512]{3,2,1,0:T(8,128)(2,1)S(1)} %all-to-all-done.1.late_ref, bf16[512,512]{1,0:T(8,128)(2,1)S(1)} %get-tuple-element.7.ut_ref, ...), custom_call_target="tpu_custom_call" | custom-call | tf_op jit(solution)/shard_map/main_products/pallas_call | solution.py:259
  125.1 3.5 %all-to-all-start.2 = ((bf16[4,2,96,512]{3,2,1,0:T(8,128)(2,1)}), bf16[4,2,96,512]{3,2,1,0:T(8,128)(2,1)S(1)}, u32[]{:S(2)}, u32[]{:S(2)}) async-start(bf16[4,2,96,512]{3,2,1,0:T(8,128)(2,1)} %main_products.1), calls=%async_computation.2 | async-start | bytes 1572864 | tf_op jit(solution)/shard_map/all_to_all | solution.py:317
  128.7 21.2 %all-to-all-done.2 = bf16[4,2,96,512]{3,2,1,0:T(8,128)(2,1)S(1)} async-done(((bf16[4,2,96,512]{3,2,1,0:T(8,128)(2,1)}), bf16[4,2,96,512]{3,2,1,0:T(8,128)(2,1)S(1)}, u32[]{:S(2)}, u32[]{:S(2)}) %all-to-all-start.2) | async-done | bytes 786464 | tf_op jit(solution)/shard_map/all_to_all | solution.py:317
  150.7 5.0 %all-to-all-start.3 = ((f32[32,1,256]{2,1,0:T(1,128)}), f32[32,1,256]{2,1,0:T(1,128)S(1)}, u32[]{:S(2)}, u32[]{:S(2)}) async-start(f32[32,1,256]{2,1,0:T(1,128)} %broadcast_in_dim.54), calls=%async_computation.3 | async-start | bytes 65536 | tf_op jit(solution)/shard_map/all_to_all | solution.py:367
  155.7 6.3 %all-to-all-done.3 = f32[32,1,256]{2,1,0:T(1,128)S(1)} async-done(((f32[32,1,256]{2,1,0:T(1,128)}), f32[32,1,256]{2,1,0:T(1,128)S(1)}, u32[]{:S(2)}, u32[]{:S(2)}) %all-to-all-start.3) | async-done | bytes 32800 | tf_op jit(solution)/shard_map/all_to_all | solution.py:367
  164.0 7.8 %collective-permute-start.4 = (bf16[160,512]{1,0:T(8,128)(2,1)S(1)}, bf16[160,512]{1,0:T(8,128)(2,1)S(1)}, u32[]{:S(2)}, u32[]{:S(2)}) collective-permute-start(bf16[160,512]{1,0:T(8,128)(2,1)S(1)} %pad_maximum_fusion.4), channel_id=1, source_target_pairs={{0,4},{1,5},{2,6},{3,7},{4,0},{5,1},{6,2},{7,3},{8,12},{9,13},{10,... | collective-permute-start | bytes 491528 | tf_op jit(solution)/shard_map/ppermute | solution.py:322
  171.9 9.8 %collective-permute-done.7 = f32[8,256]{1,0:T(8,128)S(1)} collective-permute-done((f32[8,256]{1,0:T(8,128)S(1)}, f32[8,256]{1,0:T(8,128)S(1)}, u32[]{:S(2)}, u32[]{:S(2)}) %collective-permute-start.7) | collective-permute-done | bytes 8224 | tf_op jit(solution)/shard_map/ppermute | solution.py:322
  183.6 7.6 %collective-permute-done.8 = f32[8,256]{1,0:T(8,128)S(1)} collective-permute-done((f32[8,256]{1,0:T(8,128)S(1)}, f32[8,256]{1,0:T(8,128)S(1)}, u32[]{:S(2)}, u32[]{:S(2)}) %collective-permute-start.8) | collective-permute-done | bytes 8224 | tf_op jit(solution)/shard_map/ppermute | solution.py:370
  194.0 5.9 %collective-permute-done.5 = bf16[128,512]{1,0:T(8,128)(2,1)S(1)} collective-permute-done((bf16[128,512]{1,0:T(8,128)(2,1)S(1)}, bf16[128,512]{1,0:T(8,128)(2,1)S(1)}, u32[]{:S(2)}, u32[]{:S(2)}) %collective-permute-start.5) | collective-permute-done | bytes 131104 | tf_op jit(solution)/shard_map/ppermute | solution.py:322
  202.4 5.7 %collective-permute-done.6 = bf16[256,512]{1,0:T(8,128)(2,1)S(1)} collective-permute-done((bf16[256,512]{1,0:T(8,128)(2,1)S(1)}, bf16[256,512]{1,0:T(8,128)(2,1)S(1)}, u32[]{:S(2)}, u32[]{:S(2)}) %collective-permute-start.6) | collective-permute-done | bytes 262176 | tf_op jit(solution)/shard_map/ppermute | solution.py:322
  208.2 3.3 %orthonormalize.1 = f32[64,2,256]{2,1,0:T(2,128)} custom-call(bf16[512,512]{1,0:T(8,128)(2,1)S(1)} %pad_maximum_fusion.1.x_ref, f32[64,512]{1,0:T(8,128)S(1)} %slice_bitcast_fusion.own_ref), custom_call_target="tpu_custom_call" | custom-call | tf_op jit(solution)/shard_map/orthonormalize/pallas_call | solution.py:306
  (46 shorter events, 12.5 us)
Async XLA Ops:
  3.1 41.3 %all-to-all-start = ((bf16[8,2,32,512]{3,2,1,0:T(8,128)(2,1)}), bf16[8,2,32,512]{3,2,1,0:T(8,128)(2,1)S(1)}, u32[]{:S(2)}, u32[]{:S(2)}) async-start(bf16[8,2,32,512]{3,2,1,0:T(8,128)(2,1)} %sort_mats.2), calls=%async_computation | async-start | bytes 1048576 | tf_op jit(solution)/shard_map/all_to_all | solution.py:341
  15.7 33.0 %copy-start = (bf16[1,64,2,256]{3,2,1,0:T(2,128)(2,1)S(1)}, bf16[1,64,2,256]{3,2,1,0:T(2,128)(2,1)}, u32[]{:S(2)}) copy-start(bf16[1,64,2,256]{3,2,1,0:T(2,128)(2,1)} %param.6) | copy-start | bytes 196612
  18.3 74.2 %copy-start.2 = (s32[1,8,3]{1,0,2:T(1,128)S(1)}, s32[1,8,3]{1,0,2:T(1,128)}, u32[]{:S(2)}) copy-start(s32[1,8,3]{1,0,2:T(1,128)} %param.8) | copy-start | bytes 292
  44.4 76.1 %all-to-all-start.1 = ((bf16[8,2,32,512]{3,2,1,0:T(8,128)(2,1)}), bf16[8,2,32,512]{3,2,1,0:T(8,128)(2,1)S(1)}, u32[]{:S(2)}, u32[]{:S(2)}) async-start(bf16[8,2,32,512]{3,2,1,0:T(8,128)(2,1)} %sort_mats.3), calls=%async_computation.1 | async-start | bytes 1048576 | tf_op jit(solution)/shard_map/all_to_all | solution.py:342
  48.7 34.0 %collective-permute-start = (bf16[64,512]{1,0:T(8,128)(2,1)S(1)}, bf16[64,512]{1,0:T(8,128)(2,1)S(1)}, u32[]{:S(2)}, u32[]{:S(2)}) collective-permute-start(bf16[64,512]{1,0:T(8,128)(2,1)S(1)} %bitcast.125), channel_id=1, source_target_pairs={{0,4},{1,5},{2,6},{3,7},{4,0},{5,1},{6,2},{7,3},{8,12},{9,13},{10,... | collective-permute-start | bytes 196616 | tf_op jit(solution)/shard_map/ppermute | solution.py:322
  82.7 22.4 %copy-start.1 = (s32[1,8]{1,0:T(1,128)S(1)}, s32[1,8]{1,0:T(1,128)}, u32[]{:S(2)}) copy-start(s32[1,8]{1,0:T(1,128)} %param.7) | copy-start | bytes 100
  82.7 7.8 %collective-permute-start.1 = (bf16[2,64,512]{2,1,0:T(8,128)(2,1)S(1)}, bf16[2,64,512]{2,1,0:T(8,128)(2,1)S(1)}, u32[]{:S(2)}, u32[]{:S(2)}) collective-permute-start(bf16[2,64,512]{2,1,0:T(8,128)(2,1)S(1)} %get-tuple-element.18), channel_id=1, source_target_pairs={{0,2},{1,3},{2,0},{3,1},{4,6},{5,7},{6,4},{7,5},{8,10},{9,11},{10,... | collective-permute-start | bytes 393224 | tf_op jit(solution)/shard_map/ppermute | solution.py:322
  90.5 8.5 %collective-permute-start.2 = (bf16[2,2,64,512]{3,2,1,0:T(8,128)(2,1)S(1)}, bf16[2,2,64,512]{3,2,1,0:T(8,128)(2,1)S(1)}, u32[]{:S(2)}, u32[]{:S(2)}) collective-permute-start(bf16[2,2,64,512]{3,2,1,0:T(8,128)(2,1)S(1)} %get-tuple-element.16), channel_id=1, source_target_pairs={{0,1},{1,0},{2,3},{3,2},{4,5},{5,4},{6,7},{7,6},{8,9},{9,8},{10,11... | collective-permute-start | bytes 786440 | tf_op jit(solution)/shard_map/ppermute | solution.py:322
  99.1 20.0 %collective-permute-start.3 = (bf16[8,64,512]{2,1,0:T(8,128)(2,1)S(1)}, bf16[8,64,512]{2,1,0:T(8,128)(2,1)S(1)}, u32[]{:S(2)}, u32[]{:S(2)}) collective-permute-start(bf16[8,64,512]{2,1,0:T(8,128)(2,1)S(1)} %bitcast.118), channel_id=1, source_target_pairs={{130,2},{387,3},{38,6},{96,7},{12,4},{29,5},{169,1},{511,0},{138,1... | collective-permute-start | bytes 1572872 | tf_op jit(solution)/shard_map/ppermute | solution.py:346
  125.1 24.8 %all-to-all-start.2 = ((bf16[4,2,96,512]{3,2,1,0:T(8,128)(2,1)}), bf16[4,2,96,512]{3,2,1,0:T(8,128)(2,1)S(1)}, u32[]{:S(2)}, u32[]{:S(2)}) async-start(bf16[4,2,96,512]{3,2,1,0:T(8,128)(2,1)} %main_products.1), calls=%async_computation.2 | async-start | bytes 1572864 | tf_op jit(solution)/shard_map/all_to_all | solution.py:317
  150.7 11.3 %all-to-all-start.3 = ((f32[32,1,256]{2,1,0:T(1,128)}), f32[32,1,256]{2,1,0:T(1,128)S(1)}, u32[]{:S(2)}, u32[]{:S(2)}) async-start(f32[32,1,256]{2,1,0:T(1,128)} %broadcast_in_dim.54), calls=%async_computation.3 | async-start | bytes 65536 | tf_op jit(solution)/shard_map/all_to_all | solution.py:367
  162.1 19.6 %collective-permute-start.7 = (f32[8,256]{1,0:T(8,128)S(1)}, f32[8,256]{1,0:T(8,128)S(1)}, u32[]{:S(2)}, u32[]{:S(2)}) collective-permute-start(f32[8,256]{1,0:T(8,128)S(1)} %broadcast_in_dim.55), channel_id=1, source_target_pairs={{0,4},{1,5},{2,6},{3,7},{4,0},{5,1},{6,2},{7,3},{8,12},{9,13},{10,... | collective-permute-start | bytes 24584 | tf_op jit(solution)/shard_map/ppermute | solution.py:322
  164.0 27.8 %collective-permute-start.4 = (bf16[160,512]{1,0:T(8,128)(2,1)S(1)}, bf16[160,512]{1,0:T(8,128)(2,1)S(1)}, u32[]{:S(2)}, u32[]{:S(2)}) collective-permute-start(bf16[160,512]{1,0:T(8,128)(2,1)S(1)} %pad_maximum_fusion.4), channel_id=1, source_target_pairs={{0,4},{1,5},{2,6},{3,7},{4,0},{5,1},{6,2},{7,3},{8,12},{9,13},{10,... | collective-permute-start | bytes 491528 | tf_op jit(solution)/shard_map/ppermute | solution.py:322
  181.7 9.5 %collective-permute-start.8 = (f32[8,256]{1,0:T(8,128)S(1)}, f32[8,256]{1,0:T(8,128)S(1)}, u32[]{:S(2)}, u32[]{:S(2)}) collective-permute-start(f32[8,256]{1,0:T(8,128)S(1)} %broadcast_add_fusion), channel_id=1, source_target_pairs={{0,68},{1,69},{2,70},{3,71},{4,64},{5,65},{6,66},{7,67},{8,76},{9,... | collective-permute-start | bytes 24584 | tf_op jit(solution)/shard_map/ppermute | solution.py:370
  192.0 7.9 %collective-permute-start.5 = (bf16[128,512]{1,0:T(8,128)(2,1)S(1)}, bf16[128,512]{1,0:T(8,128)(2,1)S(1)}, u32[]{:S(2)}, u32[]{:S(2)}) collective-permute-start(bf16[128,512]{1,0:T(8,128)(2,1)S(1)} %bitcast.122), channel_id=1, source_target_pairs={{0,2},{1,3},{2,0},{3,1},{4,6},{5,7},{6,4},{7,5},{8,10},{9,11},{10,... | collective-permute-start | bytes 393224 | tf_op jit(solution)/shard_map/ppermute | solution.py:322
  199.9 8.3 %collective-permute-start.6 = (bf16[256,512]{1,0:T(8,128)(2,1)S(1)}, bf16[256,512]{1,0:T(8,128)(2,1)S(1)}, u32[]{:S(2)}, u32[]{:S(2)}) collective-permute-start(bf16[256,512]{1,0:T(8,128)(2,1)S(1)} %pad_maximum_fusion.3), channel_id=1, source_target_pairs={{0,1},{1,0},{2,3},{3,2},{4,5},{5,4},{6,7},{7,6},{8,9},{9,8},{10,11... | collective-permute-start | bytes 786440 | tf_op jit(solution)/shard_map/ppermute | solution.py:322
